TPU v7x, 128 devices: a whole 4x4x4 slice. The times are simulated.
128 devices in a mesh: tile: 16 (over z, y), obs: 8 (over x, core).
Axes of the slice: x: 4, y: 4, z: 4, core: 2. Of those that a mesh axis runs over, the one named last changes fastest.
Arguments:
- control: float32 [128, 1024, 1024], P(None, 'tile', 'obs'), may hold values from -6 to 6
- background: bfloat16 [128, 1024, 1024], P(None, 'tile', 'obs'), may hold values from -6 to 6
- spread: float32 [1024, 1024], P('tile', 'obs'), may hold values from 0.03 to 0.24
- obs_holder: int32 [32768, 1], P(('tile', 'obs')), may hold values from 0 to 127; in each aligned block of 256 rows (0 to 255, 256 to 511, ...) at most 6 rows name the same one
- obs_anchor: int32 [32768], P(('tile', 'obs')), may hold values from 0 to 8000
- obs_frac: float32 [2, 32768], P(None, ('tile', 'obs')), may hold values from 0 to 1
- innovation: float32 [32768, 616], P(('tile', 'obs')), may hold values from -6 to 6
- inverse_var: float32 [616], replicated, may hold values from 0.5 to 2
- w_first: bfloat16 [128, 512], replicated, may hold values from -0.5 to 0.5
- b_first: float32 [512], replicated, may hold values from -3 to 3
- w_second: bfloat16 [512, 512], replicated, may hold values from -0.25 to 0.25
- b_second: float32 [512], replicated, may hold values from -3 to 3
- w_third: bfloat16 [512, 616], replicated, may hold values from -0.25 to 0.25
Outputs:
- departures: float32 [32768, 616], P(('tile', 'obs'))
- gradient: float32 [128, 1024, 1024], P(None, 'tile', 'obs')
Inputs may be any that keep to these rules, and one draw needn't show every extreme that they name: `obs_holder`: among the observations of one device (aligned blocks of 256 rows) at most 6 name the same holder.
All inputs are finite; a program needn't handle non-finite values.
Results may differ from a plain program's by a relative error of at most 0.0011.
Values may be sent and summed in bfloat16 or wider, within the bound.
No kernel may reach another device: no remote copies, remote signals or barrier semaphores. Data moves between devices by JAX's collectives and lax.ppermute only.
A program may use at most 64 MiB of HBM per device.

v0:
```python
import jax
import jax.numpy as jnp
from jax import lax
from jax.sharding import PartitionSpec as P

SWEEPS = 2


def padded_2(block, sides, width):
    for axis, dim in sides:
        count = lax.axis_size(axis)
        forward = [(i, i + 1) for i in range(count - 1)]
        forward.append((count - 1, 0))
        backward = [(target, source) for source, target in forward]
        low = lax.ppermute(
            lax.slice_in_dim(block, block.shape[dim] - width, None, axis=dim), axis, forward
        )
        high = lax.ppermute(lax.slice_in_dim(block, 0, width, axis=dim), axis, backward)
        block = jnp.concatenate([low, block, high], axis=dim)
    return block


def crop(array, cut):
    if cut == 0:
        return array
    return array[..., cut:-cut, cut:-cut]


def laplace(padded):
    total = padded[:, 2:, 1:-1] + padded[:, :-2, 1:-1]
    total = total + padded[:, 1:-1, 2:] + padded[:, 1:-1, :-2]
    return total - 4.0 * padded[:, 1:-1, 1:-1]


def advance(padded, margin, spread_pad, spread_margin, adjoint):
    if adjoint:
        scaled = crop(spread_pad, spread_margin - margin)[None] * padded
        return crop(padded, 1) + laplace(scaled)
    return crop(padded, 1) + crop(spread_pad, spread_margin - margin + 1)[None] * laplace(padded)


def diffuse(field, spread_pad, spread_margin, adjoint):
    padded = padded_2(field, (("tile", 1), ("obs", 2)), SWEEPS)
    for step in range(SWEEPS):
        padded = advance(padded, SWEEPS - step, spread_pad, spread_margin, adjoint)
    return padded


def corner_weights(frac_x, frac_y):
    return jnp.stack(
        [
            (1.0 - frac_x) * (1.0 - frac_y),
            frac_x * (1.0 - frac_y),
            (1.0 - frac_x) * frac_y,
            frac_x * frac_y,
        ],
        axis=1,
    )


def blend(columns, weights):
    return sum((weights[:, j, None] * columns[:, j].astype(jnp.float32) for j in range(4)))


def radiances(base, delta, innov, inverse_var, w_first, b_first, w_second, b_second, w_third):
    h_one = jnp.tanh(jnp.dot(base, w_first, preferred_element_type=jnp.float32) + b_first)
    d_one = 1.0 - h_one * h_one
    h_two = jnp.tanh(
        jnp.dot(h_one.astype(jnp.bfloat16), w_second, preferred_element_type=jnp.float32) + b_second
    )
    d_two = 1.0 - h_two * h_two
    t_one = (d_one * jnp.dot(delta, w_first, preferred_element_type=jnp.float32)).astype(
        jnp.bfloat16
    )
    t_two = (d_two * jnp.dot(t_one, w_second, preferred_element_type=jnp.float32)).astype(
        jnp.bfloat16
    )
    change = jnp.dot(t_two, w_third, preferred_element_type=jnp.float32)
    departures = (change - innov) * inverse_var
    s_two = (
        d_two
        * jnp.dot(departures.astype(jnp.bfloat16), w_third.T, preferred_element_type=jnp.float32)
    ).astype(jnp.bfloat16)
    s_one = (d_one * jnp.dot(s_two, w_second.T, preferred_element_type=jnp.float32)).astype(
        jnp.bfloat16
    )
    return (departures, jnp.dot(s_one, w_first.T, preferred_element_type=jnp.float32))


def per_device(
    control,
    background,
    spread,
    obs_holder,
    obs_anchor,
    obs_frac,
    innovation,
    inverse_var,
    w_first,
    b_first,
    w_second,
    b_second,
    w_third,
):
    levels, rows_x, rows_y = control.shape
    owners = lax.axis_size("tile") * lax.axis_size("obs")
    count = obs_anchor.shape[0]
    capacity = 3 * count // owners
    holder = obs_holder[:, 0]
    marks = (holder[:, None] == jnp.arange(owners, dtype=jnp.int32)[None, :]).astype(jnp.int32)
    before = jnp.cumsum(marks, axis=0) - marks
    position = holder * capacity + jnp.sum(before * marks, axis=1)
    asked = jnp.zeros((owners * capacity,), jnp.int32).at[position].set(obs_anchor)
    asked = lax.all_to_all(
        asked.reshape(owners, capacity), ("tile", "obs"), split_axis=0, concat_axis=0, tiled=True
    ).reshape(-1)
    corner = asked // (rows_y - 1) * rows_y + asked % (rows_y - 1)
    source = jnp.stack([corner, corner + rows_y, corner + 1, corner + rows_y + 1], axis=1)
    rim = SWEEPS
    spread_pad = padded_2(spread, (("tile", 0), ("obs", 1)), rim)
    increment = diffuse(control, spread_pad, rim, False)
    bg_cols = background.reshape(levels, rows_x * rows_y).T
    inc_cols = increment.astype(jnp.bfloat16).reshape(levels, rows_x * rows_y).T
    own_weights = corner_weights(obs_frac[0], obs_frac[1])
    bg_set, inc_set = (
        lax.all_to_all(
            bg_cols[source].reshape(owners, capacity, 4, levels),
            ("tile", "obs"),
            split_axis=0,
            concat_axis=0,
            tiled=True,
        ),
        lax.all_to_all(
            inc_cols[source].reshape(owners, capacity, 4, levels),
            ("tile", "obs"),
            split_axis=0,
            concat_axis=0,
            tiled=True,
        ),
    )
    base = blend(bg_set.reshape(-1, 4, levels)[position], own_weights).astype(jnp.bfloat16)
    delta = blend(inc_set.reshape(-1, 4, levels)[position], own_weights).astype(jnp.bfloat16)
    departures, profile_grad = radiances(
        base, delta, innovation, inverse_var, w_first, b_first, w_second, b_second, w_third
    )
    weighted = own_weights[:, :, None] * profile_grad[:, None, :]
    pieces = jnp.zeros((owners * capacity, 4, levels), jnp.float32).at[position].set(weighted)
    pieces = (
        lax.all_to_all(
            pieces.reshape(owners, capacity, 4, levels).astype(jnp.bfloat16),
            ("tile", "obs"),
            split_axis=0,
            concat_axis=0,
            tiled=True,
        )
        .astype(jnp.float32)
        .reshape(-1, 4, levels)
    )
    gathered = (
        jnp.zeros((rows_x * rows_y, levels), jnp.float32)
        .at[source.reshape(-1)]
        .add(pieces.reshape(-1, levels))
    )
    adjoint = gathered.T.reshape(levels, rows_x, rows_y)
    gradient = control + diffuse(adjoint, spread_pad, rim, True)
    return (departures, gradient)


def solution(mesh):
    return jax.shard_map(
        per_device,
        mesh=mesh,
        in_specs=(
            P(None, "tile", "obs"),
            P(None, "tile", "obs"),
            P("tile", "obs"),
            P(("tile", "obs"), None),
            P(("tile", "obs")),
            P(None, ("tile", "obs")),
            P(("tile", "obs"), None),
            P(),
            P(),
            P(),
            P(),
            P(),
            P(),
        ),
        out_specs=(P(("tile", "obs"), None), P(None, "tile", "obs")),
        check_vma=False,
    )
```

profile of v0, /device:TPU:1, one launch (start us, length us, event | category | flops | bytes accessed | tf_op | source)
XLA Modules:
  0.0 205.8 jit_solution(8204464544457574022)
XLA Ops:
  0.6 0.8 fusion.73
  1.4 2.1 %collective-permute-start.4 = (f32[2,128]{1,0:T(2,128)S(1)}, f32[2,128]{1,0:T(2,128)S(1)}, u32[]{:S(2)}, u32[]{:S(2)}) collective-permute-start(f32[2,128]{1,0:T(2,128)S(1)} %get-tuple-element.30), channel_id=1, source_target_pairs={{0,8},{8,16},{16,24},{24,32},{32,40},{40,48},{48,56},{56,64},{64,7... | collective-permute-start | bytes 3080 | tf_op jit(solution)/shard_map/ppermute | solution.py:15
  3.5 4.9 %collective-permute-start.5 = (f32[2,128]{1,0:T(2,128)S(1)}, f32[2,128]{1,0:T(2,128)S(1)}, u32[]{:S(2)}, u32[]{:S(2)}) collective-permute-start(f32[2,128]{1,0:T(2,128)S(1)} %get-tuple-element.31), channel_id=1, source_target_pairs={{8,0},{16,8},{24,16},{32,24},{40,32},{48,40},{56,48},{64,56},{72,6... | collective-permute-start | bytes 3080 | tf_op jit(solution)/shard_map/ppermute | solution.py:18
  8.4 0.8 copy.53
  9.2 0.2 fusion.30
  9.6 0.9 fusion.40
  10.4 0.7 compare_select_fusion.2
  11.1 1.6 scatter_custom_fusion
  12.7 0.8 all_to_all.15
  13.4 6.5 %all-to-all-start = ((s32[128,1,6]{2,1,0:T(1,128)}), s32[128,1,6]{2,1,0:T(1,128)S(1)}, u32[]{:S(2)}, u32[]{:S(2)}) async-start(s32[128,1,6]{2,1,0:T(1,128)} %bitcast.11), calls=%async_computation | async-start | bytes 131072 | tf_op jit(solution)/shard_map/all_to_all | solution.py:114
  19.9 5.4 %copy.60 = f32[128,64,128]{0,1,2:T(8,128)} copy(f32[128,64,128]{2,1,0:T(8,128)} %param.13) | data formatting | bytes 8388608 | tf_op args[0]
  25.3 2.0 fusion.69
  27.3 1.4 collective-permute-start
  28.7 4.2 %collective-permute-start.1 = (f32[128,2,128]{0,1,2:T(2,128)}, f32[128,2,128]{0,1,2:T(2,128)S(1)}, u32[]{:S(2)}, u32[]{:S(2)}) collective-permute-start(f32[128,2,128]{0,1,2:T(2,128)} %get-tuple-element.19), channel_id=1, source_target_pairs={{8,0},{16,8},{24,16},{32,24},{40,32},{48,40},{56,48},{64,56},{72,6... | collective-permute-start | bytes 393224 | tf_op jit(solution)/shard_map/ppermute | solution.py:18
  32.9 0.6 fusion.61
  33.5 0.6 subtract_multiply_fusion.1
  34.2 1.8 collective-permute-start.6
  35.9 0.6 pad_clamp_fusion
  36.5 0.7 copy.64
  37.3 3.3 %copy.52 = bf16[128,64,128]{0,2,1:T(8,128)(2,1)S(1)} copy(bf16[128,64,128]{2,1,0:T(8,128)(2,1)} %param.14) | data formatting | bytes 4194304 | tf_op args[1]
  40.9 0.3 compare_reduce_fusion
  41.4 0.6 divide_reduce_fusion
  42.5 0.2 reshape.540
  42.8 0.9 pad_maximum_fusion.11
  43.7 2.1 %collective-permute-start.3 = (f32[128,68,2]{0,1,2:T(8,128)S(1)}, f32[128,68,2]{0,1,2:T(8,128)S(1)}, u32[]{:S(2)}, u32[]{:S(2)}) collective-permute-start(f32[128,68,2]{0,1,2:T(8,128)S(1)} %get-tuple-element.14), channel_id=1, source_target_pairs={{1,0},{2,1},{3,2},{4,3},{5,4},{6,5},{7,6},{0,7},{9,8},{10,9},{11,1... | collective-permute-start | bytes 208904 | tf_op jit(solution)/shard_map/ppermute | solution.py:18
  45.8 11.5 %gather_fusion = bf16[3072,128]{1,0:T(8,128)(2,1)} fusion(bf16[8192,128]{1,0:T(8,128)(2,1)S(1)} %bitcast.121, s32[3072]{0:T(1024)S(1)} %broadcast_clamp_fusion), kind=kCustom, calls=%fused_computation | custom fusion | bytes 1585152 | tf_op jit(solution)/shard_map/gather | solution.py:127
  57.3 5.7 %all-to-all-start.1 = ((bf16[128,6,4,128]{3,2,1,0:T(4,128)(2,1)}), bf16[128,6,4,128]{3,2,1,0:T(4,128)(2,1)}, u32[]{:S(2)}, u32[]{:S(2)}) async-start(bf16[128,6,4,128]{3,2,1,0:T(4,128)(2,1)} %bitcast.16), calls=%async_computation.1 | async-start | bytes 1572864 | tf_op jit(solution)/shard_map/all_to_all | solution.py:126
  63.1 3.4 %pad_maximum_fusion = f32[128,68,132]{0,1,2:T(8,128)S(1)} fusion(f32[128,68,2]{0,1,2:T(8,128)S(1)} %collective-permute-done.3, f32[128,2,128]{0,1,2:T(2,128)S(1)} %collective-permute-done.1, f32[128,64,128]{0,1,2:T(8,128)} %copy.60, f32[128,2,128]{0,1,2:T(2,128)S(1)} %collective-permute-done, f32[128,68,2]{0,1,2:T(8,128)S(1)} %collective-permute-done.2), kind=kLoop, calls=%fused_computation.7 | loop fusion | flops 4595712 | bytes 9191424 | tf_op jit(solution)/shard_map/concatenate | solution.py:19
  66.5 5.2 %fusion.5 = f32[128,66,130]{0,1,2:T(8,128)S(1)} fusion(f32[128,68,2]{0,1,2:T(8,128)S(1)} %collective-permute-done.2, f32[128,2,128]{0,1,2:T(2,128)S(1)} %collective-permute-done.1, f32[128,64,128]{0,1,2:T(8,128)S(1)} %copy-done.2, f32[128,2,128]{0,1,2:T(2,128)S(1)} %collective-permute-done, f32[128,68,2]{0,1,2:T(8,128)S(1)} %collective-permute-done.3, ...), kind=kLoop, calls=%fused_computation.19 | loop fusion | flops 14277120 | bytes 22201872 | tf_op jit(solution)/shard_map/add | solution.py:39
  71.7 3.0 %fusion.13 = bf16[128,64,128]{0,1,2:T(8,128)(2,1)S(1)} fusion(f32[128,66,130]{0,1,2:T(8,128)S(1)} %fusion.5, f32[64,128]{0,1:T(8,128)S(1)} %copy-done.10), kind=kLoop, calls=%fused_computation.38 | loop fusion | flops 8388608 | bytes 23101440 | tf_op jit(solution)/shard_map/convert_element_type | solution.py:123
  74.8 1.4 copy.65
  76.2 11.5 %gather_fusion.2 = bf16[3072,128]{1,0:T(8,128)(2,1)} fusion(bf16[8192,128]{1,0:T(8,128)(2,1)S(1)} %bitcast.122, s32[3072]{0:T(1024)S(1)} %broadcast_clamp_fusion), kind=kCustom, calls=%fused_computation.2 | custom fusion | bytes 1585152 | tf_op jit(solution)/shard_map/gather | solution.py:134
  87.7 9.8 %all-to-all-start.2 = ((bf16[128,6,4,128]{3,2,1,0:T(4,128)(2,1)}), bf16[128,6,4,128]{3,2,1,0:T(4,128)(2,1)S(1)}, u32[]{:S(2)}, u32[]{:S(2)}) async-start(bf16[128,6,4,128]{3,2,1,0:T(4,128)(2,1)} %bitcast.124), calls=%async_computation.2 | async-start | bytes 1572864 | tf_op jit(solution)/shard_map/all_to_all | solution.py:133
  97.5 0.7 pad_maximum_fusion.16
  98.2 0.8 copy.71
  99.0 2.3 %gather_fusion.1 = bf16[256,4,128]{2,1,0:T(4,128)(2,1)S(1)} fusion(bf16[768,4,128]{2,1,0:T(4,128)(2,1)} %bitcast.17, s32[1024]{0:T(1024)} %pad_clamp_fusion), kind=kCustom, calls=%fused_computation.1 | custom fusion | bytes 525312 | tf_op jit(solution)/shard_map/gather | solution.py:141
  101.2 0.4 fusion.71
  101.6 1.0 fusion.18
  102.7 1.0 fusion.21
  103.7 10.2 %all-to-all-done.2 = bf16[128,6,4,128]{3,2,1,0:T(4,128)(2,1)S(1)} async-done(((bf16[128,6,4,128]{3,2,1,0:T(4,128)(2,1)}), bf16[128,6,4,128]{3,2,1,0:T(4,128)(2,1)S(1)}, u32[]{:S(2)}, u32[]{:S(2)}) %all-to-all-start.2) | async-done | bytes 786464 | tf_op jit(solution)/shard_map/all_to_all | solution.py:133
  113.9 1.1 gather_fusion.3
  115.0 1.1 fusion.70
  116.1 1.5 fusion.22
  117.6 1.4 fusion.17
  119.1 0.6 fusion.23
  119.7 0.2 fusion.75
  120.0 0.3 broadcast_multiply_fusion.2
  120.3 0.2 broadcast_in_dim.11
  120.5 7.2 %scatter_fusion = f32[768,4,128]{2,1,0:T(4,128)S(1)} fusion(f32[768,4,128]{2,1,0:T(4,128)S(1)} %broadcast_in_dim.11, s32[256]{0:T(256)} %bitcast.137, f32[256,4,128]{2,1,0:T(4,128)S(1)} %broadcast_multiply_fusion.2), kind=kCustom, calls=%fused_computation.5 | custom fusion | bytes 1573888 | tf_op jit(solution)/shard_map/scatter | solution.py:147
  127.7 1.2 convert_element_type.116
  128.9 4.5 %all-to-all-start.3 = ((bf16[128,6,4,128]{3,2,1,0:T(4,128)(2,1)}), bf16[128,6,4,128]{3,2,1,0:T(4,128)(2,1)S(1)}, u32[]{:S(2)}, u32[]{:S(2)}) async-start(bf16[128,6,4,128]{3,2,1,0:T(4,128)(2,1)} %bitcast.33), calls=%async_computation.3 | async-start | bytes 1572864 | tf_op jit(solution)/shard_map/all_to_all | solution.py:149
  133.6 0.3 reshape.527
  133.9 15.9 %all-to-all-done.3 = bf16[128,6,4,128]{3,2,1,0:T(4,128)(2,1)S(1)} async-done(((bf16[128,6,4,128]{3,2,1,0:T(4,128)(2,1)}), bf16[128,6,4,128]{3,2,1,0:T(4,128)(2,1)S(1)}, u32[]{:S(2)}, u32[]{:S(2)}) %all-to-all-start.3) | async-done | bytes 786464 | tf_op jit(solution)/shard_map/all_to_all | solution.py:149
  149.8 19.1 %scatter_custom_fusion.2 = f32[8192,128]{1,0:T(8,128)} fusion(s32[3072]{0:T(1024)S(1)} %bitcast.132, f32[]{:T(128)} %constant.49.clone.1, bf16[3072,128]{1,0:T(8,128)(2,1)S(1)} %bitcast.125), kind=kCustom, calls=%fused_computation.43 | custom fusion | flops 786432 | bytes 4980740 | tf_op jit(solution)/shard_map/scatter-add | solution.py:162
  168.9 4.6 %copy.72 = f32[128,64,128]{0,1,2:T(8,128)S(1)} copy(f32[128,64,128]{0,2,1:T(8,128)} %bitcast.123) | data formatting | bytes 8388608 | tf_op jit(solution)/shard_map/reshape | solution.py:164
  173.7 4.8 %collective-permute-start.9 = (f32[128,2,128]{0,1,2:T(2,128)S(1)}, f32[128,2,128]{0,1,2:T(2,128)S(1)}, u32[]{:S(2)}, u32[]{:S(2)}) collective-permute-start(f32[128,2,128]{0,1,2:T(2,128)S(1)} %get-tuple-element.17), channel_id=1, source_target_pairs={{8,0},{16,8},{24,16},{32,24},{40,32},{48,40},{56,48},{64,56},{72,6... | collective-permute-start | bytes 393224 | tf_op jit(solution)/shard_map/ppermute | solution.py:18
  178.5 2.4 %collective-permute-done.8 = f32[128,2,128]{0,1,2:T(2,128)S(1)} collective-permute-done((f32[128,2,128]{0,1,2:T(2,128)S(1)}, f32[128,2,128]{0,1,2:T(2,128)S(1)}, u32[]{:S(2)}, u32[]{:S(2)}) %collective-permute-start.8) | collective-permute-done | bytes 131104 | tf_op jit(solution)/shard_map/ppermute | solution.py:15
  180.9 2.3 %collective-permute-start.10 = (f32[128,68,2]{0,1,2:T(8,128)S(1)}, f32[128,68,2]{0,1,2:T(8,128)S(1)}, u32[]{:S(2)}, u32[]{:S(2)}) collective-permute-start(f32[128,68,2]{0,1,2:T(8,128)S(1)} %get-tuple-element.12), channel_id=1, source_target_pairs={{0,1},{1,2},{2,3},{3,4},{4,5},{5,6},{6,7},{7,0},{8,9},{9,10},{10,1... | collective-permute-start | bytes 208904 | tf_op jit(solution)/shard_map/ppermute | solution.py:15
  183.3 1.3 collective-permute-done.10
  184.6 2.7 %collective-permute-done.11 = f32[128,68,2]{0,1,2:T(8,128)S(1)} collective-permute-done((f32[128,68,2]{0,1,2:T(8,128)S(1)}, f32[128,68,2]{0,1,2:T(8,128)S(1)}, u32[]{:S(2)}, u32[]{:S(2)}) %collective-permute-start.11) | collective-permute-done | bytes 69664 | tf_op jit(solution)/shard_map/ppermute | solution.py:18
  187.3 4.7 %pad_maximum_fusion.1 = (f32[128,68,132]{0,1,2:T(8,128)S(1)}, f32[128,68,132]{0,1,2:T(8,128)S(1)}) fusion(f32[128,68,2]{0,1,2:T(8,128)S(1)} %collective-permute-done.11, f32[128,2,128]{0,1,2:T(2,128)S(1)} %collective-permute-done.9, f32[128,64,128]{0,1,2:T(8,128)} %copy-done.4, f32[128,2,128]{0,1,2:T(2,128)S(1)} %collective-permute-done.8, ...), kind=kLoop, calls=%fused_computation.8 | loop fusion | flops 5744640 | bytes 13823040 | tf_op jit(solution)/shard_map/concatenate | solution.py:19
  192.0 3.9 %broadcast_multiply_fusion.1 = (f32[128,66,130]{0,1,2:T(8,128)S(1)}, f32[128,66,130]{0,1,2:T(8,128)S(1)}) fusion(f32[66,130]{0,1:T(8,128)S(1)} %copy.63, f32[128,68,132]{0,1,2:T(8,128)S(1)} %get-tuple-element.11, f32[128,68,132]{0,1,2:T(8,128)S(1)} %get-tuple-element.10), kind=kLoop, calls=%fused_computation.42 | loop fusion | flops 7687680 | bytes 35178000 | tf_op jit(solution)/shard_map/mul | solution.py:37
  195.9 4.5 %fusion.9 = f32[128,64,128]{0,1,2:T(8,128)} fusion(f32[128,64,128]{0,1,2:T(8,128)S(1)} %copy-done.3, f32[128,66,130]{0,1,2:T(8,128)S(1)} %get-tuple-element.6, f32[128,66,130]{0,1,2:T(8,128)S(1)} %get-tuple-element.7), kind=kLoop, calls=%fused_computation.30 | loop fusion | flops 7340032 | bytes 33554432 | tf_op jit(solution)/shard_map/add | solution.py:165
  200.4 5.4 %copy.77 = f32[128,64,128]{2,1,0:T(8,128)} copy(f32[128,64,128]{0,1,2:T(8,128)} %fusion.9) | data formatting | bytes 8388608
  (71 shorter events, 1.7 us)
Async XLA Ops:
  0.6 117.0 %copy-start = (bf16[512,616]{0,1:T(8,128)(2,1)S(1)}, bf16[512,616]{0,1:T(8,128)(2,1)}, u32[]{:S(2)}) copy-start(bf16[512,616]{0,1:T(8,128)(2,1)} %param.25) | copy-start | bytes 1892356
  1.4 32.7 %collective-permute-start.4 = (f32[2,128]{1,0:T(2,128)S(1)}, f32[2,128]{1,0:T(2,128)S(1)}, u32[]{:S(2)}, u32[]{:S(2)}) collective-permute-start(f32[2,128]{1,0:T(2,128)S(1)} %get-tuple-element.30), channel_id=1, source_target_pairs={{0,8},{8,16},{16,24},{24,32},{32,40},{40,48},{48,56},{56,64},{64,7... | collective-permute-start | bytes 3080 | tf_op jit(solution)/shard_map/ppermute | solution.py:15
  3.5 30.6 %collective-permute-start.5 = (f32[2,128]{1,0:T(2,128)S(1)}, f32[2,128]{1,0:T(2,128)S(1)}, u32[]{:S(2)}, u32[]{:S(2)}) collective-permute-start(f32[2,128]{1,0:T(2,128)S(1)} %get-tuple-element.31), channel_id=1, source_target_pairs={{8,0},{16,8},{24,16},{32,24},{40,32},{48,40},{56,48},{64,56},{72,6... | collective-permute-start | bytes 3080 | tf_op jit(solution)/shard_map/ppermute | solution.py:18
  9.5 23.4 %copy-start.14 = (f32[2,256]{1,0:T(2,128)S(1)}, f32[2,256]{1,0:T(2,128)}, u32[]{:S(2)}) copy-start(f32[2,256]{1,0:T(2,128)} %param.18) | copy-start | bytes 6148
  9.5 24.6 %copy-start.9 = (f32[64,128]{1,0:T(8,128)S(1)}, f32[64,128]{1,0:T(8,128)}, u32[]{:S(2)}) copy-start(f32[64,128]{1,0:T(8,128)} %param.15) | copy-start | bytes 98308
  11.1 29.5 %copy-start.13 = (s32[256,1]{0,1:T(1,128)}, s32[256,1]{0,1:T(1,128)S(1)}, u32[]{:S(2)}) copy-start(s32[256,1]{0,1:T(1,128)S(1)} %compare_select_fusion.2) | copy-start | bytes 3076
  13.4 27.5 %all-to-all-start = ((s32[128,1,6]{2,1,0:T(1,128)}), s32[128,1,6]{2,1,0:T(1,128)S(1)}, u32[]{:S(2)}, u32[]{:S(2)}) async-start(s32[128,1,6]{2,1,0:T(1,128)} %bitcast.11), calls=%async_computation | async-start | bytes 131072 | tf_op jit(solution)/shard_map/all_to_all | solution.py:114
  27.3 15.4 %collective-permute-start = (f32[128,2,128]{0,1,2:T(2,128)}, f32[128,2,128]{0,1,2:T(2,128)S(1)}, u32[]{:S(2)}, u32[]{:S(2)}) collective-permute-start(f32[128,2,128]{0,1,2:T(2,128)} %get-tuple-element.18), channel_id=1, source_target_pairs={{0,8},{8,16},{16,24},{24,32},{32,40},{40,48},{48,56},{56,64},{64,7... | collective-permute-start | bytes 393224 | tf_op jit(solution)/shard_map/ppermute | solution.py:15
  28.7 14.1 %collective-permute-start.1 = (f32[128,2,128]{0,1,2:T(2,128)}, f32[128,2,128]{0,1,2:T(2,128)S(1)}, u32[]{:S(2)}, u32[]{:S(2)}) collective-permute-start(f32[128,2,128]{0,1,2:T(2,128)} %get-tuple-element.19), channel_id=1, source_target_pairs={{8,0},{16,8},{24,16},{32,24},{40,32},{48,40},{56,48},{64,56},{72,6... | collective-permute-start | bytes 393224 | tf_op jit(solution)/shard_map/ppermute | solution.py:18
  34.2 6.4 %collective-permute-start.6 = (f32[68,2]{1,0:T(8,128)S(1)}, f32[68,2]{1,0:T(8,128)S(1)}, u32[]{:S(2)}, u32[]{:S(2)}) collective-permute-start(f32[68,2]{1,0:T(8,128)S(1)} %get-tuple-element.28), channel_id=1, source_target_pairs={{0,1},{1,2},{2,3},{3,4},{4,5},{5,6},{6,7},{7,0},{8,9},{9,10},{10,1... | collective-permute-start | bytes 1640 | tf_op jit(solution)/shard_map/ppermute | solution.py:15
  35.9 4.7 %collective-permute-start.7 = (f32[68,2]{1,0:T(8,128)S(1)}, f32[68,2]{1,0:T(8,128)S(1)}, u32[]{:S(2)}, u32[]{:S(2)}) collective-permute-start(f32[68,2]{1,0:T(8,128)S(1)} %get-tuple-element.29), channel_id=1, source_target_pairs={{1,0},{2,1},{3,2},{4,3},{5,4},{6,5},{7,6},{0,7},{9,8},{10,9},{11,1... | collective-permute-start | bytes 1640 | tf_op jit(solution)/shard_map/ppermute | solution.py:18
  43.7 19.4 %collective-permute-start.3 = (f32[128,68,2]{0,1,2:T(8,128)S(1)}, f32[128,68,2]{0,1,2:T(8,128)S(1)}, u32[]{:S(2)}, u32[]{:S(2)}) collective-permute-start(f32[128,68,2]{0,1,2:T(8,128)S(1)} %get-tuple-element.14), channel_id=1, source_target_pairs={{1,0},{2,1},{3,2},{4,3},{5,4},{6,5},{7,6},{0,7},{9,8},{10,9},{11,1... | collective-permute-start | bytes 208904 | tf_op jit(solution)/shard_map/ppermute | solution.py:18
  45.8 17.3 %collective-permute-start.2 = (f32[128,68,2]{0,1,2:T(8,128)S(1)}, f32[128,68,2]{0,1,2:T(8,128)S(1)}, u32[]{:S(2)}, u32[]{:S(2)}) collective-permute-start(f32[128,68,2]{0,1,2:T(8,128)S(1)} %get-tuple-element.15), channel_id=1, source_target_pairs={{0,1},{1,2},{2,3},{3,4},{4,5},{5,6},{6,7},{7,0},{8,9},{9,10},{10,1... | collective-permute-start | bytes 208904 | tf_op jit(solution)/shard_map/ppermute | solution.py:15
  57.3 30.4 %all-to-all-start.1 = ((bf16[128,6,4,128]{3,2,1,0:T(4,128)(2,1)}), bf16[128,6,4,128]{3,2,1,0:T(4,128)(2,1)}, u32[]{:S(2)}, u32[]{:S(2)}) async-start(bf16[128,6,4,128]{3,2,1,0:T(4,128)(2,1)} %bitcast.16), calls=%async_computation.1 | async-start | bytes 1572864 | tf_op jit(solution)/shard_map/all_to_all | solution.py:126
  63.0 3.5 %copy-start.2 = (f32[128,64,128]{0,1,2:T(8,128)S(1)}, f32[128,64,128]{0,1,2:T(8,128)}, u32[]{:S(2)}) copy-start(f32[128,64,128]{0,1,2:T(8,128)} %copy.60) | copy-start | bytes 12582916
  66.5 5.2 %copy-start.10 = (f32[64,128]{0,1:T(8,128)S(1)}, f32[64,128]{0,1:T(8,128)}, u32[]{:S(2)}) copy-start(f32[64,128]{0,1:T(8,128)} %copy.64) | copy-start | bytes 98308
  76.2 25.5 %copy-start.7 = (bf16[128,512]{1,0:T(8,128)(2,1)S(1)}, bf16[128,512]{1,0:T(8,128)(2,1)}, u32[]{:S(2)}) copy-start(bf16[128,512]{1,0:T(8,128)(2,1)} %param.21) | copy-start | bytes 393220
  76.2 26.5 %copy-start.5 = (bf16[512,512]{1,0:T(8,128)(2,1)S(1)}, bf16[512,512]{1,0:T(8,128)(2,1)}, u32[]{:S(2)}) copy-start(bf16[512,512]{1,0:T(8,128)(2,1)} %param.23) | copy-start | bytes 1572868
  87.7 28.4 %copy-start.11 = (f32[256]{0:T(256)S(1)}, f32[256]{0:T(256)}, u32[]{:S(2)}) copy-start(f32[256]{0:T(256)} %get-tuple-element.41) | copy-start | bytes 3076
  87.7 28.4 %copy-start.12 = (f32[256]{0:T(256)S(1)}, f32[256]{0:T(256)}, u32[]{:S(2)}) copy-start(f32[256]{0:T(256)} %get-tuple-element.42) | copy-start | bytes 3076
  87.7 26.2 %all-to-all-start.2 = ((bf16[128,6,4,128]{3,2,1,0:T(4,128)(2,1)}), bf16[128,6,4,128]{3,2,1,0:T(4,128)(2,1)S(1)}, u32[]{:S(2)}, u32[]{:S(2)}) async-start(bf16[128,6,4,128]{3,2,1,0:T(4,128)(2,1)} %bitcast.124), calls=%async_computation.2 | async-start | bytes 1572864 | tf_op jit(solution)/shard_map/all_to_all | solution.py:133
  115.0 4.9 %copy-start.8 = (f32[256,4]{1,0:T(8,128)S(1)}, f32[256,4]{1,0:T(8,128)}, u32[]{:S(2)}) copy-start(f32[256,4]{1,0:T(8,128)} %copy.71) | copy-start | bytes 12292
  119.1 0.9 copy-start.6
  128.9 20.9 %all-to-all-start.3 = ((bf16[128,6,4,128]{3,2,1,0:T(4,128)(2,1)}), bf16[128,6,4,128]{3,2,1,0:T(4,128)(2,1)S(1)}, u32[]{:S(2)}, u32[]{:S(2)}) async-start(bf16[128,6,4,128]{3,2,1,0:T(4,128)(2,1)} %bitcast.33), calls=%async_computation.3 | async-start | bytes 1572864 | tf_op jit(solution)/shard_map/all_to_all | solution.py:149
  173.6 7.3 %copy-start.4 = (f32[128,64,128]{0,1,2:T(8,128)}, f32[128,64,128]{0,1,2:T(8,128)S(1)}, u32[]{:S(2)}) copy-start(f32[128,64,128]{0,1,2:T(8,128)S(1)} %copy.72) | copy-start | bytes 12582916
  173.7 7.2 %collective-permute-start.8 = (f32[128,2,128]{0,1,2:T(2,128)S(1)}, f32[128,2,128]{0,1,2:T(2,128)S(1)}, u32[]{:S(2)}, u32[]{:S(2)}) collective-permute-start(f32[128,2,128]{0,1,2:T(2,128)S(1)} %get-tuple-element.16), channel_id=1, source_target_pairs={{0,8},{8,16},{16,24},{24,32},{32,40},{40,48},{48,56},{56,64},{64,7... | collective-permute-start | bytes 393224 | tf_op jit(solution)/shard_map/ppermute | solution.py:15
  173.7 7.1 %collective-permute-start.9 = (f32[128,2,128]{0,1,2:T(2,128)S(1)}, f32[128,2,128]{0,1,2:T(2,128)S(1)}, u32[]{:S(2)}, u32[]{:S(2)}) collective-permute-start(f32[128,2,128]{0,1,2:T(2,128)S(1)} %get-tuple-element.17), channel_id=1, source_target_pairs={{8,0},{16,8},{24,16},{32,24},{40,32},{48,40},{56,48},{64,56},{72,6... | collective-permute-start | bytes 393224 | tf_op jit(solution)/shard_map/ppermute | solution.py:18
  180.9 3.7 %collective-permute-start.10 = (f32[128,68,2]{0,1,2:T(8,128)S(1)}, f32[128,68,2]{0,1,2:T(8,128)S(1)}, u32[]{:S(2)}, u32[]{:S(2)}) collective-permute-start(f32[128,68,2]{0,1,2:T(8,128)S(1)} %get-tuple-element.12), channel_id=1, source_target_pairs={{0,1},{1,2},{2,3},{3,4},{4,5},{5,6},{6,7},{7,0},{8,9},{9,10},{10,1... | collective-permute-start | bytes 208904 | tf_op jit(solution)/shard_map/ppermute | solution.py:15
  183.2 4.1 %collective-permute-start.11 = (f32[128,68,2]{0,1,2:T(8,128)S(1)}, f32[128,68,2]{0,1,2:T(8,128)S(1)}, u32[]{:S(2)}, u32[]{:S(2)}) collective-permute-start(f32[128,68,2]{0,1,2:T(8,128)S(1)} %get-tuple-element.13), channel_id=1, source_target_pairs={{1,0},{2,1},{3,2},{4,3},{5,4},{6,5},{7,6},{0,7},{9,8},{10,9},{11,1... | collective-permute-start | bytes 208904 | tf_op jit(solution)/shard_map/ppermute | solution.py:18
  191.9 3.9 %copy-start.3 = (f32[128,64,128]{0,1,2:T(8,128)S(1)}, f32[128,64,128]{0,1,2:T(8,128)}, u32[]{:S(2)}) copy-start(f32[128,64,128]{0,1,2:T(8,128)} %copy.60) | copy-start | bytes 12582916
  195.9 9.9 %copy-start.1 = (bf16[512,616]{0,1:T(8,128)(2,1)S(1)}, bf16[512,616]{0,1:T(8,128)(2,1)}, u32[]{:S(2)}) copy-start(bf16[512,616]{0,1:T(8,128)(2,1)} %param.25) | copy-start | bytes 1892356
where the time goes:
time: 207 us; the launch traced here: 206 us
  local copies, waits for them, and re-layouts  64.2 us (31%)
  other arithmetic  52 us (25%)
  starting transfers between devices  50.1 us (24%)
  waiting for transfers between devices  32.5 us (16%)
  matrix products  5.82 us (3%)
    scatter-add x1, other arithmetic, per_device(): gathered = jnp.zeros((rows_x * rows_y, levels), jnp.float32).at[source.re...  19.1 us
    ppermute x6, starting transfers between devices, padded_2(): lax.ppermute(lax.slice_in_dim(block, 0, width, axis=dim), axis, backward)  16 us
    all_to_all x1, waiting for transfers between devices, per_device(): lax.all_to_all(pieces.reshape(owners, capacity, 4, levels).astype(jnp.bfl...  15.9 us
    unnamed x35, local copies, waits for them, and re-layouts  14.9 us
    gather x1, local copies, waits for them, and re-layouts, per_device(): inc_cols[source].reshape(owners, capacity, 4, levels)  11.5 us
    gather x1, local copies, waits for them, and re-layouts, per_device(): bg_cols[source].reshape(owners, capacity, 4, levels)  11.5 us
    all_to_all x1, waiting for transfers between devices, per_device(): lax.all_to_all(inc_cols[source].reshape(owners, capacity, 4, levels), ('t...  10.2 us
    all_to_all x1, starting transfers between devices, per_device(): lax.all_to_all(inc_cols[source].reshape(owners, capacity, 4, levels), ('t...  9.76 us
  transfers between devices with their start and end apart: 16, of which 5 were waited for; matrix products, arithmetic and copies ran while one was open for 30% of the time, Pallas kernels for 0%

commit v1 on v0

v1 whole, which is shorter than its diff:
```python
import jax
import jax.numpy as jnp
from jax import lax
from jax.experimental import pallas as pl
from jax.experimental.pallas import tpu as pltpu
from jax.sharding import PartitionSpec as P

F32 = jnp.float32
BF16 = jnp.bfloat16
LEV = 128
BX = 64
BY = 128
CELLS = BX * BY
OWN = 256
DEV = 128
CAP = 6
ROWS = 8
SLOTS = CAP * DEV
HID = 512
CH = 616
PX = BX + 4
PY = BY + 16
CHUNK = 8
VMEM_LIMIT = 56 * 1024 * 1024


def params(**extra):
    return pltpu.CompilerParams(vmem_limit_bytes=VMEM_LIMIT, **extra)


def nn(a, b):
    return jnp.dot(a, b, preferred_element_type=F32)


def nt(a, b):
    return lax.dot_general(a, b, (((1,), (1,)), ((), ())), preferred_element_type=F32)


def iota(shape, dim):
    return lax.broadcasted_iota(jnp.int32, shape, dim)


def split_two(a):
    high = a.astype(BF16)
    return high, (a - high.astype(F32)).astype(BF16)


def eye_pair():
    row = iota((LEV, 2 * LEV), 0)
    col = iota((LEV, 2 * LEV), 1)
    return ((col == row) | (col == row + LEV)).astype(BF16)


def request_kernel(holder, anchor, frac, innov, ivar, w_third, out):
    held = holder[...]
    marks = (iota((DEV, OWN), 0) == held).astype(BF16)
    before = (iota((OWN, OWN), 0) < iota((OWN, OWN), 1)).astype(BF16)
    rank = jnp.sum(marks.astype(F32) * nn(marks, before), axis=0, keepdims=True).astype(jnp.int32)
    at = anchor[...].astype(F32)
    x = jnp.floor((at + 0.5) * (1.0 / (BY - 1)))
    y = at - (BY - 1) * x
    fields = [x + 1.0, y]
    for dim in range(2):
        value = frac[dim : dim + 1, :]
        for _ in range(3):
            piece = value.astype(BF16).astype(F32)
            fields.append(piece)
            value = value - piece
    fields = jnp.concatenate(fields, axis=0)
    fields = jnp.concatenate([fields] * (LEV // 8), axis=0)
    fields = jnp.where((iota((LEV, OWN), 0) >> 3) == rank, fields, 0.0).astype(BF16)
    scaled = (innov[...] * ivar[...]).astype(BF16)
    pulled = nt(scaled, w_third[...]).astype(BF16)
    row = iota((DEV * ROWS, OWN), 0)
    to_slot = (row == held * ROWS + rank).astype(BF16)
    to_fields = (row == held * ROWS + CAP).astype(BF16)
    out[:, :LEV] = (nn(to_slot, pulled[:, :LEV]) + nt(to_fields, fields)).astype(BF16)
    out[:, LEV:] = nn(to_slot, pulled[:, LEV:]).astype(BF16)


def requests(holder, anchor, frac, innov, ivar, w_third):
    return pl.pallas_call(
        request_kernel,
        out_shape=jax.ShapeDtypeStruct((DEV * ROWS, HID), BF16),
        compiler_params=params(),
        name="requests",
    )(holder, anchor, frac, innov, ivar, w_third)


def columns_kernel(control, background, spread, ct, bgt, x_up, x_down, y_up, y_down, wide, planes):
    step = pl.program_id(0)
    pair = eye_pair()
    wide[...] = background[...].astype(F32).reshape(LEV * CHUNK, BY)
    flat = control.reshape(LEV * CHUNK, BY)
    for i in range(CHUNK):
        here = pl.ds(i, LEV, stride=CHUNK)
        high, low = split_two(flat[here, :])
        back = wide[here, :].astype(BF16)
        both = jnp.concatenate(
            [
                jnp.concatenate([high, low], axis=1),
                jnp.concatenate([back, jnp.zeros_like(back)], axis=1),
            ],
            axis=0,
        )
        turned = nt(pair, both)
        ct[i] = turned[:, :LEV]
        bgt[i] = turned[:, LEV:]
        for n, y in enumerate((0, 1, BY - 2, BY - 1)):
            planes[n, pl.ds(step * CHUNK + i, 1), :] = turned[y : y + 1, :LEV]

    @pl.when(step == 0)
    def _():
        x_down[:BY, :] = ct[0].astype(BF16)
        x_down[BY : 2 * BY, :] = ct[1].astype(BF16)

    @pl.when(step == pl.num_programs(0) - 1)
    def _():
        x_up[:BY, :] = ct[CHUNK - 2].astype(BF16)
        x_up[BY : 2 * BY, :] = ct[CHUNK - 1].astype(BF16)
        s = spread[...]
        turned = jnp.transpose(jnp.concatenate([s, s], axis=0))

        def rows(two):
            high, low = split_two(two)
            zero = jnp.zeros((12, BY), F32)
            return jnp.concatenate([high.astype(F32), low.astype(F32), zero], axis=0).astype(BF16)

        x_down[2 * BY :, :] = rows(s[0:2, :])
        x_up[2 * BY :, :] = rows(s[BX - 2 : BX, :])
        y_down[: 2 * BX, :] = planes[0:2].reshape(2 * BX, LEV).astype(BF16)
        y_up[: 2 * BX, :] = planes[2:4].reshape(2 * BX, LEV).astype(BF16)
        y_down[2 * BX :, :] = rows(turned[0:2, :])
        y_up[2 * BX :, :] = rows(turned[BY - 2 : BY, :])


def to_columns(control, background, spread):
    keep = lambda i: (0, 0)
    return pl.pallas_call(
        columns_kernel,
        grid=(BX // CHUNK,),
        in_specs=[
            pl.BlockSpec((LEV, CHUNK, BY), lambda i: (0, i, 0)),
            pl.BlockSpec((LEV, CHUNK, BY), lambda i: (0, i, 0)),
            pl.BlockSpec((BX, BY), keep),
        ],
        out_specs=[
            pl.BlockSpec((CHUNK, BY, LEV), lambda i: (i, 0, 0)),
            pl.BlockSpec((CHUNK, BY, LEV), lambda i: (i, 0, 0)),
            pl.BlockSpec((2 * BY + 16, LEV), keep),
            pl.BlockSpec((2 * BY + 16, LEV), keep),
            pl.BlockSpec((2 * BX + 16, LEV), keep),
            pl.BlockSpec((2 * BX + 16, LEV), keep),
        ],
        out_shape=[
            jax.ShapeDtypeStruct((BX, BY, LEV), F32),
            jax.ShapeDtypeStruct((BX, BY, LEV), F32),
            jax.ShapeDtypeStruct((2 * BY + 16, LEV), BF16),
            jax.ShapeDtypeStruct((2 * BY + 16, LEV), BF16),
            jax.ShapeDtypeStruct((2 * BX + 16, LEV), BF16),
            jax.ShapeDtypeStruct((2 * BX + 16, LEV), BF16),
        ],
        scratch_shapes=[
            pltpu.VMEM((LEV * CHUNK, BY), F32),
            pltpu.VMEM((4, BX, LEV), F32),
        ],
        compiler_params=params(dimension_semantics=("arbitrary",)),
        name="columns",
    )(control, background, spread)


def shift(array, axis, by):
    count = lax.axis_size(axis)
    return lax.ppermute(array, axis, [(i, (i + by) % count) for i in range(count)])


def rims_around(x_up, x_down, y_up, y_down):
    y_low = shift(y_up, "obs", 1)
    y_high = shift(y_down, "obs", -1)
    x_low = shift(x_up, "tile", 1)
    x_high = shift(x_down, "tile", -1)

    def corner(row):
        low, high = BX + row, row
        return jnp.concatenate(
            [y_low[low : low + 1], y_high[high : high + 1], y_low[2 * BX :], y_high[2 * BX :]], axis=0
        )

    low = shift(corner(BX - 1), "tile", 1)
    high = shift(corner(0), "tile", -1)
    return x_low, x_high, y_low, y_high, low, high


def laplace(field, x, first, count):
    total = field[x + 1, pl.ds(first, count), :] + field[x - 1, pl.ds(first, count), :]
    total = total + field[x, pl.ds(first + 1, count), :]
    total = total + field[x, pl.ds(first - 1, count), :]
    return total - 4.0 * field[x, pl.ds(first, count), :]


def plane(field, x, y, count):
    flat = field.reshape(PX * PY, LEV)
    return flat[pl.ds(x * PY + y, count, stride=PY), :]


def set_plane(field, x, y, count, value):
    flat = field.reshape(PX * PY, LEV)
    flat[pl.ds(x * PY + y, count, stride=PY), :] = value


def plane_laplace(field, y):
    total = plane(field, 3, y, BX) + plane(field, 1, y, BX)
    total = total + plane(field, 2, y + 1, BX) + plane(field, 2, y - 1, BX)
    return total - 4.0 * plane(field, 2, y, BX)


def lanes(column):
    return jnp.broadcast_to(column, (column.shape[0], LEV))


def fill_rims(field, x_low, x_high, y_low, y_high, low, high):
    for n in range(2):
        field[n, 8 : 8 + BY, :] = x_low[n * BY : (n + 1) * BY, :].astype(F32)
        field[BX + 2 + n, 8 : 8 + BY, :] = x_high[n * BY : (n + 1) * BY, :].astype(F32)
        set_plane(field, 2, 6 + n, BX, y_low[n * BX : (n + 1) * BX, :].astype(F32))
        set_plane(field, 2, 8 + BY + n, BX, y_high[n * BX : (n + 1) * BX, :].astype(F32))
    low_rows = low[...].astype(F32)
    high_rows = high[...].astype(F32)
    field[1, 7:8, :] = low_rows[0:1]
    field[1, 8 + BY : 9 + BY, :] = low_rows[1:2]
    field[BX + 2, 7:8, :] = high_rows[0:1]
    field[BX + 2, 8 + BY : 9 + BY, :] = high_rows[1:2]


def joined(rows, at):
    block = rows[at : at + 16, :].astype(F32)
    return block[0:2] + block[2:4]


def increment_kernel(ct, spread, x_low, x_high, y_low, y_high, low, high, inc, coef, field, first):
    square = jnp.concatenate(
        [joined(x_low, 2 * BY), spread[...], joined(x_high, 2 * BY), jnp.zeros((BY - PX, BY), F32)],
        axis=0,
    )
    turned = jnp.transpose(square)

    def broadcast(x, carry):
        moved = pltpu.roll(turned, (LEV - x) % LEV, 1)
        coef[x, 8 : 8 + BY, :] = lanes(moved[:, 0:1])
        return carry

    lax.fori_loop(0, PX, broadcast, 0)
    sides = jnp.concatenate(
        [joined(y_low, 2 * BX), joined(y_high, 2 * BX), jnp.zeros((BY - 4, BY), F32)], axis=0
    )
    sides = jnp.transpose(sides)[:BX, :]
    for n in range(2):
        set_plane(coef, 2, 6 + n, BX, lanes(sides[:, n : n + 1]))
        set_plane(coef, 2, 8 + BY + n, BX, lanes(sides[:, 2 + n : 3 + n]))
    for rows, x, lane in ((low, 1, BX - 1), (high, BX + 2, 0)):
        block = rows[...].astype(F32)
        left = block[2:4] + block[4:6]
        right = block[18:20] + block[20:22]
        coef[x, 7:8, :] = lanes(left[1:2, lane : lane + 1])
        coef[x, 8 + BY : 9 + BY, :] = lanes(right[0:1, lane : lane + 1])
    field[2 : 2 + BX, 8 : 8 + BY, :] = ct[...]
    fill_rims(field, x_low, x_high, y_low, y_high, low, high)

    def sweep_one(x, carry):
        middle = field[x, 8 : 8 + BY, :]
        first[x, 8 : 8 + BY, :] = middle + coef[x, 8 : 8 + BY, :] * laplace(field, x, 8, BY)
        return carry

    lax.fori_loop(1, PX - 1, sweep_one, 0)
    for y in (7, 8 + BY):
        moved = plane(field, 2, y, BX) + plane(coef, 2, y, BX) * plane_laplace(field, y)
        set_plane(first, 2, y, BX, moved)

    def sweep_two(x, carry):
        middle = first[x, 8 : 8 + BY, :]
        result = middle + coef[x, 8 : 8 + BY, :] * laplace(first, x, 8, BY)
        inc[x - 2] = result.astype(BF16).astype(F32)
        return carry

    lax.fori_loop(2, PX - 2, sweep_two, 0)


def increments(ct, spread, rims):
    return pl.pallas_call(
        increment_kernel,
        out_shape=[
            jax.ShapeDtypeStruct((BX, BY, LEV), F32),
            jax.ShapeDtypeStruct((PX, PY, LEV), F32),
        ],
        scratch_shapes=[pltpu.VMEM((PX, PY, LEV), F32), pltpu.VMEM((PX, PY, LEV), F32)],
        compiler_params=params(),
        name="increment",
    )(ct, spread, *rims)


def decode(rows):
    back = lambda n: pltpu.roll(rows, LEV - n, 1)
    frac_x = back(2) + back(3) + back(4)
    frac_y = back(5) + back(6) + back(7)
    valid = rows > 0.5
    cell = jnp.where(valid, (rows - 1.0) * BY + back(1), 0.0).astype(jnp.int32)
    off = lambda w: jnp.where(valid, w, 0.0)
    return cell, (
        off((1.0 - frac_x) * (1.0 - frac_y)),
        off(frac_x * (1.0 - frac_y)),
        off((1.0 - frac_x) * frac_y),
        off(frac_x * frac_y),
    )


def gather_kernel(got, bgt, inct, reply, slots, wide, cells, table, ga, gb, gc, gd, spaced):
    wide[...] = got[...].astype(F32).reshape(DEV * ROWS, LEV)
    cell, weights = decode(wide[pl.ds(CAP, DEV, stride=ROWS), :])
    cells[...] = cell
    pltpu.sync_copy(cells, table)
    for k in range(CAP):

        def fetch(step, carry):
            for n in range(8):
                owner = step * 8 + n
                at = table[owner, 8 * k]
                to = pl.ds(2 * (k * DEV + owner), 2)
                ga[to, :] = bgt[pl.ds(at, 2), :]
                gb[to, :] = bgt[pl.ds(at + BY, 2), :]
                gc[to, :] = inct[pl.ds(at, 2), :]
                gd[to, :] = inct[pl.ds(at + BY, 2), :]
            return carry

        lax.fori_loop(0, DEV // 8, fetch, 0)
    spaced[...] = jnp.zeros_like(spaced)
    for k in range(CAP):
        w = [lanes(weight[:, 8 * k : 8 * k + 1]) for weight in weights]
        even = pl.ds(2 * DEV * k, DEV, stride=2)
        odd = pl.ds(2 * DEV * k + 1, DEV, stride=2)
        for n, (one, two) in enumerate(((ga, gb), (gc, gd))):
            mixed = w[0] * one[even, :] + w[1] * two[even, :]
            mixed = mixed + w[2] * one[odd, :]
            mixed = mixed + w[3] * two[odd, :]
            slots[k * DEV : (k + 1) * DEV, n * LEV : (n + 1) * LEV] = mixed.astype(BF16)
            spaced[n, pl.ds(k, DEV, stride=ROWS), :] = mixed
    reply[:, :LEV] = spaced[0].astype(BF16)
    reply[:, LEV:] = spaced[1].astype(BF16)


def gathered(got, bgt, inct):
    rows = pltpu.VMEM((2 * SLOTS, LEV), F32)
    whole = pl.BlockSpec(memory_space=pltpu.VMEM)
    return pl.pallas_call(
        gather_kernel,
        grid=(1,),
        in_specs=[pl.BlockSpec((DEV, ROWS, LEV), lambda i: (0, 0, 0)), whole, whole],
        out_specs=[whole, whole],
        out_shape=[
            jax.ShapeDtypeStruct((DEV * ROWS, 2 * LEV), BF16),
            jax.ShapeDtypeStruct((SLOTS, 2 * LEV), BF16),
        ],
        scratch_shapes=[
            pltpu.VMEM((DEV * ROWS, LEV), F32),
            pltpu.VMEM((DEV, LEV), jnp.int32),
            pltpu.SMEM((DEV, LEV), jnp.int32),
            rows,
            rows,
            rows,
            rows,
            pltpu.VMEM((2, DEV * ROWS, LEV), F32),
        ],
        compiler_params=params(),
        name="gather",
    )(got, bgt, inct)


def tangent(base, delta, w_first, b_first, w_second, b_second):
    h_one = jnp.tanh(nn(base, w_first) + b_first)
    d_one = 1.0 - h_one * h_one
    h_two = jnp.tanh(nn(h_one.astype(BF16), w_second) + b_second)
    d_two = 1.0 - h_two * h_two
    t_one = (d_one * nn(delta, w_first)).astype(BF16)
    t_two = (d_two * nn(t_one, w_second)).astype(BF16)
    return d_one, d_two, t_two


BLOCK = 256


def adjoint_kernel(
    got, slots, w_first, b_first, w_second, b_second, w_third, ivar,
    acc, x_up, x_down, y_up, y_down,
    wide, pulled, profile, cells, table, ca, cb,
):
    for n in range(HID // LEV):
        at = slice(n * LEV, (n + 1) * LEV)
        wide[...] = got[:, :, at].astype(F32).reshape(DEV * ROWS, LEV)
        for k in range(CAP):
            pulled[k * DEV : (k + 1) * DEV, at] = wide[pl.ds(k, DEV, stride=ROWS), :]
        if n == 0:
            cell, weights = decode(wide[pl.ds(CAP, DEV, stride=ROWS), :])
    cells[...] = cell
    pltpu.sync_copy(cells, table)

    def block(i, carry):
        here = pl.ds(pl.multiple_of(i * BLOCK, BLOCK), BLOCK)
        d_one, d_two, t_two = tangent(
            slots[here, :LEV], slots[here, LEV:],
            w_first[...], b_first[...], w_second[...], b_second[...],
        )
        change = nn(t_two, w_third[...]) * ivar[...]
        s_two = (d_two * (nt(change.astype(BF16), w_third[...]) - pulled[here, :])).astype(BF16)
        s_one = (d_one * nt(s_two, w_second[...])).astype(BF16)
        profile[here, :] = nt(s_one, w_first[...])
        return carry

    lax.fori_loop(0, SLOTS // BLOCK, block, 0)
    acc[...] = jnp.zeros_like(acc)
    for k in range(CAP):
        grad = profile[k * DEV : (k + 1) * DEV, :]
        w = [lanes(weight[:, 8 * k : 8 * k + 1]) for weight in weights]
        even = pl.ds(2 * DEV * k, DEV, stride=2)
        odd = pl.ds(2 * DEV * k + 1, DEV, stride=2)
        ca[even, :] = w[0] * grad
        cb[even, :] = w[1] * grad
        ca[odd, :] = w[2] * grad
        cb[odd, :] = w[3] * grad
    for k in range(CAP):

        def add(step, carry):
            for n in range(8):
                owner = step * 8 + n
                at = table[owner, 8 * k]
                there = pl.ds(2 * (k * DEV + owner), 2)
                one = acc[pl.ds(at, 2), :] + ca[there, :]
                two = acc[pl.ds(at + BY, 2), :] + cb[there, :]
                acc[pl.ds(at, 2), :] = one
                acc[pl.ds(at + BY, 2), :] = two
            return carry

        lax.fori_loop(0, DEV // 8, add, 0)
    x_down[...] = acc[: 2 * BY, :].astype(BF16)
    x_up[...] = acc[CELLS - 2 * BY :, :].astype(BF16)
    for n in range(2):
        y_down[n * BX : (n + 1) * BX, :] = acc[pl.ds(n, BX, stride=BY), :].astype(BF16)
        y_up[n * BX : (n + 1) * BX, :] = acc[pl.ds(BY - 2 + n, BX, stride=BY), :].astype(BF16)


def adjoint(got, slots, w_first, b_first, w_second, b_second, w_third, ivar):
    return pl.pallas_call(
        adjoint_kernel,
        out_shape=[
            jax.ShapeDtypeStruct((CELLS, LEV), F32),
            jax.ShapeDtypeStruct((2 * BY, LEV), BF16),
            jax.ShapeDtypeStruct((2 * BY, LEV), BF16),
            jax.ShapeDtypeStruct((2 * BX, LEV), BF16),
            jax.ShapeDtypeStruct((2 * BX, LEV), BF16),
        ],
        scratch_shapes=[
            pltpu.VMEM((DEV * ROWS, LEV), F32),
            pltpu.VMEM((SLOTS, HID), F32),
            pltpu.VMEM((SLOTS, LEV), F32),
            pltpu.VMEM((DEV, LEV), jnp.int32),
            pltpu.SMEM((DEV, LEV), jnp.int32),
            pltpu.VMEM((2 * SLOTS, LEV), F32),
            pltpu.VMEM((2 * SLOTS, LEV), F32),
        ],
        compiler_params=params(),
        name="adjoint",
    )(got, slots, w_first, b_first, w_second, b_second, w_third, ivar)


def departure_kernel(
    reply, holder, innov, w_first, b_first, w_second, b_second, w_third, ivar, out
):
    held = holder[...]
    marks = (iota((OWN, DEV), 1) == held).astype(BF16)
    before = (iota((OWN, OWN), 1) < iota((OWN, OWN), 0)).astype(BF16)
    rank = jnp.sum(marks.astype(F32) * nn(before, marks), axis=1, keepdims=True).astype(jnp.int32)
    pick = (iota((OWN, DEV * ROWS), 1) == held * ROWS + rank).astype(BF16)
    own = nn(pick, reply[...]).astype(BF16)
    _, _, t_two = tangent(
        own[:, :LEV], own[:, LEV:], w_first[...], b_first[...], w_second[...], b_second[...]
    )
    out[...] = (nn(t_two, w_third[...]) - innov[...]) * ivar[...]


def departures_of(reply, holder, innov, w_first, b_first, w_second, b_second, w_third, ivar):
    return pl.pallas_call(
        departure_kernel,
        out_shape=jax.ShapeDtypeStruct((OWN, CH), F32),
        compiler_params=params(),
        name="departures",
    )(reply, holder, innov, w_first, b_first, w_second, b_second, w_third, ivar)


def gradient_kernel(
    acc, coef, x_low, x_high, y_low, y_high, low, high, control, out, field, grown, second
):
    step = pl.program_id(0)

    @pl.when(step == 0)
    def _():
        fill_rims(field, x_low, x_high, y_low, y_high, low, high)

        def fill(x, carry):
            field[x, 8 : 8 + BY, :] = acc[pl.ds(pl.multiple_of((x - 2) * BY, BY), BY), :]
            return carry

        lax.fori_loop(2, PX - 2, fill, 0)
        grown[...] = field[...]

        def scale(x, carry):
            field[x] = field[x] * coef[x]
            return carry

        lax.fori_loop(0, PX, scale, 0)

        def sweep_one(x, carry):
            value = grown[x, 8 : 8 + BY, :] + laplace(field, x, 8, BY)
            grown[x, 8 : 8 + BY, :] = value
            second[x, 8 : 8 + BY, :] = coef[x, 8 : 8 + BY, :] * value
            return carry

        lax.fori_loop(1, PX - 1, sweep_one, 0)
        for y in (7, 8 + BY):
            value = plane(grown, 2, y, BX) + plane_laplace(field, y)
            set_plane(second, 2, y, BX, plane(coef, 2, y, BX) * value)

    pair = eye_pair()
    flat_out = out.reshape(LEV * CHUNK, BY)
    flat_control = control.reshape(LEV * CHUNK, BY)
    for i in range(CHUNK):
        x = step * CHUNK + i + 2
        value = grown[x, 8 : 8 + BY, :] + laplace(second, x, 8, BY)
        high_part, low_part = split_two(value)
        turned = nt(pair, jnp.concatenate([high_part, low_part], axis=1))
        here = pl.ds(i, LEV, stride=CHUNK)
        flat_out[here, :] = turned + flat_control[here, :]


def gradient_of(acc, coef, rims, control):
    whole = pl.BlockSpec(memory_space=pltpu.VMEM)
    block = pl.BlockSpec((LEV, CHUNK, BY), lambda i: (0, i, 0))
    return pl.pallas_call(
        gradient_kernel,
        grid=(BX // CHUNK,),
        in_specs=[whole] * 8 + [block],
        out_specs=block,
        out_shape=jax.ShapeDtypeStruct((LEV, BX, BY), F32),
        scratch_shapes=[pltpu.VMEM((PX, PY, LEV), F32)] * 3,
        compiler_params=params(dimension_semantics=("arbitrary",)),
        name="gradient",
    )(acc, coef, *rims, control)


def exchange(array):
    return lax.all_to_all(array, ("tile", "obs"), split_axis=0, concat_axis=0, tiled=True)


def per_device(
    control,
    background,
    spread,
    obs_holder,
    obs_anchor,
    obs_frac,
    innovation,
    inverse_var,
    w_first,
    b_first,
    w_second,
    b_second,
    w_third,
):
    ivar = inverse_var.reshape(1, CH)
    b_one = b_first.reshape(1, HID)
    b_two = b_second.reshape(1, HID)
    asked = requests(
        obs_holder.reshape(1, OWN), obs_anchor.reshape(1, OWN), obs_frac, innovation, ivar, w_third
    )
    got = exchange(asked.reshape(DEV, ROWS, HID))
    ct, bgt, *send = to_columns(control, background, spread)
    inct, coef = increments(ct, spread, rims_around(*send))
    reply, slots = gathered(got, bgt.reshape(CELLS, LEV), inct.reshape(CELLS, LEV))
    reply = exchange(reply.reshape(DEV, ROWS, 2 * LEV))
    acc, *send = adjoint(got, slots, w_first, b_one, w_second, b_two, w_third, ivar)
    departures = departures_of(
        reply.reshape(DEV * ROWS, 2 * LEV), obs_holder, innovation,
        w_first, b_one, w_second, b_two, w_third, ivar,
    )
    gradient = gradient_of(acc, coef, rims_around(*send), control)
    return departures, gradient


def solution(mesh):
    return jax.shard_map(
        per_device,
        mesh=mesh,
        in_specs=(
            P(None, "tile", "obs"),
            P(None, "tile", "obs"),
            P("tile", "obs"),
            P(("tile", "obs"), None),
            P(("tile", "obs")),
            P(None, ("tile", "obs")),
            P(("tile", "obs"), None),
            P(),
            P(),
            P(),
            P(),
            P(),
            P(),
        ),
        out_specs=(P(("tile", "obs"), None), P(None, "tile", "obs")),
        check_vma=False,
    )
```

time: 207 us -> 143 us (0.69)
  Pallas kernels: 0 us -> 78.8 us
  local copies, waits for them, and re-layouts: 64.2 us -> 11.6 us
  other arithmetic: 52 us -> 0.03 us
  waiting for transfers between devices: 32.5 us -> 6.46 us
  starting transfers between devices: 50.1 us -> 44.1 us
  matrix products: 5.82 us -> 0 us
    pallas_call x0 -> x7, Pallas kernels: none -> 78.8 us  [the longest x1 21.3 us: increments(): pl.pallas_call(increment_kernel, out_shape=[jax.ShapeDtypeStruct((BX, BY,...]
    gather x4 -> x0, local copies, waits for them, and re-layouts: 26.4 us -> none  [the longest x1 11.5 us: per_device(): inc_cols[source].reshape(owners, capacity, 4, levels)]
    all_to_all x4 -> x2, waiting for transfers between devices: 26.1 us -> 0.01 us  [exchange(): lax.all_to_all(array, ('tile', 'obs'), split_axis=0, concat_axis=0, tiled...]
    scatter-add x1 -> x0, other arithmetic: 19.1 us -> none  [per_device(): gathered = jnp.zeros((rows_x * rows_y, levels), jnp.float32).at[source.re...]
    add x4 -> x0, other arithmetic: 9.77 us -> none  [the longest x1 5.22 us: advance(): crop(padded, 1)]
    concatenate x5 -> x3, other arithmetic: 9.07 us -> 0.03 us  [corner(): jnp.concatenate([y_low[low:low + 1], y_high[high:high + 1], y_low[2 * BX:...]
    scatter x2 -> x0, local copies, waits for them, and re-layouts: 8.77 us -> none  [the longest x1 7.21 us: per_device(): jnp.zeros((owners * capacity, 4, levels), jnp.float32).at[position]]
    all_to_all x4 -> x2, starting transfers between devices: 26.5 us -> 18.2 us  [exchange(): lax.all_to_all(array, ('tile', 'obs'), split_axis=0, concat_axis=0, tiled...]
  transfers between devices with their start and end apart: 16 -> 14, of which waited for: 5 -> 2; matrix products, arithmetic and copies ran while one was open for 30% -> 1% of each run, Pallas kernels for 0% -> 32%
where the time goes in v1:
time: 143 us; the launch traced here: 142 us
  Pallas kernels  78.8 us (55%)
  starting transfers between devices  44.1 us (31%)
  local copies, waits for them, and re-layouts  11.6 us (8%)
  waiting for transfers between devices  6.46 us (5%)
    ppermute x12, starting transfers between devices, shift(): lax.ppermute(array, axis, [(i, (i + by) % count) for i in range(count)])  26 us
    pallas_call x1, Pallas kernels, increments(): pl.pallas_call(increment_kernel, out_shape=[jax.ShapeDtypeStruct((BX, BY,...  21.3 us
    all_to_all x2, starting transfers between devices, exchange(): lax.all_to_all(array, ('tile', 'obs'), split_axis=0, concat_axis=0, tiled...  18.2 us
    pallas_call x1, Pallas kernels, adjoint(): pl.pallas_call(adjoint_kernel, out_shape=[jax.ShapeDtypeStruct((CELLS, LE...  16.3 us
    pallas_call x1, Pallas kernels, gradient_of(): pl.pallas_call(gradient_kernel, grid=(BX // CHUNK,), in_specs=[whole] * 8...  14.3 us
    unnamed x34, local copies, waits for them, and re-layouts  10.3 us
    pallas_call x1, Pallas kernels, to_columns(): pl.pallas_call(columns_kernel, grid=(BX // CHUNK,), in_specs=[pl.BlockSpe...  10.1 us
    pallas_call x1, Pallas kernels, gathered(): pl.pallas_call(gather_kernel, grid=(1,), in_specs=[pl.BlockSpec((DEV, ROW...  9.13 us
  transfers between devices with their start and end apart: 14, of which 2 were waited for; matrix products, arithmetic and copies ran while one was open for 1% of the time, Pallas kernels for 32%

profile of v1, /device:TPU:1, one launch (start us, length us, event | category | flops | bytes accessed | tf_op | source)
XLA Modules:
  0.0 141.9 jit_solution(9938441848728663898)
XLA Ops:
  0.6 2.2 %copy.16.w_third = bf16[512,616]{1,0:T(8,128)(2,1)} copy(bf16[512,616]{0,1:T(8,128)(2,1)} %param.25) | data formatting | bytes 1261568 | tf_op args[12]
  2.8 1.3 reshape.36.ivar
  4.1 2.2 %copy.15.innov = f32[256,616]{1,0:T(8,128)} copy(f32[256,616]{0,1:T(8,128)} %param.19) | data formatting | bytes 1261568 | tf_op args[6]
  6.2 3.4 %requests.1 = bf16[1024,512]{1,0:T(8,128)(2,1)} custom-call(s32[1,256]{1,0:T(1,128)} %bitcast.18, s32[1,256]{1,0:T(1,128)} %bitcast.19, f32[2,256]{1,0:T(2,128)} %frac.1, f32[256,616]{1,0:T(8,128)} %copy.15.innov, f32[1,616]{1,0:T(1,128)} %reshape.36.ivar, bf16[512,616]{1,0:T(8,128)(2,1)} %copy.16.w_third), custom_call_target="tpu_custom_call" | custom-call | tf_op jit(solution)/shard_map/requests/pallas_call | solution.py:82
  9.6 11.5 %all-to-all-start = ((bf16[128,8,512]{2,1,0:T(8,128)(2,1)}), bf16[128,8,512]{2,1,0:T(8,128)(2,1)S(1)}, u32[]{:S(2)}, u32[]{:S(2)}) async-start(bf16[128,8,512]{2,1,0:T(8,128)(2,1)} %bitcast.11), calls=%async_computation | async-start | bytes 2097152 | tf_op jit(solution)/shard_map/all_to_all | solution.py:558
  21.1 10.1 %columns.1 = (f32[64,128,128]{2,1,0:T(8,128)}, f32[64,128,128]{2,1,0:T(8,128)}, bf16[272,128]{1,0:T(8,128)(2,1)}, bf16[272,128]{1,0:T(8,128)(2,1)}, bf16[144,128]{1,0:T(8,128)(2,1)}, /*index=5*/bf16[144,128]{1,0:T(8,128)(2,1)}) custom-call(f32[128,64,128]{2,1,0:T(8,128)} %control.3, bf16[128,64,128]{2,1,0:T(8,128)(2,1)} %background.1, f32[64,128]{1,0:T(8,128)} %spread.3), custom_call_target="tpu_custom_call" | custom-call | tf_op jit(solution)/shard_map/columns/pallas_call | solution.py:139
  31.3 1.6 %collective-permute-start.2 = (bf16[144,128]{1,0:T(8,128)(2,1)}, bf16[144,128]{1,0:T(8,128)(2,1)S(1)}, u32[]{:S(2)}, u32[]{:S(2)}) collective-permute-start(bf16[144,128]{1,0:T(8,128)(2,1)} %get-tuple-element.21), channel_id=1, source_target_pairs={{0,1},{1,2},{2,3},{3,4},{4,5},{5,6},{6,7},{7,0},{8,9},{9,10},{10,1... | collective-permute-start | bytes 110600 | tf_op jit(solution)/shard_map/ppermute | solution.py:174
  32.9 0.0 collective-permute-start.3
  32.9 1.2 collective-permute-start
  34.1 4.2 %collective-permute-start.1 = (bf16[272,128]{1,0:T(8,128)(2,1)}, bf16[272,128]{1,0:T(8,128)(2,1)S(1)}, u32[]{:S(2)}, u32[]{:S(2)}) collective-permute-start(bf16[272,128]{1,0:T(8,128)(2,1)} %get-tuple-element.20), channel_id=1, source_target_pairs={{0,120},{8,0},{16,8},{24,16},{32,24},{40,32},{48,40},{56,48},{64,5... | collective-permute-start | bytes 208904 | tf_op jit(solution)/shard_map/ppermute | solution.py:174
  38.3 0.0 collective-permute-done.2.y_low
  38.3 0.0 copy-start.6
  38.3 0.0 collective-permute-done.3.y_high
  38.3 0.0 copy-start.7
  38.4 0.1 collective-permute-start.4
  38.5 4.8 %collective-permute-start.5 = (bf16[34,128]{1,0:T(8,128)(2,1)S(1)}, bf16[34,128]{1,0:T(8,128)(2,1)S(1)}, u32[]{:S(2)}, u32[]{:S(2)}) collective-permute-start(bf16[34,128]{1,0:T(8,128)(2,1)S(1)} %get-tuple-element.42), channel_id=1, source_target_pairs={{0,120},{8,0},{16,8},{24,16},{32,24},{40,32},{48,40},{56,48},{64,5... | collective-permute-start | bytes 26120 | tf_op jit(solution)/shard_map/ppermute | solution.py:174
  43.3 1.1 collective-permute-done.4.low
  44.3 0.0 copy-start.10
  44.3 0.0 collective-permute-done.5.high
  44.3 0.0 copy-start.11
  44.3 0.0 collective-permute-done.x_low
  44.3 0.0 copy-start.2
  44.3 0.0 collective-permute-done.1.x_high
  44.3 0.0 copy-start.3
  44.4 0.0 copy-done.6
  44.4 0.0 copy-done.7
  44.4 0.5 copy-done.10
  44.9 0.0 copy-done.11
  44.9 0.0 copy-done.2
  45.0 0.0 copy-done.3
  45.0 21.3 %increment.1 = (f32[64,128,128]{2,1,0:T(8,128)}, f32[68,144,128]{2,1,0:T(8,128)}) custom-call(f32[64,128,128]{2,1,0:T(8,128)} %get-tuple-element.18.ct, f32[64,128]{1,0:T(8,128)} %spread.3, bf16[272,128]{1,0:T(8,128)(2,1)} %copy-done.2, bf16[272,128]{1,0:T(8,128)(2,1)} %copy-done.3, bf16[144,128]{1,0:T(8,128)(2,1)} %copy-done.6, bf16[144,128]{1,0:T(8,128)(2,1)} %copy-done.7, ...), custom_call_target="tpu_custom_call" | custom-call | tf_op jit(solution)/shard_map/increment/pallas_call | solution.py:289
  66.3 0.0 all-to-all-done.got
  66.3 1.0 copy-done
  67.3 9.1 %gather.1 = (bf16[1024,256]{1,0:T(8,128)(2,1)}, bf16[768,256]{1,0:T(8,128)(2,1)}) custom-call(bf16[128,8,512]{2,1,0:T(8,128)(2,1)} %copy-done, f32[8192,128]{1,0:T(8,128)} %bitcast.9, f32[8192,128]{1,0:T(8,128)} %bitcast.10), custom_call_target="tpu_custom_call" | custom-call | tf_op jit(solution)/shard_map/gather/pallas_call | solution.py:353
  76.4 16.3 %adjoint.1 = (f32[8192,128]{1,0:T(8,128)}, bf16[256,128]{1,0:T(8,128)(2,1)}, bf16[256,128]{1,0:T(8,128)(2,1)}, bf16[128,128]{1,0:T(8,128)(2,1)}, bf16[128,128]{1,0:T(8,128)(2,1)}) custom-call(bf16[128,8,512]{2,1,0:T(8,128)(2,1)} %copy-done, bf16[768,256]{1,0:T(8,128)(2,1)} %get-tuple-element.25.slots, bf16[128,512]{1,0:T(8,128)(2,1)} %w_first.3, ...), custom_call_target="tpu_custom_call" | custom-call | tf_op jit(solution)/shard_map/adjoint/pallas_call | solution.py:450
  92.7 3.2 %collective-permute-start.8 = (bf16[128,128]{1,0:T(8,128)(2,1)}, bf16[128,128]{1,0:T(8,128)(2,1)S(1)}, u32[]{:S(2)}, u32[]{:S(2)}) collective-permute-start(bf16[128,128]{1,0:T(8,128)(2,1)} %get-tuple-element.30), channel_id=1, source_target_pairs={{0,1},{1,2},{2,3},{3,4},{4,5},{5,6},{6,7},{7,0},{8,9},{9,10},{10,1... | collective-permute-start | bytes 98312 | tf_op jit(solution)/shard_map/ppermute | solution.py:174
  95.8 0.0 collective-permute-start.9
  95.8 0.0 collective-permute-start.6
  95.8 4.9 %collective-permute-start.7 = (bf16[256,128]{1,0:T(8,128)(2,1)}, bf16[256,128]{1,0:T(8,128)(2,1)S(1)}, u32[]{:S(2)}, u32[]{:S(2)}) collective-permute-start(bf16[256,128]{1,0:T(8,128)(2,1)} %get-tuple-element.29), channel_id=1, source_target_pairs={{0,120},{8,0},{16,8},{24,16},{32,24},{40,32},{48,40},{56,48},{64,5... | collective-permute-start | bytes 196616 | tf_op jit(solution)/shard_map/ppermute | solution.py:174
  100.8 6.7 %all-to-all-start.1 = ((bf16[128,8,256]{2,1,0:T(8,128)(2,1)}), bf16[128,8,256]{2,1,0:T(8,128)(2,1)S(1)}, u32[]{:S(2)}, u32[]{:S(2)}) async-start(bf16[128,8,256]{2,1,0:T(8,128)(2,1)} %bitcast.13), calls=%async_computation.1 | async-start | bytes 1048576 | tf_op jit(solution)/shard_map/all_to_all | solution.py:558
  107.5 0.0 collective-permute-done.8.y_low
  107.5 0.0 copy-start.8
  107.5 0.0 collective-permute-done.9.y_high
  107.5 0.0 copy-start.9
  107.5 5.8 %collective-permute-start.11 = (bf16[2,128]{1,0:T(2,128)(2,1)S(1)}, bf16[2,128]{1,0:T(2,128)(2,1)S(1)}, u32[]{:S(2)}, u32[]{:S(2)}) collective-permute-start(bf16[2,128]{1,0:T(2,128)(2,1)S(1)} %pad_maximum_fusion.5), channel_id=1, source_target_pairs={{0,120},{8,0},{16,8},{24,16},{32,24},{40,32},{48,40},{56,48},{64,5... | collective-permute-start | bytes 1544 | tf_op jit(solution)/shard_map/ppermute | solution.py:174
  113.3 0.2 collective-permute-start.10
  113.6 0.0 copy-done.12
  113.6 0.8 copy.17.holder
  114.4 0.0 collective-permute-done.11.high
  114.4 5.4 %collective-permute-done.10.low = bf16[2,128]{1,0:T(2,128)(2,1)S(1)} collective-permute-done((bf16[2,128]{1,0:T(2,128)(2,1)S(1)}, bf16[2,128]{1,0:T(2,128)(2,1)S(1)}, u32[]{:S(2)}, u32[]{:S(2)}) %collective-permute-start.10) | collective-permute-done | bytes 544 | tf_op jit(solution)/shard_map/ppermute | solution.py:174
  119.8 0.0 collective-permute-done.6.x_low
  119.8 0.0 collective-permute-done.7.x_high
  119.8 0.0 copy-start.5
  119.8 0.0 copy-done.8
  119.8 0.0 copy-done.9
  119.8 0.0 copy-done.13
  119.8 0.4 copy-done.14
  120.3 0.1 copy-done.4
  120.4 0.0 copy-done.5
  120.4 14.3 %gradient.1 = f32[128,64,128]{2,1,0:T(8,128)} custom-call(f32[8192,128]{1,0:T(8,128)} %get-tuple-element.26.acc, f32[68,144,128]{2,1,0:T(8,128)} %get-tuple-element.27.coef, bf16[256,128]{1,0:T(8,128)(2,1)} %copy-done.4, bf16[256,128]{1,0:T(8,128)(2,1)} %copy-done.5, bf16[128,128]{1,0:T(8,128)(2,1)} %copy-done.8, bf16[128,128]{1,0:T(8,128)(2,1)} %copy-done.9, ...), custom_call_target="tpu_custom_call" | custom-call | tf_op jit(solution)/shard_map/gradient/pallas_call | solution.py:545
  134.7 0.0 all-to-all-done.1
  134.7 0.8 copy-done.1
  135.5 4.3 %departures.1 = f32[256,616]{1,0:T(8,128)} custom-call(bf16[1024,256]{1,0:T(8,128)(2,1)} %bitcast.12, s32[256,1]{1,0:T(8,128)} %copy.17.holder, f32[256,616]{1,0:T(8,128)} %copy.15.innov, bf16[128,512]{1,0:T(8,128)(2,1)} %w_first.3, f32[1,512]{1,0:T(1,128)} %bitcast.15, bf16[512,512]{1,0:T(8,128)(2,1)} %w_second.3, f32[1,512]{1,0:T(1,128)} %bitcast.17, ...), custom_call_target="tpu_custom_call" | custom-call | tf_op jit(solution)/shard_map/departures/pallas_call | solution.py:489
  139.8 2.1 %copy.21 = f32[256,616]{0,1:T(8,128)} copy(f32[256,616]{1,0:T(8,128)} %departures.1) | data formatting | bytes 1261568
  (15 shorter events, 0.1 us)
Async XLA Ops:
  9.6 56.7 %all-to-all-start = ((bf16[128,8,512]{2,1,0:T(8,128)(2,1)}), bf16[128,8,512]{2,1,0:T(8,128)(2,1)S(1)}, u32[]{:S(2)}, u32[]{:S(2)}) async-start(bf16[128,8,512]{2,1,0:T(8,128)(2,1)} %bitcast.11), calls=%async_computation | async-start | bytes 2097152 | tf_op jit(solution)/shard_map/all_to_all | solution.py:558
  31.3 7.0 %collective-permute-start.2 = (bf16[144,128]{1,0:T(8,128)(2,1)}, bf16[144,128]{1,0:T(8,128)(2,1)S(1)}, u32[]{:S(2)}, u32[]{:S(2)}) collective-permute-start(bf16[144,128]{1,0:T(8,128)(2,1)} %get-tuple-element.21), channel_id=1, source_target_pairs={{0,1},{1,2},{2,3},{3,4},{4,5},{5,6},{6,7},{7,0},{8,9},{9,10},{10,1... | collective-permute-start | bytes 110600 | tf_op jit(solution)/shard_map/ppermute | solution.py:174
  32.9 5.4 %collective-permute-start.3 = (bf16[144,128]{1,0:T(8,128)(2,1)}, bf16[144,128]{1,0:T(8,128)(2,1)S(1)}, u32[]{:S(2)}, u32[]{:S(2)}) collective-permute-start(bf16[144,128]{1,0:T(8,128)(2,1)} %get-tuple-element.22), channel_id=1, source_target_pairs={{0,7},{1,0},{2,1},{3,2},{4,3},{5,4},{6,5},{7,6},{8,15},{9,8},{10,9... | collective-permute-start | bytes 110600 | tf_op jit(solution)/shard_map/ppermute | solution.py:174
  32.9 11.4 %collective-permute-start = (bf16[272,128]{1,0:T(8,128)(2,1)}, bf16[272,128]{1,0:T(8,128)(2,1)S(1)}, u32[]{:S(2)}, u32[]{:S(2)}) collective-permute-start(bf16[272,128]{1,0:T(8,128)(2,1)} %get-tuple-element.19), channel_id=1, source_target_pairs={{0,8},{8,16},{16,24},{24,32},{32,40},{40,48},{48,56},{56,64},{64,7... | collective-permute-start | bytes 208904 | tf_op jit(solution)/shard_map/ppermute | solution.py:174
  34.1 10.2 %collective-permute-start.1 = (bf16[272,128]{1,0:T(8,128)(2,1)}, bf16[272,128]{1,0:T(8,128)(2,1)S(1)}, u32[]{:S(2)}, u32[]{:S(2)}) collective-permute-start(bf16[272,128]{1,0:T(8,128)(2,1)} %get-tuple-element.20), channel_id=1, source_target_pairs={{0,120},{8,0},{16,8},{24,16},{32,24},{40,32},{48,40},{56,48},{64,5... | collective-permute-start | bytes 208904 | tf_op jit(solution)/shard_map/ppermute | solution.py:174
  38.3 6.0 %copy-start.6 = (bf16[144,128]{1,0:T(8,128)(2,1)}, bf16[144,128]{1,0:T(8,128)(2,1)S(1)}, u32[]{:S(2)}) copy-start(bf16[144,128]{1,0:T(8,128)(2,1)S(1)} %collective-permute-done.2.y_low) | copy-start | bytes 110596
  38.3 6.0 %copy-start.7 = (bf16[144,128]{1,0:T(8,128)(2,1)}, bf16[144,128]{1,0:T(8,128)(2,1)S(1)}, u32[]{:S(2)}) copy-start(bf16[144,128]{1,0:T(8,128)(2,1)S(1)} %collective-permute-done.3.y_high) | copy-start | bytes 110596
  38.4 5.9 %collective-permute-start.4 = (bf16[34,128]{1,0:T(8,128)(2,1)S(1)}, bf16[34,128]{1,0:T(8,128)(2,1)S(1)}, u32[]{:S(2)}, u32[]{:S(2)}) collective-permute-start(bf16[34,128]{1,0:T(8,128)(2,1)S(1)} %get-tuple-element.43), channel_id=1, source_target_pairs={{0,8},{8,16},{16,24},{24,32},{32,40},{40,48},{48,56},{56,64},{64,7... | collective-permute-start | bytes 26120 | tf_op jit(solution)/shard_map/ppermute | solution.py:174
  38.5 5.8 %collective-permute-start.5 = (bf16[34,128]{1,0:T(8,128)(2,1)S(1)}, bf16[34,128]{1,0:T(8,128)(2,1)S(1)}, u32[]{:S(2)}, u32[]{:S(2)}) collective-permute-start(bf16[34,128]{1,0:T(8,128)(2,1)S(1)} %get-tuple-element.42), channel_id=1, source_target_pairs={{0,120},{8,0},{16,8},{24,16},{32,24},{40,32},{48,40},{56,48},{64,5... | collective-permute-start | bytes 26120 | tf_op jit(solution)/shard_map/ppermute | solution.py:174
  44.3 0.6 copy-start.10
  44.3 0.6 copy-start.11
  44.3 0.6 copy-start.2
  44.3 0.6 copy-start.3
  66.3 1.0 copy-start
  67.3 46.3 %copy-start.12 = (s32[256,1]{0,1:T(1,128)S(1)}, s32[256,1]{0,1:T(1,128)}, u32[]{:S(2)}) copy-start(s32[256,1]{0,1:T(1,128)} %param.16) | copy-start | bytes 3076
  92.7 14.8 %collective-permute-start.8 = (bf16[128,128]{1,0:T(8,128)(2,1)}, bf16[128,128]{1,0:T(8,128)(2,1)S(1)}, u32[]{:S(2)}, u32[]{:S(2)}) collective-permute-start(bf16[128,128]{1,0:T(8,128)(2,1)} %get-tuple-element.30), channel_id=1, source_target_pairs={{0,1},{1,2},{2,3},{3,4},{4,5},{5,6},{6,7},{7,0},{8,9},{9,10},{10,1... | collective-permute-start | bytes 98312 | tf_op jit(solution)/shard_map/ppermute | solution.py:174
  95.8 11.7 %collective-permute-start.9 = (bf16[128,128]{1,0:T(8,128)(2,1)}, bf16[128,128]{1,0:T(8,128)(2,1)S(1)}, u32[]{:S(2)}, u32[]{:S(2)}) collective-permute-start(bf16[128,128]{1,0:T(8,128)(2,1)} %get-tuple-element.31), channel_id=1, source_target_pairs={{0,7},{1,0},{2,1},{3,2},{4,3},{5,4},{6,5},{7,6},{8,15},{9,8},{10,9... | collective-permute-start | bytes 98312 | tf_op jit(solution)/shard_map/ppermute | solution.py:174
  95.8 23.9 %collective-permute-start.6 = (bf16[256,128]{1,0:T(8,128)(2,1)}, bf16[256,128]{1,0:T(8,128)(2,1)S(1)}, u32[]{:S(2)}, u32[]{:S(2)}) collective-permute-start(bf16[256,128]{1,0:T(8,128)(2,1)} %get-tuple-element.28), channel_id=1, source_target_pairs={{0,8},{8,16},{16,24},{24,32},{32,40},{40,48},{48,56},{56,64},{64,7... | collective-permute-start | bytes 196616 | tf_op jit(solution)/shard_map/ppermute | solution.py:174
  95.8 23.9 %collective-permute-start.7 = (bf16[256,128]{1,0:T(8,128)(2,1)}, bf16[256,128]{1,0:T(8,128)(2,1)S(1)}, u32[]{:S(2)}, u32[]{:S(2)}) collective-permute-start(bf16[256,128]{1,0:T(8,128)(2,1)} %get-tuple-element.29), channel_id=1, source_target_pairs={{0,120},{8,0},{16,8},{24,16},{32,24},{40,32},{48,40},{56,48},{64,5... | collective-permute-start | bytes 196616 | tf_op jit(solution)/shard_map/ppermute | solution.py:174
  100.8 33.9 %all-to-all-start.1 = ((bf16[128,8,256]{2,1,0:T(8,128)(2,1)}), bf16[128,8,256]{2,1,0:T(8,128)(2,1)S(1)}, u32[]{:S(2)}, u32[]{:S(2)}) async-start(bf16[128,8,256]{2,1,0:T(8,128)(2,1)} %bitcast.13), calls=%async_computation.1 | async-start | bytes 1048576 | tf_op jit(solution)/shard_map/all_to_all | solution.py:558
  107.5 12.3 %copy-start.8 = (bf16[128,128]{1,0:T(8,128)(2,1)}, bf16[128,128]{1,0:T(8,128)(2,1)S(1)}, u32[]{:S(2)}) copy-start(bf16[128,128]{1,0:T(8,128)(2,1)S(1)} %collective-permute-done.8.y_low) | copy-start | bytes 98308
  107.5 12.3 %copy-start.9 = (bf16[128,128]{1,0:T(8,128)(2,1)}, bf16[128,128]{1,0:T(8,128)(2,1)S(1)}, u32[]{:S(2)}) copy-start(bf16[128,128]{1,0:T(8,128)(2,1)S(1)} %collective-permute-done.9.y_high) | copy-start | bytes 98308
  107.5 6.8 %collective-permute-start.11 = (bf16[2,128]{1,0:T(2,128)(2,1)S(1)}, bf16[2,128]{1,0:T(2,128)(2,1)S(1)}, u32[]{:S(2)}, u32[]{:S(2)}) collective-permute-start(bf16[2,128]{1,0:T(2,128)(2,1)S(1)} %pad_maximum_fusion.5), channel_id=1, source_target_pairs={{0,120},{8,0},{16,8},{24,16},{32,24},{40,32},{48,40},{56,48},{64,5... | collective-permute-start | bytes 1544 | tf_op jit(solution)/shard_map/ppermute | solution.py:174
  113.3 6.4 %collective-permute-start.10 = (bf16[2,128]{1,0:T(2,128)(2,1)S(1)}, bf16[2,128]{1,0:T(2,128)(2,1)S(1)}, u32[]{:S(2)}, u32[]{:S(2)}) collective-permute-start(bf16[2,128]{1,0:T(2,128)(2,1)S(1)} %pad_maximum_fusion.4), channel_id=1, source_target_pairs={{0,8},{8,16},{16,24},{24,32},{32,40},{40,48},{48,56},{56,64},{64,7... | collective-permute-start | bytes 1544 | tf_op jit(solution)/shard_map/ppermute | solution.py:174
  114.4 5.4 %copy-start.13 = (bf16[2,128]{1,0:T(2,128)(2,1)}, bf16[2,128]{1,0:T(2,128)(2,1)S(1)}, u32[]{:S(2)}) copy-start(bf16[2,128]{1,0:T(2,128)(2,1)S(1)} %collective-permute-done.11.high) | copy-start | bytes 1540
  119.8 0.5 copy-start.14
  119.8 0.6 copy-start.4
  119.8 0.6 copy-start.5
  134.7 0.8 copy-start.1

commit v2 on v1

--- a/solution.py
+++ b/solution.py
@@ -21,11 +21,22 @@
 PX = BX + 4
 PY = BY + 16
 CHUNK = 8
-VMEM_LIMIT = 56 * 1024 * 1024
-
-
-def params(**extra):
-    return pltpu.CompilerParams(vmem_limit_bytes=VMEM_LIMIT, **extra)
+
+
+def params(mib, **extra):
+    return pltpu.CompilerParams(vmem_limit_bytes=mib * 1024 * 1024, **extra)
+
+
+def cost(us):
+    return pl.CostEstimate(flops=int(us * 1.0e9), bytes_accessed=0, transcendentals=0)
+
+
+def tn(a, b):
+    return lax.dot_general(a, b, (((0,), (0,)), ((), ())), preferred_element_type=F32)
+
+
+def down(row):
+    return jnp.transpose(jnp.broadcast_to(row, (LEV, row.shape[1])))
 
 
 def nn(a, b):
@@ -51,11 +62,15 @@
     return ((col == row) | (col == row + LEV)).astype(BF16)
 
 
+def ranks(held):
+    marks = (iota((DEV, OWN), 0) == held).astype(BF16)
+    before = (iota((OWN, OWN), 0) < iota((OWN, OWN), 1)).astype(BF16)
+    return jnp.sum(marks.astype(F32) * nn(marks, before), axis=0, keepdims=True).astype(jnp.int32)
+
+
 def request_kernel(holder, anchor, frac, innov, ivar, w_third, out):
     held = holder[...]
-    marks = (iota((DEV, OWN), 0) == held).astype(BF16)
-    before = (iota((OWN, OWN), 0) < iota((OWN, OWN), 1)).astype(BF16)
-    rank = jnp.sum(marks.astype(F32) * nn(marks, before), axis=0, keepdims=True).astype(jnp.int32)
+    rank = ranks(held)
     at = anchor[...].astype(F32)
     x = jnp.floor((at + 0.5) * (1.0 / (BY - 1)))
     y = at - (BY - 1) * x
@@ -69,8 +84,9 @@
     fields = jnp.concatenate(fields, axis=0)
     fields = jnp.concatenate([fields] * (LEV // 8), axis=0)
     fields = jnp.where((iota((LEV, OWN), 0) >> 3) == rank, fields, 0.0).astype(BF16)
-    scaled = (innov[...] * ivar[...]).astype(BF16)
-    pulled = nt(scaled, w_third[...]).astype(BF16)
+    each = down(ivar[...].reshape(1, CH))
+    scaled = (innov[...] * jnp.concatenate([each, each], axis=1)).astype(BF16)
+    pulled = tn(scaled, w_third[...]).astype(BF16)
     row = iota((DEV * ROWS, OWN), 0)
     to_slot = (row == held * ROWS + rank).astype(BF16)
     to_fields = (row == held * ROWS + CAP).astype(BF16)
@@ -82,7 +98,8 @@
     return pl.pallas_call(
         request_kernel,
         out_shape=jax.ShapeDtypeStruct((DEV * ROWS, HID), BF16),
-        compiler_params=params(),
+        compiler_params=params(12),
+        cost_estimate=cost(4),
         name="requests",
     )(holder, anchor, frac, innov, ivar, w_third)
 
@@ -164,7 +181,8 @@
             pltpu.VMEM((LEV * CHUNK, BY), F32),
             pltpu.VMEM((4, BX, LEV), F32),
         ],
-        compiler_params=params(dimension_semantics=("arbitrary",)),
+        compiler_params=params(10, dimension_semantics=("arbitrary",)),
+        cost_estimate=cost(6),
         name="columns",
     )(control, background, spread)
 
@@ -244,12 +262,8 @@
     )
     turned = jnp.transpose(square)
 
-    def broadcast(x, carry):
-        moved = pltpu.roll(turned, (LEV - x) % LEV, 1)
-        coef[x, 8 : 8 + BY, :] = lanes(moved[:, 0:1])
-        return carry
-
-    lax.fori_loop(0, PX, broadcast, 0)
+    for x in range(PX):
+        coef[x, 8 : 8 + BY, :] = lanes(turned[:, x : x + 1])
     sides = jnp.concatenate(
         [joined(y_low, 2 * BX), joined(y_high, 2 * BX), jnp.zeros((BY - 4, BY), F32)], axis=0
     )
@@ -293,7 +307,8 @@
             jax.ShapeDtypeStruct((PX, PY, LEV), F32),
         ],
         scratch_shapes=[pltpu.VMEM((PX, PY, LEV), F32), pltpu.VMEM((PX, PY, LEV), F32)],
-        compiler_params=params(),
+        compiler_params=params(27),
+        cost_estimate=cost(6),
         name="increment",
     )(ct, spread, *rims)
 
@@ -369,7 +384,8 @@
             rows,
             pltpu.VMEM((2, DEV * ROWS, LEV), F32),
         ],
-        compiler_params=params(),
+        compiler_params=params(18),
+        cost_estimate=cost(5),
         name="gather",
     )(got, bgt, inct)
 
@@ -408,8 +424,8 @@
             slots[here, :LEV], slots[here, LEV:],
             w_first[...], b_first[...], w_second[...], b_second[...],
         )
-        change = nn(t_two, w_third[...]) * ivar[...]
-        s_two = (d_two * (nt(change.astype(BF16), w_third[...]) - pulled[here, :])).astype(BF16)
+        change = nt(t_two, w_third[...]) * ivar[...].reshape(1, CH)
+        s_two = (d_two * (nn(change.astype(BF16), w_third[...]) - pulled[here, :])).astype(BF16)
         s_one = (d_one * nt(s_two, w_second[...])).astype(BF16)
         profile[here, :] = nt(s_one, w_first[...])
         return carry
@@ -465,7 +481,8 @@
             pltpu.VMEM((2 * SLOTS, LEV), F32),
             pltpu.VMEM((2 * SLOTS, LEV), F32),
         ],
-        compiler_params=params(),
+        compiler_params=params(24),
+        cost_estimate=cost(10),
         name="adjoint",
     )(got, slots, w_first, b_first, w_second, b_second, w_third, ivar)
 
@@ -474,22 +491,21 @@
     reply, holder, innov, w_first, b_first, w_second, b_second, w_third, ivar, out
 ):
     held = holder[...]
-    marks = (iota((OWN, DEV), 1) == held).astype(BF16)
-    before = (iota((OWN, OWN), 1) < iota((OWN, OWN), 0)).astype(BF16)
-    rank = jnp.sum(marks.astype(F32) * nn(before, marks), axis=1, keepdims=True).astype(jnp.int32)
-    pick = (iota((OWN, DEV * ROWS), 1) == held * ROWS + rank).astype(BF16)
+    pick = (iota((OWN, DEV * ROWS), 1) == down(held * ROWS + ranks(held)).astype(jnp.int32)[:, 0:1]).astype(BF16)
     own = nn(pick, reply[...]).astype(BF16)
     _, _, t_two = tangent(
         own[:, :LEV], own[:, LEV:], w_first[...], b_first[...], w_second[...], b_second[...]
     )
-    out[...] = (nn(t_two, w_third[...]) - innov[...]) * ivar[...]
+    each = down(ivar[...].reshape(1, CH))
+    out[...] = (nt(w_third[...], t_two) - innov[...]) * jnp.concatenate([each, each], axis=1)
 
 
 def departures_of(reply, holder, innov, w_first, b_first, w_second, b_second, w_third, ivar):
     return pl.pallas_call(
         departure_kernel,
-        out_shape=jax.ShapeDtypeStruct((OWN, CH), F32),
-        compiler_params=params(),
+        out_shape=jax.ShapeDtypeStruct((CH, OWN), F32),
+        compiler_params=params(12),
+        cost_estimate=cost(4),
         name="departures",
     )(reply, holder, innov, w_first, b_first, w_second, b_second, w_third, ivar)
 
@@ -549,7 +565,8 @@
         out_specs=block,
         out_shape=jax.ShapeDtypeStruct((LEV, BX, BY), F32),
         scratch_shapes=[pltpu.VMEM((PX, PY, LEV), F32)] * 3,
-        compiler_params=params(dimension_semantics=("arbitrary",)),
+        compiler_params=params(30, dimension_semantics=("arbitrary",)),
+        cost_estimate=cost(8),
         name="gradient",
     )(acc, coef, *rims, control)
 
@@ -573,22 +590,22 @@
     b_second,
     w_third,
 ):
-    ivar = inverse_var.reshape(1, CH)
     b_one = b_first.reshape(1, HID)
     b_two = b_second.reshape(1, HID)
-    asked = requests(
-        obs_holder.reshape(1, OWN), obs_anchor.reshape(1, OWN), obs_frac, innovation, ivar, w_third
-    )
+    holder = obs_holder.reshape(1, OWN)
+    innov = innovation.T
+    w_last = w_third.T
+    asked = requests(holder, obs_anchor.reshape(1, OWN), obs_frac, innov, inverse_var, w_last)
     got = exchange(asked.reshape(DEV, ROWS, HID))
     ct, bgt, *send = to_columns(control, background, spread)
     inct, coef = increments(ct, spread, rims_around(*send))
     reply, slots = gathered(got, bgt.reshape(CELLS, LEV), inct.reshape(CELLS, LEV))
     reply = exchange(reply.reshape(DEV, ROWS, 2 * LEV))
-    acc, *send = adjoint(got, slots, w_first, b_one, w_second, b_two, w_third, ivar)
+    acc, *send = adjoint(got, slots, w_first, b_one, w_second, b_two, w_last, inverse_var)
     departures = departures_of(
-        reply.reshape(DEV * ROWS, 2 * LEV), obs_holder, innovation,
-        w_first, b_one, w_second, b_two, w_third, ivar,
-    )
+        reply.reshape(DEV * ROWS, 2 * LEV), holder, innov,
+        w_first, b_one, w_second, b_two, w_last, inverse_var,
+    ).T
     gradient = gradient_of(acc, coef, rims_around(*send), control)
     return departures, gradient
 

time: 143 us -> 118 us (0.83)
  Pallas kernels: 78.8 us -> 42.7 us
  local copies, waits for them, and re-layouts: 11.6 us -> 24.3 us
    pallas_call x1, Pallas kernels: 21.3 us -> 5.92 us  [increments(): pl.pallas_call(increment_kernel, out_shape=[jax.ShapeDtypeStruct((BX, BY,...]
    unnamed x34 -> x50, local copies, waits for them, and re-layouts: 10.3 us -> 24.2 us
    pallas_call x1, Pallas kernels: 14.3 us -> 9.09 us  [gradient_of(): pl.pallas_call(gradient_kernel, grid=(BX // CHUNK,), in_specs=[whole] * 8...]
    pallas_call x1, Pallas kernels: 10.1 us -> 5.26 us  [to_columns(): pl.pallas_call(columns_kernel, grid=(BX // CHUNK,), in_specs=[pl.BlockSpe...]
    pallas_call x1, Pallas kernels: 16.3 us -> 12.2 us  [adjoint(): pl.pallas_call(adjoint_kernel, out_shape=[jax.ShapeDtypeStruct((CELLS, LE...]
    pallas_call x1, Pallas kernels: 9.13 us -> 5.49 us  [gathered(): pl.pallas_call(gather_kernel, grid=(1,), in_specs=[pl.BlockSpec((DEV, ROW...]
    all_to_all x2, starting transfers between devices: 18.2 us -> 15.5 us  [exchange(): lax.all_to_all(array, ('tile', 'obs'), split_axis=0, concat_axis=0, tiled...]
    ppermute x12, starting transfers between devices: 26 us -> 28.5 us  [shift(): lax.ppermute(array, axis, [(i, (i + by) % count) for i in range(count)])]
  transfers between devices with their start and end apart: 14 -> 14, of which waited for: 2 -> 1; matrix products, arithmetic and copies ran while one was open for 1% -> 0% of each run, Pallas kernels for 32% -> 15%
where the time goes in v2:
time: 118 us; the launch traced here: 117 us
  starting transfers between devices  44 us (37%)
  Pallas kernels  42.7 us (36%)
  local copies, waits for them, and re-layouts  24.3 us (21%)
  waiting for transfers between devices  5.47 us (5%)
    ppermute x12, starting transfers between devices, shift(): lax.ppermute(array, axis, [(i, (i + by) % count) for i in range(count)])  28.5 us
    unnamed x50, local copies, waits for them, and re-layouts  24.2 us
    all_to_all x2, starting transfers between devices, exchange(): lax.all_to_all(array, ('tile', 'obs'), split_axis=0, concat_axis=0, tiled...  15.5 us
    pallas_call x1, Pallas kernels, adjoint(): pl.pallas_call(adjoint_kernel, out_shape=[jax.ShapeDtypeStruct((CELLS, LE...  12.2 us
    pallas_call x1, Pallas kernels, gradient_of(): pl.pallas_call(gradient_kernel, grid=(BX // CHUNK,), in_specs=[whole] * 8...  9.09 us
    pallas_call x1, Pallas kernels, increments(): pl.pallas_call(increment_kernel, out_shape=[jax.ShapeDtypeStruct((BX, BY,...  5.92 us
    pallas_call x1, Pallas kernels, gathered(): pl.pallas_call(gather_kernel, grid=(1,), in_specs=[pl.BlockSpec((DEV, ROW...  5.49 us
    ppermute x12, waiting for transfers between devices, shift(): lax.ppermute(array, axis, [(i, (i + by) % count) for i in range(count)])  5.47 us
  transfers between devices with their start and end apart: 14, of which 1 were waited for; matrix products, arithmetic and copies ran while one was open for 0% of the time, Pallas kernels for 15%

profile of v2, /device:TPU:1, one launch (start us, length us, event | category | flops | bytes accessed | tf_op | source)
XLA Modules:
  0.0 117.4 jit_solution(6553325463871697435)
XLA Ops:
  0.6 0.0 copy-start
  0.6 2.2 %copy-done = f32[128,64,128]{2,1,0:T(8,128)S(1)} copy-done((f32[128,64,128]{2,1,0:T(8,128)S(1)}, f32[128,64,128]{2,1,0:T(8,128)}, u32[]{:S(2)}) %copy-start) | copy-done | bytes 4194328
  2.8 1.6 %copy-done.2 = bf16[128,64,128]{2,1,0:T(8,128)(2,1)S(1)} copy-done((bf16[128,64,128]{2,1,0:T(8,128)(2,1)S(1)}, bf16[128,64,128]{2,1,0:T(8,128)(2,1)}, u32[]{:S(2)}) %copy-start.2) | copy-done | bytes 2097176
  4.4 0.8 copy-done.7
  5.2 0.0 copy-start.13
  5.2 0.0 copy-start.14
  5.2 5.3 %columns.1 = (f32[64,128,128]{2,1,0:T(8,128)S(1)}, f32[64,128,128]{2,1,0:T(8,128)S(1)}, bf16[272,128]{1,0:T(8,128)(2,1)S(1)}, bf16[272,128]{1,0:T(8,128)(2,1)S(1...) custom-call(f32[128,64,128]{2,1,0:T(8,128)S(1)} %copy-done, bf16[128,64,128]{2,1,0:T(8,128)(2,1)S(1)} %copy-done.2, ...), custom_call_target="tpu_custom_call" | custom-call | flops 6000000000 | tf_op jit(solution)/shard_map/columns/pallas_call | solution.py:156
  10.5 0.0 copy-start.15
  10.5 0.0 copy-start.23
  10.5 2.6 %collective-permute-start.2 = (bf16[144,128]{1,0:T(8,128)(2,1)S(1)}, bf16[144,128]{1,0:T(8,128)(2,1)S(1)}, u32[]{:S(2)}, u32[]{:S(2)}) collective-permute-start(bf16[144,128]{1,0:T(8,128)(2,1)S(1)} %get-tuple-element.21), channel_id=1, source_target_pairs={{0,1},{1,2},{2,3},{3,4},{4,5},{5,6},{6,7},{7,0},{8,9},{9,10},{10,1... | collective-permute-start | bytes 110600 | tf_op jit(solution)/shard_map/ppermute | solution.py:192
  13.1 0.0 collective-permute-start.3
  13.1 1.3 %collective-permute-start = (bf16[272,128]{1,0:T(8,128)(2,1)S(1)}, bf16[272,128]{1,0:T(8,128)(2,1)S(1)}, u32[]{:S(2)}, u32[]{:S(2)}) collective-permute-start(bf16[272,128]{1,0:T(8,128)(2,1)S(1)} %get-tuple-element.19), channel_id=1, source_target_pairs={{0,8},{8,16},{16,24},{24,32},{32,40},{40,48},{48,56},{56,64},{64,7... | collective-permute-start | bytes 208904 | tf_op jit(solution)/shard_map/ppermute | solution.py:192
  14.4 4.9 %collective-permute-start.1 = (bf16[272,128]{1,0:T(8,128)(2,1)S(1)}, bf16[272,128]{1,0:T(8,128)(2,1)S(1)}, u32[]{:S(2)}, u32[]{:S(2)}) collective-permute-start(bf16[272,128]{1,0:T(8,128)(2,1)S(1)} %get-tuple-element.20), channel_id=1, source_target_pairs={{0,120},{8,0},{16,8},{24,16},{32,24},{40,32},{48,40},{56,48},{64,5... | collective-permute-start | bytes 208904 | tf_op jit(solution)/shard_map/ppermute | solution.py:192
  19.3 0.0 copy-done.3
  19.3 0.0 copy-done.4
  19.3 0.0 copy-done.9
  19.3 0.0 copy-done.10
  19.3 0.0 copy-done.13
  19.3 0.0 copy-done.14
  19.4 0.0 copy-start.8
  19.4 2.3 %requests.1 = bf16[1024,512]{1,0:T(8,128)(2,1)} custom-call(s32[1,256]{1,0:T(1,128)S(1)} %bitcast.23, s32[1,256]{1,0:T(1,128)S(1)} %bitcast.22, f32[2,256]{1,0:T(2,128)S(1)} %copy-done.10, f32[616,256]{1,0:T(8,128)S(1)} %bitcast.13, f32[616]{0:T(1024)S(1)} %copy-done.9, bf16[616,512]{1,0:T(8,128)(2,1)S(1)} %bitcast.15), custom_call_target="tpu_custom_call" | custom-call | flops 4000000000 | tf_op jit(solution)/shard_map/requests/pallas_call | solution.py:98
  21.6 0.0 copy-done.15
  21.6 0.0 copy-done.23
  21.6 6.4 %all-to-all-start = ((bf16[128,8,512]{2,1,0:T(8,128)(2,1)}), bf16[128,8,512]{2,1,0:T(8,128)(2,1)S(1)}, u32[]{:S(2)}, u32[]{:S(2)}) async-start(bf16[128,8,512]{2,1,0:T(8,128)(2,1)} %bitcast.4), calls=%async_computation | async-start | bytes 2097152 | tf_op jit(solution)/shard_map/all_to_all | solution.py:575
  28.1 0.0 collective-permute-done.2.y_low
  28.1 0.0 collective-permute-done.3.y_high
  28.2 1.4 %collective-permute-start.4 = (bf16[34,128]{1,0:T(8,128)(2,1)S(1)}, bf16[34,128]{1,0:T(8,128)(2,1)S(1)}, u32[]{:S(2)}, u32[]{:S(2)}) collective-permute-start(bf16[34,128]{1,0:T(8,128)(2,1)S(1)} %get-tuple-element.41), channel_id=1, source_target_pairs={{0,8},{8,16},{16,24},{24,32},{32,40},{40,48},{48,56},{56,64},{64,7... | collective-permute-start | bytes 26120 | tf_op jit(solution)/shard_map/ppermute | solution.py:192
  29.6 4.3 %collective-permute-start.5 = (bf16[34,128]{1,0:T(8,128)(2,1)S(1)}, bf16[34,128]{1,0:T(8,128)(2,1)S(1)}, u32[]{:S(2)}, u32[]{:S(2)}) collective-permute-start(bf16[34,128]{1,0:T(8,128)(2,1)S(1)} %get-tuple-element.40), channel_id=1, source_target_pairs={{0,120},{8,0},{16,8},{24,16},{32,24},{40,32},{48,40},{56,48},{64,5... | collective-permute-start | bytes 26120 | tf_op jit(solution)/shard_map/ppermute | solution.py:192
  33.9 5.4 %collective-permute-done.4.low = bf16[34,128]{1,0:T(8,128)(2,1)S(1)} collective-permute-done((bf16[34,128]{1,0:T(8,128)(2,1)S(1)}, bf16[34,128]{1,0:T(8,128)(2,1)S(1)}, u32[]{:S(2)}, u32[]{:S(2)}) %collective-permute-start.4) | collective-permute-done | bytes 8736 | tf_op jit(solution)/shard_map/ppermute | solution.py:192
  39.3 0.0 collective-permute-done.5.high
  39.3 0.0 collective-permute-done.x_low
  39.3 0.0 collective-permute-done.1.x_high
  39.3 2.2 %copy-done.24 = f32[64,128,128]{2,1,0:T(8,128)S(1)} copy-done((f32[64,128,128]{2,1,0:T(8,128)S(1)}, f32[64,128,128]{2,1,0:T(8,128)}, u32[]{:S(2)}) %copy-start.24) | copy-done | bytes 4194328
  41.5 5.9 %increment.1 = (f32[64,128,128]{2,1,0:T(8,128)S(1)}, f32[68,144,128]{2,1,0:T(8,128)S(1)}) custom-call(f32[64,128,128]{2,1,0:T(8,128)S(1)} %copy-done.24, f32[64,128]{1,0:T(8,128)S(1)} %copy-done.8, bf16[272,128]{1,0:T(8,128)(2,1)S(1)} %collective-permute-done.x_low, bf16[272,128]{1,0:T(8,128)(2,1)S(1)} %collective-permute-done.1.x_high, ...), custom_call_target="tpu_custom_call" | custom-call | flops 6000000000 | tf_op jit(solution)/shard_map/increment/pallas_call | solution.py:303
  47.5 2.0 %copy-done.17 = f32[64,128,128]{2,1,0:T(8,128)} copy-done((f32[64,128,128]{2,1,0:T(8,128)}, f32[64,128,128]{2,1,0:T(8,128)S(1)}, u32[]{:S(2)}) %copy-start.17) | copy-done | bytes 4194328
  49.5 2.3 %copy-done.19 = f32[68,144,128]{2,1,0:T(8,128)} copy-done((f32[68,144,128]{2,1,0:T(8,128)}, f32[68,144,128]{2,1,0:T(8,128)S(1)}, u32[]{:S(2)}) %copy-start.19) | copy-done | bytes 5013528
  51.8 0.0 all-to-all-done.got
  51.8 2.2 %copy-done.16 = f32[64,128,128]{2,1,0:T(8,128)S(1)} copy-done((f32[64,128,128]{2,1,0:T(8,128)S(1)}, f32[64,128,128]{2,1,0:T(8,128)}, u32[]{:S(2)}) %copy-start.16) | copy-done | bytes 4194328
  54.0 2.2 %copy-done.18 = f32[64,128,128]{2,1,0:T(8,128)S(1)} copy-done((f32[64,128,128]{2,1,0:T(8,128)S(1)}, f32[64,128,128]{2,1,0:T(8,128)}, u32[]{:S(2)}) %copy-start.18) | copy-done | bytes 4194328
  56.1 5.5 %gather.1 = (bf16[1024,256]{1,0:T(8,128)(2,1)}, bf16[768,256]{1,0:T(8,128)(2,1)S(1)}) custom-call(bf16[128,8,512]{2,1,0:T(8,128)(2,1)S(1)} %all-to-all-done.got, f32[8192,128]{1,0:T(8,128)S(1)} %bitcast.25, f32[8192,128]{1,0:T(8,128)S(1)} %bitcast.26), custom_call_target="tpu_custom_call" | custom-call | flops 5000000000 | tf_op jit(solution)/shard_map/gather/pallas_call | solution.py:368
  61.6 0.0 copy-done.12
  61.7 12.2 %adjoint.1 = (f32[8192,128]{1,0:T(8,128)S(1)}, bf16[256,128]{1,0:T(8,128)(2,1)S(1)}, bf16[256,128]{1,0:T(8,128)(2,1)S(1)}, bf16[128,128]{1,0:T(8,128)(2,1)S(1)}, bf16[128,128]{1,0:T(8,128)(2,1)S(1)}) custom-call(bf16[128,8,512]{2,1,0:T(8,128)(2,1)S(1)} %all-to-all-done.got, bf16[768,256]{1,0:T(8,128)(2,1)S(1)} %get-tuple-element.25.slots, ...), custom_call_target="tpu_custom_call" | custom-call | flops 10000000000 | tf_op jit(solution)/shard_map/adjoint/pallas_call | solution.py:466
  73.8 0.0 copy-start.21
  73.9 2.0 %copy-done.21 = f32[8192,128]{1,0:T(8,128)} copy-done((f32[8192,128]{1,0:T(8,128)}, f32[8192,128]{1,0:T(8,128)S(1)}, u32[]{:S(2)}) %copy-start.21) | copy-done | bytes 4194328
  75.9 7.6 %collective-permute-start.8 = (bf16[128,128]{1,0:T(8,128)(2,1)S(1)}, bf16[128,128]{1,0:T(8,128)(2,1)S(1)}, u32[]{:S(2)}, u32[]{:S(2)}) collective-permute-start(bf16[128,128]{1,0:T(8,128)(2,1)S(1)} %get-tuple-element.30), channel_id=1, source_target_pairs={{0,1},{1,2},{2,3},{3,4},{4,5},{5,6},{6,7},{7,0},{8,9},{9,10},{10,1... | collective-permute-start | bytes 98312 | tf_op jit(solution)/shard_map/ppermute | solution.py:192
  83.4 0.0 collective-permute-start.9
  83.4 0.0 collective-permute-start.6
  83.4 4.8 %collective-permute-start.7 = (bf16[256,128]{1,0:T(8,128)(2,1)S(1)}, bf16[256,128]{1,0:T(8,128)(2,1)S(1)}, u32[]{:S(2)}, u32[]{:S(2)}) collective-permute-start(bf16[256,128]{1,0:T(8,128)(2,1)S(1)} %get-tuple-element.29), channel_id=1, source_target_pairs={{0,120},{8,0},{16,8},{24,16},{32,24},{40,32},{48,40},{56,48},{64,5... | collective-permute-start | bytes 196616 | tf_op jit(solution)/shard_map/ppermute | solution.py:192
  88.2 0.0 collective-permute-done.8.y_low
  88.2 0.0 collective-permute-done.9.y_high
  88.3 0.1 collective-permute-start.11
  88.4 1.5 %collective-permute-start.10 = (bf16[2,128]{1,0:T(2,128)(2,1)S(1)}, bf16[2,128]{1,0:T(2,128)(2,1)S(1)}, u32[]{:S(2)}, u32[]{:S(2)}) collective-permute-start(bf16[2,128]{1,0:T(2,128)(2,1)S(1)} %pad_maximum_fusion.4), channel_id=1, source_target_pairs={{0,8},{8,16},{16,24},{24,32},{32,40},{40,48},{48,56},{56,64},{64,7... | collective-permute-start | bytes 1544 | tf_op jit(solution)/shard_map/ppermute | solution.py:192
  89.9 9.1 %all-to-all-start.1 = ((bf16[128,8,256]{2,1,0:T(8,128)(2,1)}), bf16[128,8,256]{2,1,0:T(8,128)(2,1)S(1)}, u32[]{:S(2)}, u32[]{:S(2)}) async-start(bf16[128,8,256]{2,1,0:T(8,128)(2,1)} %bitcast.7), calls=%async_computation.1 | async-start | bytes 1048576 | tf_op jit(solution)/shard_map/all_to_all | solution.py:575
  99.0 0.0 collective-permute-done.11.high
  99.0 0.0 collective-permute-done.10.low
  99.0 0.0 collective-permute-done.6.x_low
  99.0 0.0 collective-permute-done.7.x_high
  99.0 0.0 copy-start.1
  99.0 2.2 %copy-done.1 = f32[128,64,128]{2,1,0:T(8,128)S(1)} copy-done((f32[128,64,128]{2,1,0:T(8,128)S(1)}, f32[128,64,128]{2,1,0:T(8,128)}, u32[]{:S(2)}) %copy-start.1) | copy-done | bytes 4194328
  101.2 2.4 %copy-done.20 = f32[68,144,128]{2,1,0:T(8,128)S(1)} copy-done((f32[68,144,128]{2,1,0:T(8,128)S(1)}, f32[68,144,128]{2,1,0:T(8,128)}, u32[]{:S(2)}) %copy-start.20) | copy-done | bytes 5013528
  103.6 2.2 %copy-done.22 = f32[8192,128]{1,0:T(8,128)S(1)} copy-done((f32[8192,128]{1,0:T(8,128)S(1)}, f32[8192,128]{1,0:T(8,128)}, u32[]{:S(2)}) %copy-start.22) | copy-done | bytes 4194328
  105.8 9.1 %gradient.1 = f32[128,64,128]{2,1,0:T(8,128)} custom-call(f32[8192,128]{1,0:T(8,128)S(1)} %copy-done.22, f32[68,144,128]{2,1,0:T(8,128)S(1)} %copy-done.20, bf16[256,128]{1,0:T(8,128)(2,1)S(1)} %collective-permute-done.6.x_low, bf16[256,128]{1,0:T(8,128)(2,1)S(1)} %collective-permute-done.7.x_high, bf16[128,128]{1,0:T(8,128)(2,1)S(1)} %collective-permute-done.8.y_low, ...), custom_call_target="tpu_custom_call" | custom-call | flops 8000000000 | tf_op jit(solution)/shard_map/gradient/pallas_call | solution.py:561
  114.9 0.0 all-to-all-done.1
  114.9 2.5 %departures.1 = f32[616,256]{1,0:T(8,128)} custom-call(bf16[1024,256]{1,0:T(8,128)(2,1)S(1)} %bitcast.12, s32[1,256]{1,0:T(1,128)S(1)} %bitcast.24, f32[616,256]{1,0:T(8,128)S(1)} %bitcast.14, bf16[128,512]{1,0:T(8,128)(2,1)S(1)} %copy-done.6, f32[1,512]{1,0:T(1,128)S(1)} %bitcast.19, bf16[512,512]{1,0:T(8,128)(2,1)S(1)} %copy-done.5, ...), custom_call_target="tpu_custom_call" | custom-call | flops 4000000000 | tf_op jit(solution)/shard_map/departures/pallas_call | solution.py:504
  (30 shorter events, 0.1 us)
Async XLA Ops:
  0.6 2.2 %copy-start = (f32[128,64,128]{2,1,0:T(8,128)S(1)}, f32[128,64,128]{2,1,0:T(8,128)}, u32[]{:S(2)}) copy-start(f32[128,64,128]{2,1,0:T(8,128)} %control.3) | copy-start | bytes 12582916
  2.8 1.6 %copy-start.2 = (bf16[128,64,128]{2,1,0:T(8,128)(2,1)S(1)}, bf16[128,64,128]{2,1,0:T(8,128)(2,1)}, u32[]{:S(2)}) copy-start(bf16[128,64,128]{2,1,0:T(8,128)(2,1)} %background.1) | copy-start | bytes 6291460
  4.4 0.8 copy-start.7
  5.2 14.1 %copy-start.3 = (f32[256,616]{0,1:T(8,128)S(1)}, f32[256,616]{0,1:T(8,128)}, u32[]{:S(2)}) copy-start(f32[256,616]{0,1:T(8,128)} %param.19) | copy-start | bytes 1892356
  5.2 14.1 %copy-start.4 = (bf16[512,616]{0,1:T(8,128)(2,1)S(1)}, bf16[512,616]{0,1:T(8,128)(2,1)}, u32[]{:S(2)}) copy-start(bf16[512,616]{0,1:T(8,128)(2,1)} %param.25) | copy-start | bytes 1892356
  5.2 14.1 %copy-start.9 = (f32[616]{0:T(1024)S(1)}, f32[616]{0:T(1024)}, u32[]{:S(2)}) copy-start(f32[616]{0:T(1024)} %ivar.5) | copy-start | bytes 7396
  5.2 14.2 %copy-start.10 = (f32[2,256]{1,0:T(2,128)S(1)}, f32[2,256]{1,0:T(2,128)}, u32[]{:S(2)}) copy-start(f32[2,256]{1,0:T(2,128)} %frac.1) | copy-start | bytes 6148
  5.2 14.2 %copy-start.13 = (s32[256]{0:T(256)S(1)}, s32[256]{0:T(256)}, u32[]{:S(2)}) copy-start(s32[256]{0:T(256)} %param.17) | copy-start | bytes 3076
  5.2 14.2 %copy-start.14 = (s32[256,1]{0,1:T(1,128)S(1)}, s32[256,1]{0,1:T(1,128)}, u32[]{:S(2)}) copy-start(s32[256,1]{0,1:T(1,128)} %param.16) | copy-start | bytes 3076
  10.5 11.2 %copy-start.15 = (f32[64,128,128]{2,1,0:T(8,128)}, f32[64,128,128]{2,1,0:T(8,128)S(1)}, u32[]{:S(2)}) copy-start(f32[64,128,128]{2,1,0:T(8,128)S(1)} %get-tuple-element.17) | copy-start | bytes 12582916
  10.5 11.2 %copy-start.23 = (f32[64,128,128]{2,1,0:T(8,128)}, f32[64,128,128]{2,1,0:T(8,128)S(1)}, u32[]{:S(2)}) copy-start(f32[64,128,128]{2,1,0:T(8,128)S(1)} %get-tuple-element.18.ct) | copy-start | bytes 12582916
  10.5 17.6 %collective-permute-start.2 = (bf16[144,128]{1,0:T(8,128)(2,1)S(1)}, bf16[144,128]{1,0:T(8,128)(2,1)S(1)}, u32[]{:S(2)}, u32[]{:S(2)}) collective-permute-start(bf16[144,128]{1,0:T(8,128)(2,1)S(1)} %get-tuple-element.21), channel_id=1, source_target_pairs={{0,1},{1,2},{2,3},{3,4},{4,5},{5,6},{6,7},{7,0},{8,9},{9,10},{10,1... | collective-permute-start | bytes 110600 | tf_op jit(solution)/shard_map/ppermute | solution.py:192
  13.1 15.0 %collective-permute-start.3 = (bf16[144,128]{1,0:T(8,128)(2,1)S(1)}, bf16[144,128]{1,0:T(8,128)(2,1)S(1)}, u32[]{:S(2)}, u32[]{:S(2)}) collective-permute-start(bf16[144,128]{1,0:T(8,128)(2,1)S(1)} %get-tuple-element.22), channel_id=1, source_target_pairs={{0,7},{1,0},{2,1},{3,2},{4,3},{5,4},{6,5},{7,6},{8,15},{9,8},{10,9... | collective-permute-start | bytes 110600 | tf_op jit(solution)/shard_map/ppermute | solution.py:192
  13.1 26.2 %collective-permute-start = (bf16[272,128]{1,0:T(8,128)(2,1)S(1)}, bf16[272,128]{1,0:T(8,128)(2,1)S(1)}, u32[]{:S(2)}, u32[]{:S(2)}) collective-permute-start(bf16[272,128]{1,0:T(8,128)(2,1)S(1)} %get-tuple-element.19), channel_id=1, source_target_pairs={{0,8},{8,16},{16,24},{24,32},{32,40},{40,48},{48,56},{56,64},{64,7... | collective-permute-start | bytes 208904 | tf_op jit(solution)/shard_map/ppermute | solution.py:192
  14.4 24.9 %collective-permute-start.1 = (bf16[272,128]{1,0:T(8,128)(2,1)S(1)}, bf16[272,128]{1,0:T(8,128)(2,1)S(1)}, u32[]{:S(2)}, u32[]{:S(2)}) collective-permute-start(bf16[272,128]{1,0:T(8,128)(2,1)S(1)} %get-tuple-element.20), channel_id=1, source_target_pairs={{0,120},{8,0},{16,8},{24,16},{32,24},{40,32},{48,40},{56,48},{64,5... | collective-permute-start | bytes 208904 | tf_op jit(solution)/shard_map/ppermute | solution.py:192
  19.4 20.0 %copy-start.8 = (f32[64,128]{1,0:T(8,128)S(1)}, f32[64,128]{1,0:T(8,128)}, u32[]{:S(2)}) copy-start(f32[64,128]{1,0:T(8,128)} %spread.3) | copy-start | bytes 98308
  21.6 30.1 %all-to-all-start = ((bf16[128,8,512]{2,1,0:T(8,128)(2,1)}), bf16[128,8,512]{2,1,0:T(8,128)(2,1)S(1)}, u32[]{:S(2)}, u32[]{:S(2)}) async-start(bf16[128,8,512]{2,1,0:T(8,128)(2,1)} %bitcast.4), calls=%async_computation | async-start | bytes 2097152 | tf_op jit(solution)/shard_map/all_to_all | solution.py:575
  28.2 11.1 %collective-permute-start.4 = (bf16[34,128]{1,0:T(8,128)(2,1)S(1)}, bf16[34,128]{1,0:T(8,128)(2,1)S(1)}, u32[]{:S(2)}, u32[]{:S(2)}) collective-permute-start(bf16[34,128]{1,0:T(8,128)(2,1)S(1)} %get-tuple-element.41), channel_id=1, source_target_pairs={{0,8},{8,16},{16,24},{24,32},{32,40},{40,48},{48,56},{56,64},{64,7... | collective-permute-start | bytes 26120 | tf_op jit(solution)/shard_map/ppermute | solution.py:192
  29.6 9.7 %collective-permute-start.5 = (bf16[34,128]{1,0:T(8,128)(2,1)S(1)}, bf16[34,128]{1,0:T(8,128)(2,1)S(1)}, u32[]{:S(2)}, u32[]{:S(2)}) collective-permute-start(bf16[34,128]{1,0:T(8,128)(2,1)S(1)} %get-tuple-element.40), channel_id=1, source_target_pairs={{0,120},{8,0},{16,8},{24,16},{32,24},{40,32},{48,40},{56,48},{64,5... | collective-permute-start | bytes 26120 | tf_op jit(solution)/shard_map/ppermute | solution.py:192
  39.3 2.2 %copy-start.24 = (f32[64,128,128]{2,1,0:T(8,128)S(1)}, f32[64,128,128]{2,1,0:T(8,128)}, u32[]{:S(2)}) copy-start(f32[64,128,128]{2,1,0:T(8,128)} %copy-done.23) | copy-start | bytes 12582916
  47.4 2.0 %copy-start.17 = (f32[64,128,128]{2,1,0:T(8,128)}, f32[64,128,128]{2,1,0:T(8,128)S(1)}, u32[]{:S(2)}) copy-start(f32[64,128,128]{2,1,0:T(8,128)S(1)} %get-tuple-element.23) | copy-start | bytes 12582916
  49.5 2.3 %copy-start.19 = (f32[68,144,128]{2,1,0:T(8,128)}, f32[68,144,128]{2,1,0:T(8,128)S(1)}, u32[]{:S(2)}) copy-start(f32[68,144,128]{2,1,0:T(8,128)S(1)} %get-tuple-element.27.coef) | copy-start | bytes 15040516
  51.8 2.2 %copy-start.16 = (f32[64,128,128]{2,1,0:T(8,128)S(1)}, f32[64,128,128]{2,1,0:T(8,128)}, u32[]{:S(2)}) copy-start(f32[64,128,128]{2,1,0:T(8,128)} %copy-done.15) | copy-start | bytes 12582916
  53.9 2.2 %copy-start.18 = (f32[64,128,128]{2,1,0:T(8,128)S(1)}, f32[64,128,128]{2,1,0:T(8,128)}, u32[]{:S(2)}) copy-start(f32[64,128,128]{2,1,0:T(8,128)} %copy-done.17) | copy-start | bytes 12582916
  56.1 5.5 %copy-start.5 = (bf16[512,512]{1,0:T(8,128)(2,1)S(1)}, bf16[512,512]{1,0:T(8,128)(2,1)}, u32[]{:S(2)}) copy-start(bf16[512,512]{1,0:T(8,128)(2,1)} %w_second.3) | copy-start | bytes 1572868
  56.1 5.5 %copy-start.6 = (bf16[128,512]{1,0:T(8,128)(2,1)S(1)}, bf16[128,512]{1,0:T(8,128)(2,1)}, u32[]{:S(2)}) copy-start(bf16[128,512]{1,0:T(8,128)(2,1)} %w_first.3) | copy-start | bytes 393220
  56.1 5.5 %copy-start.11 = (f32[512]{0:T(512)S(1)}, f32[512]{0:T(512)}, u32[]{:S(2)}) copy-start(f32[512]{0:T(512)} %param.22) | copy-start | bytes 6148
  56.1 5.5 %copy-start.12 = (f32[512]{0:T(512)S(1)}, f32[512]{0:T(512)}, u32[]{:S(2)}) copy-start(f32[512]{0:T(512)} %param.24) | copy-start | bytes 6148
  73.8 2.0 %copy-start.21 = (f32[8192,128]{1,0:T(8,128)}, f32[8192,128]{1,0:T(8,128)S(1)}, u32[]{:S(2)}) copy-start(f32[8192,128]{1,0:T(8,128)S(1)} %get-tuple-element.26.acc) | copy-start | bytes 12582916
  75.9 12.4 %collective-permute-start.8 = (bf16[128,128]{1,0:T(8,128)(2,1)S(1)}, bf16[128,128]{1,0:T(8,128)(2,1)S(1)}, u32[]{:S(2)}, u32[]{:S(2)}) collective-permute-start(bf16[128,128]{1,0:T(8,128)(2,1)S(1)} %get-tuple-element.30), channel_id=1, source_target_pairs={{0,1},{1,2},{2,3},{3,4},{4,5},{5,6},{6,7},{7,0},{8,9},{9,10},{10,1... | collective-permute-start | bytes 98312 | tf_op jit(solution)/shard_map/ppermute | solution.py:192
  83.4 4.8 %collective-permute-start.9 = (bf16[128,128]{1,0:T(8,128)(2,1)S(1)}, bf16[128,128]{1,0:T(8,128)(2,1)S(1)}, u32[]{:S(2)}, u32[]{:S(2)}) collective-permute-start(bf16[128,128]{1,0:T(8,128)(2,1)S(1)} %get-tuple-element.31), channel_id=1, source_target_pairs={{0,7},{1,0},{2,1},{3,2},{4,3},{5,4},{6,5},{7,6},{8,15},{9,8},{10,9... | collective-permute-start | bytes 98312 | tf_op jit(solution)/shard_map/ppermute | solution.py:192
  83.4 15.5 %collective-permute-start.6 = (bf16[256,128]{1,0:T(8,128)(2,1)S(1)}, bf16[256,128]{1,0:T(8,128)(2,1)S(1)}, u32[]{:S(2)}, u32[]{:S(2)}) collective-permute-start(bf16[256,128]{1,0:T(8,128)(2,1)S(1)} %get-tuple-element.28), channel_id=1, source_target_pairs={{0,8},{8,16},{16,24},{24,32},{32,40},{40,48},{48,56},{56,64},{64,7... | collective-permute-start | bytes 196616 | tf_op jit(solution)/shard_map/ppermute | solution.py:192
  83.4 15.6 %collective-permute-start.7 = (bf16[256,128]{1,0:T(8,128)(2,1)S(1)}, bf16[256,128]{1,0:T(8,128)(2,1)S(1)}, u32[]{:S(2)}, u32[]{:S(2)}) collective-permute-start(bf16[256,128]{1,0:T(8,128)(2,1)S(1)} %get-tuple-element.29), channel_id=1, source_target_pairs={{0,120},{8,0},{16,8},{24,16},{32,24},{40,32},{48,40},{56,48},{64,5... | collective-permute-start | bytes 196616 | tf_op jit(solution)/shard_map/ppermute | solution.py:192
  88.3 10.7 %collective-permute-start.11 = (bf16[2,128]{1,0:T(2,128)(2,1)S(1)}, bf16[2,128]{1,0:T(2,128)(2,1)S(1)}, u32[]{:S(2)}, u32[]{:S(2)}) collective-permute-start(bf16[2,128]{1,0:T(2,128)(2,1)S(1)} %pad_maximum_fusion.5), channel_id=1, source_target_pairs={{0,120},{8,0},{16,8},{24,16},{32,24},{40,32},{48,40},{56,48},{64,5... | collective-permute-start | bytes 1544 | tf_op jit(solution)/shard_map/ppermute | solution.py:192
  88.4 10.6 %collective-permute-start.10 = (bf16[2,128]{1,0:T(2,128)(2,1)S(1)}, bf16[2,128]{1,0:T(2,128)(2,1)S(1)}, u32[]{:S(2)}, u32[]{:S(2)}) collective-permute-start(bf16[2,128]{1,0:T(2,128)(2,1)S(1)} %pad_maximum_fusion.4), channel_id=1, source_target_pairs={{0,8},{8,16},{16,24},{24,32},{32,40},{40,48},{48,56},{56,64},{64,7... | collective-permute-start | bytes 1544 | tf_op jit(solution)/shard_map/ppermute | solution.py:192
  89.9 25.0 %all-to-all-start.1 = ((bf16[128,8,256]{2,1,0:T(8,128)(2,1)}), bf16[128,8,256]{2,1,0:T(8,128)(2,1)S(1)}, u32[]{:S(2)}, u32[]{:S(2)}) async-start(bf16[128,8,256]{2,1,0:T(8,128)(2,1)} %bitcast.7), calls=%async_computation.1 | async-start | bytes 1048576 | tf_op jit(solution)/shard_map/all_to_all | solution.py:575
  99.0 2.2 %copy-start.1 = (f32[128,64,128]{2,1,0:T(8,128)S(1)}, f32[128,64,128]{2,1,0:T(8,128)}, u32[]{:S(2)}) copy-start(f32[128,64,128]{2,1,0:T(8,128)} %control.3) | copy-start | bytes 12582916
  101.2 2.4 %copy-start.20 = (f32[68,144,128]{2,1,0:T(8,128)S(1)}, f32[68,144,128]{2,1,0:T(8,128)}, u32[]{:S(2)}) copy-start(f32[68,144,128]{2,1,0:T(8,128)} %copy-done.19) | copy-start | bytes 15040516
  103.6 2.2 %copy-start.22 = (f32[8192,128]{1,0:T(8,128)S(1)}, f32[8192,128]{1,0:T(8,128)}, u32[]{:S(2)}) copy-start(f32[8192,128]{1,0:T(8,128)} %copy-done.21) | copy-start | bytes 12582916

commit v3 on v2

--- a/solution.py
+++ b/solution.py
@@ -1,9 +1,12 @@
+import functools
+
 import jax
 import jax.numpy as jnp
 from jax import lax
 from jax.experimental import pallas as pl
 from jax.experimental.pallas import tpu as pltpu
 from jax.sharding import PartitionSpec as P
+
 
 F32 = jnp.float32
 BF16 = jnp.bfloat16
@@ -37,6 +40,14 @@
 
 def down(row):
     return jnp.transpose(jnp.broadcast_to(row, (LEV, row.shape[1])))
+
+
+def in_vmem(array):
+    return pltpu.with_memory_space_constraint(array, pltpu.VMEM)
+
+
+def in_hbm(array):
+    return pltpu.with_memory_space_constraint(array, pltpu.HBM)
 
 
 def nn(a, b):
@@ -122,7 +133,7 @@
         )
         turned = nt(pair, both)
         ct[i] = turned[:, :LEV]
-        bgt[i] = turned[:, LEV:]
+        bgt[i] = turned[:, LEV:].astype(BF16)
         for n, y in enumerate((0, 1, BY - 2, BY - 1)):
             planes[n, pl.ds(step * CHUNK + i, 1), :] = turned[y : y + 1, :LEV]
 
@@ -170,8 +181,8 @@
             pl.BlockSpec((2 * BX + 16, LEV), keep),
         ],
         out_shape=[
-            jax.ShapeDtypeStruct((BX, BY, LEV), F32),
-            jax.ShapeDtypeStruct((BX, BY, LEV), F32),
+            pltpu.HBM((BX, BY, LEV), F32),
+            pltpu.HBM((BX, BY, LEV), BF16),
             jax.ShapeDtypeStruct((2 * BY + 16, LEV), BF16),
             jax.ShapeDtypeStruct((2 * BY + 16, LEV), BF16),
             jax.ShapeDtypeStruct((2 * BX + 16, LEV), BF16),
@@ -184,7 +195,7 @@
         compiler_params=params(10, dimension_semantics=("arbitrary",)),
         cost_estimate=cost(6),
         name="columns",
-    )(control, background, spread)
+    )(in_hbm(control), in_hbm(background), spread)
 
 
 def shift(array, axis, by):
@@ -192,21 +203,26 @@
     return lax.ppermute(array, axis, [(i, (i + by) % count) for i in range(count)])
 
 
-def rims_around(x_up, x_down, y_up, y_down):
-    y_low = shift(y_up, "obs", 1)
-    y_high = shift(y_down, "obs", -1)
-    x_low = shift(x_up, "tile", 1)
-    x_high = shift(x_down, "tile", -1)
-
-    def corner(row):
-        low, high = BX + row, row
-        return jnp.concatenate(
-            [y_low[low : low + 1], y_high[high : high + 1], y_low[2 * BX :], y_high[2 * BX :]], axis=0
-        )
-
-    low = shift(corner(BX - 1), "tile", 1)
-    high = shift(corner(0), "tile", -1)
-    return x_low, x_high, y_low, y_high, low, high
+def compose_kernel(x_up, x_down, y_low, y_high, up, down):
+    rows = x_up.shape[0]
+    up[:rows, :] = x_up[...]
+    down[:rows, :] = x_down[...]
+    low = y_low[...].astype(F32)
+    high = y_high[...].astype(F32)
+    fields = [low[2 * BX :], high[2 * BX :]] if low.shape[0] > 2 * BX else []
+    for out, row in ((up, BX - 1), (down, 0)):
+        pair = [low[BX + row : BX + row + 1], high[row : row + 1], jnp.zeros((14, LEV), F32)]
+        out[rows:, :] = jnp.concatenate(pair + fields, axis=0).astype(BF16)
+
+
+def compose(x_up, x_down, y_low, y_high):
+    rows = x_up.shape[0] + 16 + 2 * (y_low.shape[0] - 2 * BX)
+    return pl.pallas_call(
+        compose_kernel,
+        out_shape=[jax.ShapeDtypeStruct((rows, LEV), BF16)] * 2,
+        compiler_params=params(2),
+        name="compose",
+    )(x_up, x_down, y_low, y_high)
 
 
 def laplace(field, x, first, count):
@@ -236,33 +252,34 @@
     return jnp.broadcast_to(column, (column.shape[0], LEV))
 
 
-def fill_rims(field, x_low, x_high, y_low, y_high, low, high):
+def joined(rows, at):
+    block = rows[at : at + 16, :].astype(F32)
+    return block[0:2] + block[2:4]
+
+
+def fill_y(field, y_low, y_high):
+    for n in range(2):
+        set_plane(field, 2, 6 + n, BX, y_low[n * BX : (n + 1) * BX, :].astype(F32))
+        set_plane(field, 2, 8 + BY + n, BX, y_high[n * BX : (n + 1) * BX, :].astype(F32))
+
+
+def fill_x(field, x_low, x_high, at):
     for n in range(2):
         field[n, 8 : 8 + BY, :] = x_low[n * BY : (n + 1) * BY, :].astype(F32)
         field[BX + 2 + n, 8 : 8 + BY, :] = x_high[n * BY : (n + 1) * BY, :].astype(F32)
-        set_plane(field, 2, 6 + n, BX, y_low[n * BX : (n + 1) * BX, :].astype(F32))
-        set_plane(field, 2, 8 + BY + n, BX, y_high[n * BX : (n + 1) * BX, :].astype(F32))
-    low_rows = low[...].astype(F32)
-    high_rows = high[...].astype(F32)
-    field[1, 7:8, :] = low_rows[0:1]
-    field[1, 8 + BY : 9 + BY, :] = low_rows[1:2]
-    field[BX + 2, 7:8, :] = high_rows[0:1]
-    field[BX + 2, 8 + BY : 9 + BY, :] = high_rows[1:2]
-
-
-def joined(rows, at):
-    block = rows[at : at + 16, :].astype(F32)
-    return block[0:2] + block[2:4]
-
-
-def increment_kernel(ct, spread, x_low, x_high, y_low, y_high, low, high, inc, coef, field, first):
+    for rows, x in ((x_low, 1), (x_high, BX + 2)):
+        pair = rows[at : at + 16, :].astype(F32)
+        field[x, 7:8, :] = pair[0:1]
+        field[x, 8 + BY : 9 + BY, :] = pair[1:2]
+
+
+def coefficients(coef, spread, x_low, x_high, y_low, y_high, rows):
     square = jnp.concatenate(
         [joined(x_low, 2 * BY), spread[...], joined(x_high, 2 * BY), jnp.zeros((BY - PX, BY), F32)],
         axis=0,
     )
     turned = jnp.transpose(square)
-
-    for x in range(PX):
+    for x in rows:
         coef[x, 8 : 8 + BY, :] = lanes(turned[:, x : x + 1])
     sides = jnp.concatenate(
         [joined(y_low, 2 * BX), joined(y_high, 2 * BX), jnp.zeros((BY - 4, BY), F32)], axis=0
@@ -271,21 +288,48 @@
     for n in range(2):
         set_plane(coef, 2, 6 + n, BX, lanes(sides[:, n : n + 1]))
         set_plane(coef, 2, 8 + BY + n, BX, lanes(sides[:, 2 + n : 3 + n]))
-    for rows, x, lane in ((low, 1, BX - 1), (high, BX + 2, 0)):
-        block = rows[...].astype(F32)
-        left = block[2:4] + block[4:6]
-        right = block[18:20] + block[20:22]
+    for block, x, lane in ((x_low, 1, BX - 1), (x_high, BX + 2, 0)):
+        left = joined(block, 2 * BY + 32)
+        right = joined(block, 2 * BY + 48)
         coef[x, 7:8, :] = lanes(left[1:2, lane : lane + 1])
         coef[x, 8 + BY : 9 + BY, :] = lanes(right[0:1, lane : lane + 1])
-    field[2 : 2 + BX, 8 : 8 + BY, :] = ct[...]
-    fill_rims(field, x_low, x_high, y_low, y_high, low, high)
+
+
+def joined(rows, at):
+    block = rows[at : at + 16, :].astype(F32)
+    return block[0:2] + block[2:4]
+
+
+PARTS = BX // CHUNK
+
+
+def increment_kernel(
+    ct, spread, x_low, x_high, y_low, y_high, inc, coef, field, first, done, came, went
+):
+    def bring(part):
+        at = pl.ds(part * CHUNK, CHUNK)
+        to = field.at[pl.ds(2 + part * CHUNK, CHUNK), pl.ds(8, BY)]
+        return pltpu.make_async_copy(ct.at[at], to, came.at[part])
+
+    def leave(part):
+        at = pl.ds(part * CHUNK, CHUNK)
+        return pltpu.make_async_copy(done.at[at], inc.at[at], went.at[part])
+
+    for part in range(PARTS):
+        bring(part).start()
+    coefficients(coef, spread, x_low, x_high, y_low, y_high, range(PX))
+    fill_x(field, x_low, x_high, 2 * BY + 16)
+    fill_y(field, y_low, y_high)
 
     def sweep_one(x, carry):
         middle = field[x, 8 : 8 + BY, :]
         first[x, 8 : 8 + BY, :] = middle + coef[x, 8 : 8 + BY, :] * laplace(field, x, 8, BY)
         return carry
 
-    lax.fori_loop(1, PX - 1, sweep_one, 0)
+    for part in range(PARTS):
+        bring(part).wait()
+        last = PX - 1 if part == PARTS - 1 else 1 + CHUNK * (part + 1)
+        lax.fori_loop(1 + CHUNK * part, last, sweep_one, 0)
     for y in (7, 8 + BY):
         moved = plane(field, 2, y, BX) + plane(coef, 2, y, BX) * plane_laplace(field, y)
         set_plane(first, 2, y, BX, moved)
@@ -293,24 +337,34 @@
     def sweep_two(x, carry):
         middle = first[x, 8 : 8 + BY, :]
         result = middle + coef[x, 8 : 8 + BY, :] * laplace(first, x, 8, BY)
-        inc[x - 2] = result.astype(BF16).astype(F32)
+        done[x - 2] = result.astype(BF16)
         return carry
 
-    lax.fori_loop(2, PX - 2, sweep_two, 0)
+    for part in range(PARTS):
+        lax.fori_loop(2 + CHUNK * part, 2 + CHUNK * (part + 1), sweep_two, 0)
+        leave(part).start()
+    for part in range(PARTS):
+        leave(part).wait()
 
 
 def increments(ct, spread, rims):
+    any_space = pl.BlockSpec(memory_space=pltpu.HBM)
+    whole = pl.BlockSpec(memory_space=pltpu.VMEM)
     return pl.pallas_call(
         increment_kernel,
-        out_shape=[
-            jax.ShapeDtypeStruct((BX, BY, LEV), F32),
-            jax.ShapeDtypeStruct((PX, PY, LEV), F32),
-        ],
-        scratch_shapes=[pltpu.VMEM((PX, PY, LEV), F32), pltpu.VMEM((PX, PY, LEV), F32)],
+        in_specs=[any_space] + [whole] * 5,
+        out_specs=any_space,
+        out_shape=pltpu.HBM((BX, BY, LEV), BF16),
+        scratch_shapes=[pltpu.VMEM((PX, PY, LEV), F32)] * 3
+        + [
+            pltpu.VMEM((BX, BY, LEV), BF16),
+            pltpu.SemaphoreType.DMA((PARTS,)),
+            pltpu.SemaphoreType.DMA((PARTS,)),
+        ],
         compiler_params=params(27),
         cost_estimate=cost(6),
         name="increment",
-    )(ct, spread, *rims)
+    )(in_hbm(ct), spread, *rims)
 
 
 def decode(rows):
@@ -328,11 +382,34 @@
     )
 
 
-def gather_kernel(got, bgt, inct, reply, slots, wide, cells, table, ga, gb, gc, gd, spaced):
+def gather_kernel(
+    got, background, increment, reply, slots,
+    wide, cells, table, ga, gb, gc, gd, spaced, bgt, inct, packed, came,
+):
+    part = CELLS // PARTS
+
+    def bring(n, i):
+        at = pl.ds(i * part, part)
+        source = (background, increment)[n]
+        return pltpu.make_async_copy(source.at[at], packed.at[n, at], came.at[n, i])
+
+    for i in range(PARTS):
+        bring(0, i).start()
+        bring(1, i).start()
     wide[...] = got[...].astype(F32).reshape(DEV * ROWS, LEV)
     cell, weights = decode(wide[pl.ds(CAP, DEV, stride=ROWS), :])
     cells[...] = cell
     pltpu.sync_copy(cells, table)
+    for i in range(PARTS):
+        for n, wider in ((0, bgt), (1, inct)):
+            bring(n, i).wait()
+
+            def widen(j, carry):
+                at = pl.ds(pl.multiple_of(i * part + j * BY, BY), BY)
+                wider[at, :] = packed[n, at, :].astype(F32)
+                return carry
+
+            lax.fori_loop(0, part // BY, widen, 0)
     for k in range(CAP):
 
         def fetch(step, carry):
@@ -368,7 +445,8 @@
     return pl.pallas_call(
         gather_kernel,
         grid=(1,),
-        in_specs=[pl.BlockSpec((DEV, ROWS, LEV), lambda i: (0, 0, 0)), whole, whole],
+        in_specs=[pl.BlockSpec((DEV, ROWS, LEV), lambda i: (0, 0, 0))]
+        + [pl.BlockSpec(memory_space=pltpu.HBM)] * 2,
         out_specs=[whole, whole],
         out_shape=[
             jax.ShapeDtypeStruct((DEV * ROWS, 2 * LEV), BF16),
@@ -383,11 +461,15 @@
             rows,
             rows,
             pltpu.VMEM((2, DEV * ROWS, LEV), F32),
-        ],
-        compiler_params=params(18),
+            pltpu.VMEM((CELLS, LEV), F32),
+            pltpu.VMEM((CELLS, LEV), F32),
+            pltpu.VMEM((2, CELLS, LEV), BF16),
+            pltpu.SemaphoreType.DMA((2, PARTS)),
+        ],
+        compiler_params=params(26),
         cost_estimate=cost(5),
         name="gather",
-    )(got, bgt, inct)
+    )(got, in_hbm(bgt), in_hbm(inct))
 
 
 def tangent(base, delta, w_first, b_first, w_second, b_second):
@@ -466,7 +548,7 @@
     return pl.pallas_call(
         adjoint_kernel,
         out_shape=[
-            jax.ShapeDtypeStruct((CELLS, LEV), F32),
+            pltpu.VMEM((CELLS, LEV), F32),
             jax.ShapeDtypeStruct((2 * BY, LEV), BF16),
             jax.ShapeDtypeStruct((2 * BY, LEV), BF16),
             jax.ShapeDtypeStruct((2 * BX, LEV), BF16),
@@ -510,65 +592,102 @@
     )(reply, holder, innov, w_first, b_first, w_second, b_second, w_third, ivar)
 
 
-def gradient_kernel(
-    acc, coef, x_low, x_high, y_low, y_high, low, high, control, out, field, grown, second
-):
+def gradient_kernel(edge, acc, spread, ax_low, ax_high, ay_low, ay_high, y_low, y_high, *rest):
+    if edge:
+        x_low, x_high, control, _, out, coef, field, grown, second = rest
+    else:
+        control, out, coef, field, grown, second = rest
     step = pl.program_id(0)
+    first = step * (PARTS - 1) * CHUNK if edge else (step + 1) * CHUNK
 
     @pl.when(step == 0)
     def _():
-        fill_rims(field, x_low, x_high, y_low, y_high, low, high)
-
-        def fill(x, carry):
-            field[x, 8 : 8 + BY, :] = acc[pl.ds(pl.multiple_of((x - 2) * BY, BY), BY), :]
-            return carry
-
-        lax.fori_loop(2, PX - 2, fill, 0)
-        grown[...] = field[...]
-
-        def scale(x, carry):
-            field[x] = field[x] * coef[x]
-            return carry
-
-        lax.fori_loop(0, PX, scale, 0)
-
-        def sweep_one(x, carry):
-            value = grown[x, 8 : 8 + BY, :] + laplace(field, x, 8, BY)
-            grown[x, 8 : 8 + BY, :] = value
-            second[x, 8 : 8 + BY, :] = coef[x, 8 : 8 + BY, :] * value
-            return carry
-
-        lax.fori_loop(1, PX - 1, sweep_one, 0)
-        for y in (7, 8 + BY):
-            value = plane(grown, 2, y, BX) + plane_laplace(field, y)
-            set_plane(second, 2, y, BX, plane(coef, 2, y, BX) * value)
-
+        rows = [*range(12), *range(PX - 12, PX)] if edge else range(CHUNK, PX - CHUNK)
+        coefficients(coef, spread, ax_low, ax_high, ay_low, ay_high, rows)
+        fill_y(field, y_low, y_high)
+        if edge:
+            fill_x(field, x_low, x_high, 2 * BY)
+
+    def fill(x, carry):
+        field[x, 8 : 8 + BY, :] = acc[pl.ds(pl.multiple_of((x - 2) * BY, BY), BY), :]
+        return carry
+
+    if edge:
+        start, stop = jnp.where(step == 0, 2, first), jnp.where(step == 0, 12, PX - 2)
+        lax.fori_loop(start, stop, fill, 0)
+    else:
+        lax.fori_loop(jnp.where(step == 0, first, first + 4), first + CHUNK + 4, fill, 0)
+    span = CHUNK + 4
+
+    def scale(i, carry):
+        grown[i] = field[first + i] * coef[first + i]
+        return carry
+
+    lax.fori_loop(0, span, scale, 0)
+
+    def sweep_one(i, carry):
+        value = field[first + i, 8 : 8 + BY, :] + laplace(grown, i, 8, BY)
+        second[1, i, 8 : 8 + BY, :] = value
+        second[0, i, 8 : 8 + BY, :] = coef[first + i, 8 : 8 + BY, :] * value
+        return carry
+
+    lax.fori_loop(1, span - 1, sweep_one, 0)
+
+    def column(ref, offset, y):
+        flat = ref.reshape(ref.shape[0] * PY, LEV)
+        return flat[pl.ds((first + offset) * PY + y, CHUNK, stride=PY), :]
+
+    def local(ref, offset, y):
+        flat = ref.reshape(ref.shape[0] * PY, LEV)
+        return flat[pl.ds(offset * PY + y, CHUNK, stride=PY), :]
+
+    scaled = second.at[0]
+    flat_scaled = scaled.reshape(span * PY, LEV)
+    for y in (7, 8 + BY):
+        total = local(grown, 3, y) + local(grown, 1, y)
+        total = total + local(grown, 2, y + 1) + local(grown, 2, y - 1)
+        value = column(field, 2, y) + (total - 4.0 * local(grown, 2, y))
+        flat_scaled[pl.ds(2 * PY + y, CHUNK, stride=PY), :] = column(coef, 2, y) * value
     pair = eye_pair()
     flat_out = out.reshape(LEV * CHUNK, BY)
     flat_control = control.reshape(LEV * CHUNK, BY)
     for i in range(CHUNK):
-        x = step * CHUNK + i + 2
-        value = grown[x, 8 : 8 + BY, :] + laplace(second, x, 8, BY)
+        value = second[1, 2 + i, 8 : 8 + BY, :] + laplace(scaled, 2 + i, 8, BY)
         high_part, low_part = split_two(value)
         turned = nt(pair, jnp.concatenate([high_part, low_part], axis=1))
         here = pl.ds(i, LEV, stride=CHUNK)
         flat_out[here, :] = turned + flat_control[here, :]
 
 
-def gradient_of(acc, coef, rims, control):
+def gradient_of(acc, spread, before, rims, control, so_far=None):
+    edge = so_far is not None
     whole = pl.BlockSpec(memory_space=pltpu.VMEM)
-    block = pl.BlockSpec((LEV, CHUNK, BY), lambda i: (0, i, 0))
+    if edge:
+        block = pl.BlockSpec((LEV, CHUNK, BY), lambda i: (0, i * (PARTS - 1), 0))
+    else:
+        block = pl.BlockSpec((LEV, CHUNK, BY), lambda i: (0, i + 1, 0))
+    operands = [in_vmem(acc), spread, *before, *rims, in_hbm(control)]
+    specs = [whole] * (len(operands) - 1) + [block]
+    if edge:
+        operands.append(in_hbm(so_far))
+        specs.append(pl.BlockSpec(memory_space=pltpu.HBM))
     return pl.pallas_call(
-        gradient_kernel,
-        grid=(BX // CHUNK,),
-        in_specs=[whole] * 8 + [block],
+        functools.partial(gradient_kernel, edge),
+        grid=(2 if edge else PARTS - 2,),
+        in_specs=specs,
         out_specs=block,
-        out_shape=jax.ShapeDtypeStruct((LEV, BX, BY), F32),
-        scratch_shapes=[pltpu.VMEM((PX, PY, LEV), F32)] * 3,
-        compiler_params=params(30, dimension_semantics=("arbitrary",)),
-        cost_estimate=cost(8),
-        name="gradient",
-    )(acc, coef, *rims, control)
+        out_shape=pltpu.HBM((LEV, BX, BY), F32),
+        input_output_aliases={len(operands) - 1: 0} if edge else {},
+        scratch_shapes=[
+            pltpu.VMEM((PX, PY, LEV), F32),
+            pltpu.VMEM((PX, PY, LEV), F32),
+            pltpu.VMEM((CHUNK + 4, PY, LEV), F32),
+            pltpu.VMEM((2, CHUNK + 4, PY, LEV), F32),
+        ],
+        compiler_params=params(20, dimension_semantics=("arbitrary",)),
+        cost_estimate=cost(2 if edge else 6),
+        name="edges" if edge else "interior",
+    )(*operands)
 
 
 def exchange(array):
@@ -595,18 +714,28 @@
     holder = obs_holder.reshape(1, OWN)
     innov = innovation.T
     w_last = w_third.T
+    ct, bgt, x_up, x_down, y_up, y_down = to_columns(control, background, spread)
+    ay_low, ay_high = shift(y_up, "obs", 1), shift(y_down, "obs", -1)
     asked = requests(holder, obs_anchor.reshape(1, OWN), obs_frac, innov, inverse_var, w_last)
+    x_up, x_down = compose(x_up, x_down, ay_low, ay_high)
+    ax_low, ax_high = shift(x_up, "tile", 1), shift(x_down, "tile", -1)
+    before = (ax_low, ax_high, ay_low, ay_high)
     got = exchange(asked.reshape(DEV, ROWS, HID))
-    ct, bgt, *send = to_columns(control, background, spread)
-    inct, coef = increments(ct, spread, rims_around(*send))
+    inct = increments(ct, spread, before)
     reply, slots = gathered(got, bgt.reshape(CELLS, LEV), inct.reshape(CELLS, LEV))
     reply = exchange(reply.reshape(DEV, ROWS, 2 * LEV))
-    acc, *send = adjoint(got, slots, w_first, b_one, w_second, b_two, w_last, inverse_var)
+    acc, x_up, x_down, y_up, y_down = adjoint(
+        got, slots, w_first, b_one, w_second, b_two, w_last, inverse_var
+    )
+    y_low, y_high = shift(y_up, "obs", 1), shift(y_down, "obs", -1)
+    x_up, x_down = compose(x_up, x_down, y_low, y_high)
+    x_low, x_high = shift(x_up, "tile", 1), shift(x_down, "tile", -1)
+    gradient = gradient_of(acc, spread, before, (y_low, y_high), control)
+    gradient = gradient_of(acc, spread, before, (y_low, y_high, x_low, x_high), control, gradient)
     departures = departures_of(
         reply.reshape(DEV * ROWS, 2 * LEV), holder, innov,
         w_first, b_one, w_second, b_two, w_last, inverse_var,
     ).T
-    gradient = gradient_of(acc, coef, rims_around(*send), control)
     return departures, gradient
 
 

time: 118 us -> 104 us (0.88)
  local copies, waits for them, and re-layouts: 24.3 us -> 9.12 us
  Pallas kernels: 42.7 us -> 52.6 us
  starting transfers between devices: 44 us -> 35.4 us
    unnamed x50 -> x34, local copies, waits for them, and re-layouts: 24.2 us -> 9.12 us
    ppermute x12 -> x8, starting transfers between devices: 28.5 us -> 15 us  [shift(): lax.ppermute(array, axis, [(i, (i + by) % count) for i in range(count)])]
    all_to_all x2, starting transfers between devices: 15.5 us -> 20.3 us  [exchange(): lax.all_to_all(array, ('tile', 'obs'), split_axis=0, concat_axis=0, tiled...]
    pallas_call x3 -> x6, Pallas kernels: 27.2 us -> 32 us  [the longest x2 13.4 us: gradient_of(): pl.pallas_call(functools.partial(gradient_kernel, edge), grid=(2 if edge...]
    pallas_call x1, Pallas kernels: 5.26 us -> 9.06 us  [to_columns(): pl.pallas_call(columns_kernel, grid=(BX // CHUNK,), in_specs=[pl.BlockSpe...]
    pallas_call x1, Pallas kernels: 5.49 us -> 6.71 us  [gathered(): pl.pallas_call(gather_kernel, grid=(1,), in_specs=[pl.BlockSpec((DEV, ROW...]
    ppermute x12 -> x8, waiting for transfers between devices: 5.47 us -> 5.44 us  [shift(): lax.ppermute(array, axis, [(i, (i + by) % count) for i in range(count)])]
  transfers between devices with their start and end apart: 14 -> 10, of which waited for: 1 -> 3; matrix products, arithmetic and copies ran while one was open for 0% -> 0% of each run, Pallas kernels for 15% -> 28%
where the time goes in v3:
time: 104 us; the launch traced here: 103 us
  Pallas kernels  52.6 us (51%)
  starting transfers between devices  35.4 us (34%)
  local copies, waits for them, and re-layouts  9.12 us (9%)
  waiting for transfers between devices  5.44 us (5%)
    all_to_all x2, starting transfers between devices, exchange(): lax.all_to_all(array, ('tile', 'obs'), split_axis=0, concat_axis=0, tiled...  20.3 us
    ppermute x8, starting transfers between devices, shift(): lax.ppermute(array, axis, [(i, (i + by) % count) for i in range(count)])  15 us
    pallas_call x2, Pallas kernels, gradient_of(): pl.pallas_call(functools.partial(gradient_kernel, edge), grid=(2 if edge...  13.4 us
    pallas_call x1, Pallas kernels, adjoint(): pl.pallas_call(adjoint_kernel, out_shape=[pltpu.VMEM((CELLS, LEV), F32),...  12.2 us
    unnamed x34, local copies, waits for them, and re-layouts  9.12 us
    pallas_call x1, Pallas kernels, to_columns(): pl.pallas_call(columns_kernel, grid=(BX // CHUNK,), in_specs=[pl.BlockSpe...  9.06 us
    pallas_call x1, Pallas kernels, gathered(): pl.pallas_call(gather_kernel, grid=(1,), in_specs=[pl.BlockSpec((DEV, ROW...  6.71 us
    pallas_call x1, Pallas kernels, increments(): pl.pallas_call(increment_kernel, in_specs=[any_space] + [whole] * 5, out_...  6.42 us
  transfers between devices with their start and end apart: 10, of which 3 were waited for; matrix products, arithmetic and copies ran while one was open for 0% of the time, Pallas kernels for 28%

profile of v3, /device:TPU:1, one launch (start us, length us, event | category | flops | bytes accessed | tf_op | source)
XLA Modules:
  0.0 103.4 jit_solution(5702942747644101308)
XLA Ops:
  0.6 0.0 copy-start.3
  0.6 1.1 %copy-done.3 = f32[256,616]{0,1:T(8,128)S(1)} copy-done((f32[256,616]{0,1:T(8,128)S(1)}, f32[256,616]{0,1:T(8,128)}, u32[]{:S(2)}) %copy-start.3) | copy-done | bytes 630808
  1.7 0.0 copy-start.5
  1.7 1.1 %copy-done.5 = bf16[512,616]{0,1:T(8,128)(2,1)S(1)} copy-done((bf16[512,616]{0,1:T(8,128)(2,1)S(1)}, bf16[512,616]{0,1:T(8,128)(2,1)}, u32[]{:S(2)}) %copy-start.5) | copy-done | bytes 630808
  2.8 0.0 copy-start.9
  2.8 0.7 copy-done.9
  3.5 0.0 copy-start.11
  3.5 0.7 copy-done.11
  4.2 0.0 copy-start.14
  4.2 0.7 copy-done.14
  4.8 0.0 copy-start.15
  4.8 0.7 copy-done.15
  5.5 0.0 copy-start.2
  5.5 2.3 %requests.1 = bf16[1024,512]{1,0:T(8,128)(2,1)} custom-call(s32[1,256]{1,0:T(1,128)S(1)} %bitcast.23, s32[1,256]{1,0:T(1,128)S(1)} %bitcast.22, f32[2,256]{1,0:T(2,128)S(1)} %copy-done.11, f32[616,256]{1,0:T(8,128)S(1)} %bitcast.13, f32[616]{0:T(1024)S(1)} %copy-done.9, bf16[616,512]{1,0:T(8,128)(2,1)S(1)} %bitcast.15), custom_call_target="tpu_custom_call" | custom-call | flops 4000000000 | tf_op jit(solution)/shard_map/requests/pallas_call | solution.py:109
  7.8 11.5 %all-to-all-start = ((bf16[128,8,512]{2,1,0:T(8,128)(2,1)}), bf16[128,8,512]{2,1,0:T(8,128)(2,1)S(1)}, u32[]{:S(2)}, u32[]{:S(2)}) async-start(bf16[128,8,512]{2,1,0:T(8,128)(2,1)} %bitcast.4), calls=%async_computation | async-start | bytes 2097152 | tf_op jit(solution)/shard_map/all_to_all | solution.py:694
  19.3 0.0 copy-done.2
  19.3 9.1 %columns.1 = (f32[64,128,128]{2,1,0:T(8,128)}, bf16[64,128,128]{2,1,0:T(8,128)(2,1)}, bf16[272,128]{1,0:T(8,128)(2,1)S(1)}, bf16[272,128]{1,0:T(8,128)(2,1)S(1)}...) custom-call(f32[128,64,128]{2,1,0:T(8,128)} %rest_2_.1, bf16[128,64,128]{2,1,0:T(8,128)(2,1)} %background.1, ...), custom_call_target="tpu_custom_call" | custom-call | flops 6000000000 | tf_op jit(solution)/shard_map/columns/pallas_call | solution.py:167
  28.4 1.6 %collective-permute-start = (bf16[144,128]{1,0:T(8,128)(2,1)S(1)}, bf16[144,128]{1,0:T(8,128)(2,1)S(1)}, u32[]{:S(2)}, u32[]{:S(2)}) collective-permute-start(bf16[144,128]{1,0:T(8,128)(2,1)S(1)} %get-tuple-element.23), channel_id=1, source_target_pairs={{0,1},{1,2},{2,3},{3,4},{4,5},{5,6},{6,7},{7,0},{8,9},{9,10},{10,1... | collective-permute-start | bytes 110600 | tf_op jit(solution)/shard_map/ppermute | solution.py:203
  30.0 0.0 collective-permute-start.1
  30.0 1.1 %collective-permute-done.y_low.ay_low = bf16[144,128]{1,0:T(8,128)(2,1)S(1)} collective-permute-done((bf16[144,128]{1,0:T(8,128)(2,1)S(1)}, bf16[144,128]{1,0:T(8,128)(2,1)S(1)}, u32[]{:S(2)}, u32[]{:S(2)}) %collective-permute-start) | collective-permute-done | bytes 36896 | tf_op jit(solution)/shard_map/ppermute | solution.py:203
  31.1 2.6 %collective-permute-done.1.y_high.ay_high = bf16[144,128]{1,0:T(8,128)(2,1)S(1)} collective-permute-done((bf16[144,128]{1,0:T(8,128)(2,1)S(1)}, bf16[144,128]{1,0:T(8,128)(2,1)S(1)}, u32[]{:S(2)}, u32[]{:S(2)}) %collective-permute-start.1) | collective-permute-done | bytes 36896 | tf_op jit(solution)/shard_map/ppermute | solution.py:203
  33.7 1.3 %collective-permute-start.2 = (bf16[320,128]{1,0:T(8,128)(2,1)S(1)}, bf16[320,128]{1,0:T(8,128)(2,1)S(1)}, u32[]{:S(2)}, u32[]{:S(2)}) collective-permute-start(bf16[320,128]{1,0:T(8,128)(2,1)S(1)} %get-tuple-element.25), channel_id=1, source_target_pairs={{0,8},{8,16},{16,24},{24,32},{32,40},{40,48},{48,56},{56,64},{64,7... | collective-permute-start | bytes 245768 | tf_op jit(solution)/shard_map/ppermute | solution.py:203
  35.0 4.3 %collective-permute-start.3 = (bf16[320,128]{1,0:T(8,128)(2,1)S(1)}, bf16[320,128]{1,0:T(8,128)(2,1)S(1)}, u32[]{:S(2)}, u32[]{:S(2)}) collective-permute-start(bf16[320,128]{1,0:T(8,128)(2,1)S(1)} %get-tuple-element.26), channel_id=1, source_target_pairs={{0,120},{8,0},{16,8},{24,16},{32,24},{40,32},{48,40},{56,48},{64,5... | collective-permute-start | bytes 245768 | tf_op jit(solution)/shard_map/ppermute | solution.py:203
  39.3 1.7 %collective-permute-done.2.x_low.ax_low = bf16[320,128]{1,0:T(8,128)(2,1)S(1)} collective-permute-done((bf16[320,128]{1,0:T(8,128)(2,1)S(1)}, bf16[320,128]{1,0:T(8,128)(2,1)S(1)}, u32[]{:S(2)}, u32[]{:S(2)}) %collective-permute-start.2) | collective-permute-done | bytes 81952 | tf_op jit(solution)/shard_map/ppermute | solution.py:203
  41.0 0.0 collective-permute-done.3.x_high.ax_high
  41.0 6.4 %increment.1 = bf16[64,128,128]{2,1,0:T(8,128)(2,1)} custom-call(f32[64,128,128]{2,1,0:T(8,128)} %get-tuple-element.20.ct, f32[64,128]{1,0:T(8,128)S(1)} %copy-done.2, bf16[320,128]{1,0:T(8,128)(2,1)S(1)} %collective-permute-done.2.x_low.ax_low, bf16[320,128]{1,0:T(8,128)(2,1)S(1)} %collective-permute-done.3.x_high.ax_high, ...), custom_call_target="tpu_custom_call" | custom-call | flops 6000000000 | tf_op jit(solution)/shard_map/increment/pallas_call | solution.py:353
  47.4 0.0 all-to-all-done.got
  47.4 0.0 copy-start.6
  47.5 0.0 copy-start.7
  47.5 0.0 copy-start.8
  47.5 0.0 copy-start.10
  47.5 0.0 copy-start.12
  47.5 0.0 copy-start.13
  47.5 6.7 %gather.1 = (bf16[1024,256]{1,0:T(8,128)(2,1)}, bf16[768,256]{1,0:T(8,128)(2,1)S(1)}) custom-call(bf16[128,8,512]{2,1,0:T(8,128)(2,1)S(1)} %all-to-all-done.got, bf16[8192,128]{1,0:T(8,128)(2,1)} %bitcast.25, bf16[8192,128]{1,0:T(8,128)(2,1)} %bitcast.26), custom_call_target="tpu_custom_call" | custom-call | flops 5000000000 | tf_op jit(solution)/shard_map/gather/pallas_call | solution.py:445
  54.2 0.0 copy-done.6
  54.2 0.0 copy-done.7
  54.3 0.0 copy-done.8
  54.3 0.0 copy-done.10
  54.3 0.0 copy-done.12
  54.3 0.0 copy-done.13
  54.3 12.2 %adjoint.1 = (f32[8192,128]{1,0:T(8,128)S(1)}, bf16[256,128]{1,0:T(8,128)(2,1)S(1)}, bf16[256,128]{1,0:T(8,128)(2,1)S(1)}, bf16[128,128]{1,0:T(8,128)(2,1)S(1)}, bf16[128,128]{1,0:T(8,128)(2,1)S(1)}) custom-call(bf16[128,8,512]{2,1,0:T(8,128)(2,1)S(1)} %all-to-all-done.got, bf16[768,256]{1,0:T(8,128)(2,1)S(1)} %get-tuple-element.28.slots, ...), custom_call_target="tpu_custom_call" | custom-call | flops 10000000000 | tf_op jit(solution)/shard_map/adjoint/pallas_call | solution.py:548
  66.5 0.0 copy-start
  66.5 2.0 %copy-done = f32[8192,128]{1,0:T(8,128)} copy-done((f32[8192,128]{1,0:T(8,128)}, f32[8192,128]{1,0:T(8,128)S(1)}, u32[]{:S(2)}) %copy-start) | copy-done | bytes 4194328
  68.5 0.6 collective-permute-start.4
  69.1 1.4 %collective-permute-start.5 = (bf16[128,128]{1,0:T(8,128)(2,1)S(1)}, bf16[128,128]{1,0:T(8,128)(2,1)S(1)}, u32[]{:S(2)}, u32[]{:S(2)}) collective-permute-start(bf16[128,128]{1,0:T(8,128)(2,1)S(1)} %get-tuple-element.31), channel_id=1, source_target_pairs={{0,7},{1,0},{2,1},{3,2},{4,3},{5,4},{6,5},{7,6},{8,15},{9,8},{10,9... | collective-permute-start | bytes 98312 | tf_op jit(solution)/shard_map/ppermute | solution.py:203
  70.5 8.8 %all-to-all-start.1 = ((bf16[128,8,256]{2,1,0:T(8,128)(2,1)}), bf16[128,8,256]{2,1,0:T(8,128)(2,1)S(1)}, u32[]{:S(2)}, u32[]{:S(2)}) async-start(bf16[128,8,256]{2,1,0:T(8,128)(2,1)} %bitcast.7), calls=%async_computation.1 | async-start | bytes 1048576 | tf_op jit(solution)/shard_map/all_to_all | solution.py:694
  79.3 0.0 collective-permute-done.4.y_low
  79.3 0.0 collective-permute-done.5.y_high
  79.4 1.4 %collective-permute-start.6 = (bf16[272,128]{1,0:T(8,128)(2,1)S(1)}, bf16[272,128]{1,0:T(8,128)(2,1)S(1)}, u32[]{:S(2)}, u32[]{:S(2)}) collective-permute-start(bf16[272,128]{1,0:T(8,128)(2,1)S(1)} %get-tuple-element.34), channel_id=1, source_target_pairs={{0,8},{8,16},{16,24},{24,32},{32,40},{40,48},{48,56},{56,64},{64,7... | collective-permute-start | bytes 208904 | tf_op jit(solution)/shard_map/ppermute | solution.py:203
  80.8 4.4 %collective-permute-start.7 = (bf16[272,128]{1,0:T(8,128)(2,1)S(1)}, bf16[272,128]{1,0:T(8,128)(2,1)S(1)}, u32[]{:S(2)}, u32[]{:S(2)}) collective-permute-start(bf16[272,128]{1,0:T(8,128)(2,1)S(1)} %get-tuple-element.35), channel_id=1, source_target_pairs={{0,120},{8,0},{16,8},{24,16},{32,24},{40,32},{48,40},{56,48},{64,5... | collective-permute-start | bytes 208904 | tf_op jit(solution)/shard_map/ppermute | solution.py:203
  85.3 0.0 copy-start.1
  85.3 2.2 %copy-done.1 = f32[8192,128]{1,0:T(8,128)S(1)} copy-done((f32[8192,128]{1,0:T(8,128)S(1)}, f32[8192,128]{1,0:T(8,128)}, u32[]{:S(2)}) %copy-start.1) | copy-done | bytes 4194328
  87.4 9.0 %interior.1.rest_3_ = f32[128,64,128]{2,1,0:T(8,128)} custom-call(f32[8192,128]{1,0:T(8,128)S(1)} %copy-done.1, f32[64,128]{1,0:T(8,128)S(1)} %copy-done.2, bf16[320,128]{1,0:T(8,128)(2,1)S(1)} %collective-permute-done.2.x_low.ax_low, bf16[320,128]{1,0:T(8,128)(2,1)S(1)} %collective-permute-done.3.x_high.ax_high, ...), custom_call_target="tpu_custom_call" | custom-call | flops 6000000000 | tf_op jit(solution)/shard_map/interior/pallas_call | solution.py:674
  96.5 0.0 copy-start.4
  96.5 0.0 copy-start.16
  96.5 0.0 collective-permute-done.6.rest_0_
  96.5 0.0 collective-permute-done.7.rest_1_
  96.5 4.3 %edges.1 = f32[128,64,128]{2,1,0:T(8,128)} custom-call(f32[8192,128]{1,0:T(8,128)S(1)} %copy-done.1, f32[64,128]{1,0:T(8,128)S(1)} %copy-done.2, bf16[320,128]{1,0:T(8,128)(2,1)S(1)} %collective-permute-done.2.x_low.ax_low, bf16[320,128]{1,0:T(8,128)(2,1)S(1)} %collective-permute-done.3.x_high.ax_high, ...), custom_call_target="tpu_custom_call", output_to_operand_aliasing={{}: (11, {})} | custom-call | flops 2000000000 | tf_op jit(solution)/shard_map/edges/pallas_call | solution.py:674
  100.8 0.0 all-to-all-done.1
  100.8 0.0 copy-done.4
  100.8 0.0 copy-done.16
  100.8 2.5 %departures.1 = f32[616,256]{1,0:T(8,128)} custom-call(bf16[1024,256]{1,0:T(8,128)(2,1)S(1)} %bitcast.12, s32[1,256]{1,0:T(1,128)S(1)} %bitcast.24, f32[616,256]{1,0:T(8,128)S(1)} %bitcast.14, bf16[128,512]{1,0:T(8,128)(2,1)S(1)} %copy-done.8, f32[1,512]{1,0:T(1,128)S(1)} %bitcast.19, bf16[512,512]{1,0:T(8,128)(2,1)S(1)} %copy-done.7, ...), custom_call_target="tpu_custom_call" | custom-call | flops 4000000000 | tf_op jit(solution)/shard_map/departures/pallas_call | solution.py:586
  (2 shorter events, 0.0 us)
Async XLA Ops:
  0.6 1.1 %copy-start.3 = (f32[256,616]{0,1:T(8,128)S(1)}, f32[256,616]{0,1:T(8,128)}, u32[]{:S(2)}) copy-start(f32[256,616]{0,1:T(8,128)} %param.19) | copy-start | bytes 1892356
  1.7 1.1 %copy-start.5 = (bf16[512,616]{0,1:T(8,128)(2,1)S(1)}, bf16[512,616]{0,1:T(8,128)(2,1)}, u32[]{:S(2)}) copy-start(bf16[512,616]{0,1:T(8,128)(2,1)} %param.25) | copy-start | bytes 1892356
  2.8 0.7 copy-start.9
  3.5 0.7 copy-start.11
  4.2 0.7 copy-start.14
  4.8 0.7 copy-start.15
  5.5 13.8 %copy-start.2 = (f32[64,128]{1,0:T(8,128)S(1)}, f32[64,128]{1,0:T(8,128)}, u32[]{:S(2)}) copy-start(f32[64,128]{1,0:T(8,128)} %spread.7) | copy-start | bytes 98308
  7.8 39.6 %all-to-all-start = ((bf16[128,8,512]{2,1,0:T(8,128)(2,1)}), bf16[128,8,512]{2,1,0:T(8,128)(2,1)S(1)}, u32[]{:S(2)}, u32[]{:S(2)}) async-start(bf16[128,8,512]{2,1,0:T(8,128)(2,1)} %bitcast.4), calls=%async_computation | async-start | bytes 2097152 | tf_op jit(solution)/shard_map/all_to_all | solution.py:694
  28.4 2.7 %collective-permute-start = (bf16[144,128]{1,0:T(8,128)(2,1)S(1)}, bf16[144,128]{1,0:T(8,128)(2,1)S(1)}, u32[]{:S(2)}, u32[]{:S(2)}) collective-permute-start(bf16[144,128]{1,0:T(8,128)(2,1)S(1)} %get-tuple-element.23), channel_id=1, source_target_pairs={{0,1},{1,2},{2,3},{3,4},{4,5},{5,6},{6,7},{7,0},{8,9},{9,10},{10,1... | collective-permute-start | bytes 110600 | tf_op jit(solution)/shard_map/ppermute | solution.py:203
  30.0 3.7 %collective-permute-start.1 = (bf16[144,128]{1,0:T(8,128)(2,1)S(1)}, bf16[144,128]{1,0:T(8,128)(2,1)S(1)}, u32[]{:S(2)}, u32[]{:S(2)}) collective-permute-start(bf16[144,128]{1,0:T(8,128)(2,1)S(1)} %get-tuple-element.24), channel_id=1, source_target_pairs={{0,7},{1,0},{2,1},{3,2},{4,3},{5,4},{6,5},{7,6},{8,15},{9,8},{10,9... | collective-permute-start | bytes 110600 | tf_op jit(solution)/shard_map/ppermute | solution.py:203
  33.7 7.3 %collective-permute-start.2 = (bf16[320,128]{1,0:T(8,128)(2,1)S(1)}, bf16[320,128]{1,0:T(8,128)(2,1)S(1)}, u32[]{:S(2)}, u32[]{:S(2)}) collective-permute-start(bf16[320,128]{1,0:T(8,128)(2,1)S(1)} %get-tuple-element.25), channel_id=1, source_target_pairs={{0,8},{8,16},{16,24},{24,32},{32,40},{40,48},{48,56},{56,64},{64,7... | collective-permute-start | bytes 245768 | tf_op jit(solution)/shard_map/ppermute | solution.py:203
  35.0 6.0 %collective-permute-start.3 = (bf16[320,128]{1,0:T(8,128)(2,1)S(1)}, bf16[320,128]{1,0:T(8,128)(2,1)S(1)}, u32[]{:S(2)}, u32[]{:S(2)}) collective-permute-start(bf16[320,128]{1,0:T(8,128)(2,1)S(1)} %get-tuple-element.26), channel_id=1, source_target_pairs={{0,120},{8,0},{16,8},{24,16},{32,24},{40,32},{48,40},{56,48},{64,5... | collective-permute-start | bytes 245768 | tf_op jit(solution)/shard_map/ppermute | solution.py:203
  47.4 6.8 %copy-start.6 = (bf16[512,616]{0,1:T(8,128)(2,1)S(1)}, bf16[512,616]{0,1:T(8,128)(2,1)}, u32[]{:S(2)}) copy-start(bf16[512,616]{0,1:T(8,128)(2,1)} %param.25) | copy-start | bytes 1892356
  47.5 6.8 %copy-start.7 = (bf16[512,512]{1,0:T(8,128)(2,1)S(1)}, bf16[512,512]{1,0:T(8,128)(2,1)}, u32[]{:S(2)}) copy-start(bf16[512,512]{1,0:T(8,128)(2,1)} %w_second.3) | copy-start | bytes 1572868
  47.5 6.8 %copy-start.8 = (bf16[128,512]{1,0:T(8,128)(2,1)S(1)}, bf16[128,512]{1,0:T(8,128)(2,1)}, u32[]{:S(2)}) copy-start(bf16[128,512]{1,0:T(8,128)(2,1)} %w_first.3) | copy-start | bytes 393220
  47.5 6.8 %copy-start.10 = (f32[616]{0:T(1024)S(1)}, f32[616]{0:T(1024)}, u32[]{:S(2)}) copy-start(f32[616]{0:T(1024)} %ivar.5) | copy-start | bytes 7396
  47.5 6.8 %copy-start.12 = (f32[512]{0:T(512)S(1)}, f32[512]{0:T(512)}, u32[]{:S(2)}) copy-start(f32[512]{0:T(512)} %param.22) | copy-start | bytes 6148
  47.5 6.8 %copy-start.13 = (f32[512]{0:T(512)S(1)}, f32[512]{0:T(512)}, u32[]{:S(2)}) copy-start(f32[512]{0:T(512)} %param.24) | copy-start | bytes 6148
  66.5 2.0 %copy-start = (f32[8192,128]{1,0:T(8,128)}, f32[8192,128]{1,0:T(8,128)S(1)}, u32[]{:S(2)}) copy-start(f32[8192,128]{1,0:T(8,128)S(1)} %get-tuple-element.29.acc) | copy-start | bytes 12582916
  68.5 10.8 %collective-permute-start.4 = (bf16[128,128]{1,0:T(8,128)(2,1)S(1)}, bf16[128,128]{1,0:T(8,128)(2,1)S(1)}, u32[]{:S(2)}, u32[]{:S(2)}) collective-permute-start(bf16[128,128]{1,0:T(8,128)(2,1)S(1)} %get-tuple-element.30), channel_id=1, source_target_pairs={{0,1},{1,2},{2,3},{3,4},{4,5},{5,6},{6,7},{7,0},{8,9},{9,10},{10,1... | collective-permute-start | bytes 98312 | tf_op jit(solution)/shard_map/ppermute | solution.py:203
  69.1 10.2 %collective-permute-start.5 = (bf16[128,128]{1,0:T(8,128)(2,1)S(1)}, bf16[128,128]{1,0:T(8,128)(2,1)S(1)}, u32[]{:S(2)}, u32[]{:S(2)}) collective-permute-start(bf16[128,128]{1,0:T(8,128)(2,1)S(1)} %get-tuple-element.31), channel_id=1, source_target_pairs={{0,7},{1,0},{2,1},{3,2},{4,3},{5,4},{6,5},{7,6},{8,15},{9,8},{10,9... | collective-permute-start | bytes 98312 | tf_op jit(solution)/shard_map/ppermute | solution.py:203
  70.5 30.3 %all-to-all-start.1 = ((bf16[128,8,256]{2,1,0:T(8,128)(2,1)}), bf16[128,8,256]{2,1,0:T(8,128)(2,1)S(1)}, u32[]{:S(2)}, u32[]{:S(2)}) async-start(bf16[128,8,256]{2,1,0:T(8,128)(2,1)} %bitcast.7), calls=%async_computation.1 | async-start | bytes 1048576 | tf_op jit(solution)/shard_map/all_to_all | solution.py:694
  79.4 17.1 %collective-permute-start.6 = (bf16[272,128]{1,0:T(8,128)(2,1)S(1)}, bf16[272,128]{1,0:T(8,128)(2,1)S(1)}, u32[]{:S(2)}, u32[]{:S(2)}) collective-permute-start(bf16[272,128]{1,0:T(8,128)(2,1)S(1)} %get-tuple-element.34), channel_id=1, source_target_pairs={{0,8},{8,16},{16,24},{24,32},{32,40},{40,48},{48,56},{56,64},{64,7... | collective-permute-start | bytes 208904 | tf_op jit(solution)/shard_map/ppermute | solution.py:203
  80.8 15.7 %collective-permute-start.7 = (bf16[272,128]{1,0:T(8,128)(2,1)S(1)}, bf16[272,128]{1,0:T(8,128)(2,1)S(1)}, u32[]{:S(2)}, u32[]{:S(2)}) collective-permute-start(bf16[272,128]{1,0:T(8,128)(2,1)S(1)} %get-tuple-element.35), channel_id=1, source_target_pairs={{0,120},{8,0},{16,8},{24,16},{32,24},{40,32},{48,40},{56,48},{64,5... | collective-permute-start | bytes 208904 | tf_op jit(solution)/shard_map/ppermute | solution.py:203
  85.3 2.2 %copy-start.1 = (f32[8192,128]{1,0:T(8,128)S(1)}, f32[8192,128]{1,0:T(8,128)}, u32[]{:S(2)}) copy-start(f32[8192,128]{1,0:T(8,128)} %copy-done) | copy-start | bytes 12582916
  96.5 4.4 %copy-start.4 = (f32[256,616]{0,1:T(8,128)S(1)}, f32[256,616]{0,1:T(8,128)}, u32[]{:S(2)}) copy-start(f32[256,616]{0,1:T(8,128)} %param.19) | copy-start | bytes 1892356
  96.5 4.4 %copy-start.16 = (s32[256,1]{0,1:T(1,128)S(1)}, s32[256,1]{0,1:T(1,128)}, u32[]{:S(2)}) copy-start(s32[256,1]{0,1:T(1,128)} %param.16) | copy-start | bytes 3076

commit v4 on v3

--- a/solution.py
+++ b/solution.py
@@ -1,5 +1,3 @@
-import functools
-
 import jax
 import jax.numpy as jnp
 from jax import lax
@@ -24,6 +22,7 @@
 PX = BX + 4
 PY = BY + 16
 CHUNK = 8
+TALL = 16
 
 
 def params(mib, **extra):
@@ -112,16 +111,16 @@
         compiler_params=params(12),
         cost_estimate=cost(4),
         name="requests",
-    )(holder, anchor, frac, innov, ivar, w_third)
-
-
-def columns_kernel(control, background, spread, ct, bgt, x_up, x_down, y_up, y_down, wide, planes):
+    )(*map(in_hbm, (holder, anchor, frac, innov, ivar, w_third)))
+
+
+def columns_kernel(control, background, spread, field, bgt, x_up, x_down, y_up, y_down, wide, planes):
     step = pl.program_id(0)
     pair = eye_pair()
-    wide[...] = background[...].astype(F32).reshape(LEV * CHUNK, BY)
-    flat = control.reshape(LEV * CHUNK, BY)
-    for i in range(CHUNK):
-        here = pl.ds(i, LEV, stride=CHUNK)
+    wide[...] = background[...].astype(F32).reshape(LEV * TALL, BY)
+    flat = control.reshape(LEV * TALL, BY)
+    for i in range(TALL):
+        here = pl.ds(i, LEV, stride=TALL)
         high, low = split_two(flat[here, :])
         back = wide[here, :].astype(BF16)
         both = jnp.concatenate(
@@ -132,20 +131,20 @@
             axis=0,
         )
         turned = nt(pair, both)
-        ct[i] = turned[:, :LEV]
+        field[step * TALL + i + 2, 8 : 8 + BY, :] = turned[:, :LEV]
         bgt[i] = turned[:, LEV:].astype(BF16)
         for n, y in enumerate((0, 1, BY - 2, BY - 1)):
-            planes[n, pl.ds(step * CHUNK + i, 1), :] = turned[y : y + 1, :LEV]
+            planes[n, pl.ds(step * TALL + i, 1), :] = turned[y : y + 1, :LEV]
 
     @pl.when(step == 0)
     def _():
-        x_down[:BY, :] = ct[0].astype(BF16)
-        x_down[BY : 2 * BY, :] = ct[1].astype(BF16)
+        x_down[:BY, :] = field[2, 8 : 8 + BY, :].astype(BF16)
+        x_down[BY : 2 * BY, :] = field[3, 8 : 8 + BY, :].astype(BF16)
 
     @pl.when(step == pl.num_programs(0) - 1)
     def _():
-        x_up[:BY, :] = ct[CHUNK - 2].astype(BF16)
-        x_up[BY : 2 * BY, :] = ct[CHUNK - 1].astype(BF16)
+        x_up[:BY, :] = field[BX, 8 : 8 + BY, :].astype(BF16)
+        x_up[BY : 2 * BY, :] = field[BX + 1, 8 : 8 + BY, :].astype(BF16)
         s = spread[...]
         turned = jnp.transpose(jnp.concatenate([s, s], axis=0))
 
@@ -166,22 +165,22 @@
     keep = lambda i: (0, 0)
     return pl.pallas_call(
         columns_kernel,
-        grid=(BX // CHUNK,),
+        grid=(BX // TALL,),
         in_specs=[
-            pl.BlockSpec((LEV, CHUNK, BY), lambda i: (0, i, 0)),
-            pl.BlockSpec((LEV, CHUNK, BY), lambda i: (0, i, 0)),
+            pl.BlockSpec((LEV, TALL, BY), lambda i: (0, i, 0)),
+            pl.BlockSpec((LEV, TALL, BY), lambda i: (0, i, 0)),
             pl.BlockSpec((BX, BY), keep),
         ],
         out_specs=[
-            pl.BlockSpec((CHUNK, BY, LEV), lambda i: (i, 0, 0)),
-            pl.BlockSpec((CHUNK, BY, LEV), lambda i: (i, 0, 0)),
+            pl.BlockSpec(memory_space=pltpu.VMEM),
+            pl.BlockSpec((TALL, BY, LEV), lambda i: (i, 0, 0)),
             pl.BlockSpec((2 * BY + 16, LEV), keep),
             pl.BlockSpec((2 * BY + 16, LEV), keep),
             pl.BlockSpec((2 * BX + 16, LEV), keep),
             pl.BlockSpec((2 * BX + 16, LEV), keep),
         ],
         out_shape=[
-            pltpu.HBM((BX, BY, LEV), F32),
+            pltpu.VMEM((PX, PY, LEV), F32),
             pltpu.HBM((BX, BY, LEV), BF16),
             jax.ShapeDtypeStruct((2 * BY + 16, LEV), BF16),
             jax.ShapeDtypeStruct((2 * BY + 16, LEV), BF16),
@@ -189,10 +188,10 @@
             jax.ShapeDtypeStruct((2 * BX + 16, LEV), BF16),
         ],
         scratch_shapes=[
-            pltpu.VMEM((LEV * CHUNK, BY), F32),
+            pltpu.VMEM((LEV * TALL, BY), F32),
             pltpu.VMEM((4, BX, LEV), F32),
         ],
-        compiler_params=params(10, dimension_semantics=("arbitrary",)),
+        compiler_params=params(16, dimension_semantics=("arbitrary",)),
         cost_estimate=cost(6),
         name="columns",
     )(in_hbm(control), in_hbm(background), spread)
@@ -273,14 +272,20 @@
         field[x, 8 + BY : 9 + BY, :] = pair[1:2]
 
 
-def coefficients(coef, spread, x_low, x_high, y_low, y_high, rows):
-    square = jnp.concatenate(
-        [joined(x_low, 2 * BY), spread[...], joined(x_high, 2 * BY), jnp.zeros((BY - PX, BY), F32)],
-        axis=0,
+def main_coefficients(coef, spread):
+    square = jnp.concatenate([spread[...], jnp.zeros((BY - BX, BY), F32)], axis=0)
+    turned = jnp.transpose(square)
+    for x in range(BX):
+        coef[x + 2, 8 : 8 + BY, :] = lanes(turned[:, x : x + 1])
+
+
+def rim_coefficients(coef, x_low, x_high, y_low, y_high):
+    ends = jnp.concatenate(
+        [joined(x_low, 2 * BY), joined(x_high, 2 * BY), jnp.zeros((BY - 4, BY), F32)], axis=0
     )
-    turned = jnp.transpose(square)
-    for x in rows:
-        coef[x, 8 : 8 + BY, :] = lanes(turned[:, x : x + 1])
+    ends = jnp.transpose(ends)
+    for n, x in enumerate((0, 1, BX + 2, BX + 3)):
+        coef[x, 8 : 8 + BY, :] = lanes(ends[:, n : n + 1])
     sides = jnp.concatenate(
         [joined(y_low, 2 * BX), joined(y_high, 2 * BX), jnp.zeros((BY - 4, BY), F32)], axis=0
     )
@@ -295,6 +300,20 @@
         coef[x, 8 + BY : 9 + BY, :] = lanes(right[0:1, lane : lane + 1])
 
 
+def spread_kernel(spread, coef):
+    main_coefficients(coef, spread)
+
+
+def over_lanes(spread):
+    return pl.pallas_call(
+        spread_kernel,
+        out_shape=pltpu.VMEM((PX, PY, LEV), F32),
+        compiler_params=params(2),
+        cost_estimate=cost(1),
+        name="spread",
+    )(spread)
+
+
 def joined(rows, at):
     block = rows[at : at + 16, :].astype(F32)
     return block[0:2] + block[2:4]
@@ -304,20 +323,13 @@
 
 
 def increment_kernel(
-    ct, spread, x_low, x_high, y_low, y_high, inc, coef, field, first, done, came, went
+    _field, _coef, x_low, x_high, y_low, y_high, inc, field, coef, first, done, went
 ):
-    def bring(part):
-        at = pl.ds(part * CHUNK, CHUNK)
-        to = field.at[pl.ds(2 + part * CHUNK, CHUNK), pl.ds(8, BY)]
-        return pltpu.make_async_copy(ct.at[at], to, came.at[part])
-
     def leave(part):
         at = pl.ds(part * CHUNK, CHUNK)
         return pltpu.make_async_copy(done.at[at], inc.at[at], went.at[part])
 
-    for part in range(PARTS):
-        bring(part).start()
-    coefficients(coef, spread, x_low, x_high, y_low, y_high, range(PX))
+    rim_coefficients(coef, x_low, x_high, y_low, y_high)
     fill_x(field, x_low, x_high, 2 * BY + 16)
     fill_y(field, y_low, y_high)
 
@@ -326,10 +338,7 @@
         first[x, 8 : 8 + BY, :] = middle + coef[x, 8 : 8 + BY, :] * laplace(field, x, 8, BY)
         return carry
 
-    for part in range(PARTS):
-        bring(part).wait()
-        last = PX - 1 if part == PARTS - 1 else 1 + CHUNK * (part + 1)
-        lax.fori_loop(1 + CHUNK * part, last, sweep_one, 0)
+    lax.fori_loop(1, PX - 1, sweep_one, 0)
     for y in (7, 8 + BY):
         moved = plane(field, 2, y, BX) + plane(coef, 2, y, BX) * plane_laplace(field, y)
         set_plane(first, 2, y, BX, moved)
@@ -347,24 +356,27 @@
         leave(part).wait()
 
 
-def increments(ct, spread, rims):
-    any_space = pl.BlockSpec(memory_space=pltpu.HBM)
+def increments(field, coef, rims):
     whole = pl.BlockSpec(memory_space=pltpu.VMEM)
     return pl.pallas_call(
         increment_kernel,
-        in_specs=[any_space] + [whole] * 5,
-        out_specs=any_space,
-        out_shape=pltpu.HBM((BX, BY, LEV), BF16),
-        scratch_shapes=[pltpu.VMEM((PX, PY, LEV), F32)] * 3
-        + [
+        in_specs=[whole] * 6,
+        out_specs=[pl.BlockSpec(memory_space=pltpu.HBM), whole, whole],
+        out_shape=[
+            pltpu.HBM((BX, BY, LEV), BF16),
+            pltpu.VMEM((PX, PY, LEV), F32),
+            pltpu.VMEM((PX, PY, LEV), F32),
+        ],
+        input_output_aliases={0: 1, 1: 2},
+        scratch_shapes=[
+            pltpu.VMEM((PX, PY, LEV), F32),
             pltpu.VMEM((BX, BY, LEV), BF16),
             pltpu.SemaphoreType.DMA((PARTS,)),
-            pltpu.SemaphoreType.DMA((PARTS,)),
-        ],
-        compiler_params=params(27),
+        ],
+        compiler_params=params(12),
         cost_estimate=cost(6),
         name="increment",
-    )(in_hbm(ct), spread, *rims)
+    )(in_vmem(field), in_vmem(coef), *rims)[0]
 
 
 def decode(rows):
@@ -482,7 +494,7 @@
     return d_one, d_two, t_two
 
 
-BLOCK = 256
+BLOCK = 768
 
 
 def adjoint_kernel(
@@ -563,7 +575,7 @@
             pltpu.VMEM((2 * SLOTS, LEV), F32),
             pltpu.VMEM((2 * SLOTS, LEV), F32),
         ],
-        compiler_params=params(24),
+        compiler_params=params(32),
         cost_estimate=cost(10),
         name="adjoint",
     )(got, slots, w_first, b_first, w_second, b_second, w_third, ivar)
@@ -592,102 +604,214 @@
     )(reply, holder, innov, w_first, b_first, w_second, b_second, w_third, ivar)
 
 
-def gradient_kernel(edge, acc, spread, ax_low, ax_high, ay_low, ay_high, y_low, y_high, *rest):
-    if edge:
-        x_low, x_high, control, _, out, coef, field, grown, second = rest
-    else:
-        control, out, coef, field, grown, second = rest
-    step = pl.program_id(0)
-    first = step * (PARTS - 1) * CHUNK if edge else (step + 1) * CHUNK
-
-    @pl.when(step == 0)
-    def _():
-        rows = [*range(12), *range(PX - 12, PX)] if edge else range(CHUNK, PX - CHUNK)
-        coefficients(coef, spread, ax_low, ax_high, ay_low, ay_high, rows)
-        fill_y(field, y_low, y_high)
-        if edge:
-            fill_x(field, x_low, x_high, 2 * BY)
-
-    def fill(x, carry):
-        field[x, 8 : 8 + BY, :] = acc[pl.ds(pl.multiple_of((x - 2) * BY, BY), BY), :]
+def ready_kernel(
+    acc, spread, ax_low, ax_high, ay_low, ay_high, control,
+    coef, grown, scaled, held, low, high, field, came,
+):
+    copies = [
+        pltpu.make_async_copy(control.at[:, pl.ds(at, to.shape[1])], to, came.at[n])
+        for n, (to, at) in enumerate(((held, CHUNK), (low, 0), (high, BX - CHUNK)))
+    ]
+    for copy in copies:
+        copy.start()
+    main_coefficients(coef, spread)
+    rim_coefficients(coef, ax_low, ax_high, ay_low, ay_high)
+    for x in (1, BX + 2):
+        field[x] = jnp.zeros((PY, LEV), F32)
+    for y in (7, 8 + BY):
+        set_plane(field, 2, y, BX, jnp.zeros((BX, LEV), F32))
+
+    def scale(x, carry):
+        at = pl.ds(pl.multiple_of((x - 2) * BY, BY), BY)
+        field[x, 8 : 8 + BY, :] = coef[x, 8 : 8 + BY, :] * acc[at, :]
         return carry
 
-    if edge:
-        start, stop = jnp.where(step == 0, 2, first), jnp.where(step == 0, 12, PX - 2)
-        lax.fori_loop(start, stop, fill, 0)
-    else:
-        lax.fori_loop(jnp.where(step == 0, first, first + 4), first + CHUNK + 4, fill, 0)
-    span = CHUNK + 4
-
-    def scale(i, carry):
-        grown[i] = field[first + i] * coef[first + i]
+    lax.fori_loop(2, PX - 2, scale, 0)
+
+    def sweep_one(x, carry):
+        at = pl.ds(pl.multiple_of((x - 2) * BY, BY), BY)
+        value = acc[at, :] + laplace(field, x, 8, BY)
+        grown[x - 2] = value
+        scaled[x, 8 : 8 + BY, :] = coef[x, 8 : 8 + BY, :] * value
         return carry
 
-    lax.fori_loop(0, span, scale, 0)
-
-    def sweep_one(i, carry):
-        value = field[first + i, 8 : 8 + BY, :] + laplace(grown, i, 8, BY)
-        second[1, i, 8 : 8 + BY, :] = value
-        second[0, i, 8 : 8 + BY, :] = coef[first + i, 8 : 8 + BY, :] * value
-        return carry
-
-    lax.fori_loop(1, span - 1, sweep_one, 0)
-
-    def column(ref, offset, y):
-        flat = ref.reshape(ref.shape[0] * PY, LEV)
-        return flat[pl.ds((first + offset) * PY + y, CHUNK, stride=PY), :]
-
-    def local(ref, offset, y):
-        flat = ref.reshape(ref.shape[0] * PY, LEV)
-        return flat[pl.ds(offset * PY + y, CHUNK, stride=PY), :]
-
-    scaled = second.at[0]
-    flat_scaled = scaled.reshape(span * PY, LEV)
-    for y in (7, 8 + BY):
-        total = local(grown, 3, y) + local(grown, 1, y)
-        total = total + local(grown, 2, y + 1) + local(grown, 2, y - 1)
-        value = column(field, 2, y) + (total - 4.0 * local(grown, 2, y))
-        flat_scaled[pl.ds(2 * PY + y, CHUNK, stride=PY), :] = column(coef, 2, y) * value
+    lax.fori_loop(2, PX - 2, sweep_one, 0)
+    for copy in copies:
+        copy.wait()
+
+
+INNER = BX - 2 * CHUNK
+
+
+def ready(acc, spread, before, control):
+    whole = pl.BlockSpec(memory_space=pltpu.VMEM)
+    return pl.pallas_call(
+        ready_kernel,
+        in_specs=[whole] * 6 + [pl.BlockSpec(memory_space=pltpu.HBM)],
+        out_specs=[whole] * 6,
+        out_shape=[
+            pltpu.VMEM((PX, PY, LEV), F32),
+            pltpu.VMEM((BX, BY, LEV), F32),
+            pltpu.VMEM((PX, PY, LEV), F32),
+            pltpu.VMEM((LEV, INNER, BY), F32),
+            pltpu.VMEM((LEV, CHUNK, BY), F32),
+            pltpu.VMEM((LEV, CHUNK, BY), F32),
+        ],
+        scratch_shapes=[pltpu.VMEM((PX, PY, LEV), F32), pltpu.SemaphoreType.DMA((3,))],
+        compiler_params=params(8),
+        cost_estimate=cost(3),
+        name="ready",
+    )(in_vmem(acc), spread, *before, in_hbm(control))
+
+
+def finish_rows(grown, scaled, held, first, count, offset, pair):
+    flat = held.reshape(LEV * held.shape[1], BY)
+    for i in range(count):
+        x = first + i
+        value = grown[x] + laplace(scaled, x + 2, 8, BY)
+        high, low = split_two(value)
+        turned = nt(pair, jnp.concatenate([high, low], axis=1))
+        here = pl.ds(offset + i, LEV, stride=held.shape[1])
+        flat[here, :] = turned + flat[here, :]
+
+
+def interior_kernel(
+    acc, coef, y_low, y_high, _held, _grown, _scaled, out, held, grown, scaled, went
+):
+    edge = iota((BX, LEV), 0)
+    for rows, near, far, side, inner in (
+        (y_low, 1, 0, 7, 8),
+        (y_high, 0, 1, 8 + BY, 7 + BY),
+    ):
+        here = rows[near * BX : (near + 1) * BX, :].astype(F32)
+        there = rows[far * BX : (far + 1) * BX, :].astype(F32)
+        weight = plane(coef, 2, side, BX)
+        mine = weight * here
+        over = side + (-1 if side < 8 else 1)
+        total = jnp.where(edge == BX - 1, 0.0, pltpu.roll(mine, BX - 1, 0))
+        total = total + jnp.where(edge == 0, 0.0, pltpu.roll(mine, 1, 0))
+        touching = acc[pl.ds(inner - 8, BX, stride=BY), :]
+        inside = plane(coef, 2, inner, BX)
+        total = total + inside * touching + plane(coef, 2, over, BX) * there
+        set_plane(scaled, 2, side, BX, weight * (here + (total - 4.0 * mine)))
+        flat = grown.reshape(CELLS, LEV)
+        at = pl.ds(inner - 8, BX, stride=BY)
+        fixed = flat[at, :] + mine
+        flat[at, :] = fixed
+        set_plane(scaled, 2, inner, BX, inside * fixed)
     pair = eye_pair()
-    flat_out = out.reshape(LEV * CHUNK, BY)
-    flat_control = control.reshape(LEV * CHUNK, BY)
-    for i in range(CHUNK):
-        value = second[1, 2 + i, 8 : 8 + BY, :] + laplace(scaled, 2 + i, 8, BY)
-        high_part, low_part = split_two(value)
-        turned = nt(pair, jnp.concatenate([high_part, low_part], axis=1))
-        here = pl.ds(i, LEV, stride=CHUNK)
-        flat_out[here, :] = turned + flat_control[here, :]
-
-
-def gradient_of(acc, spread, before, rims, control, so_far=None):
-    edge = so_far is not None
+
+    def leave(part):
+        return pltpu.make_async_copy(
+            held.at[:, pl.ds(part * TALL, TALL)],
+            out.at[:, pl.ds(CHUNK + part * TALL, TALL)],
+            went.at[part],
+        )
+
+    for part in range(INNER // TALL):
+        first = part * TALL
+
+        def some(step, carry):
+            flat = held.reshape(LEV * INNER, BY)
+            for i in range(4):
+                at = first + step * 4 + i
+                value = grown[CHUNK + at] + laplace(scaled, CHUNK + at + 2, 8, BY)
+                high, low = split_two(value)
+                turned = nt(pair, jnp.concatenate([high, low], axis=1))
+                here = pl.ds(at, LEV, stride=INNER)
+                flat[here, :] = turned + flat[here, :]
+            return carry
+
+        lax.fori_loop(0, TALL // 4, some, 0)
+        leave(part).start()
+    for part in range(INNER // TALL):
+        leave(part).wait()
+
+
+def interior(acc, coef, rims, held, grown, scaled):
     whole = pl.BlockSpec(memory_space=pltpu.VMEM)
-    if edge:
-        block = pl.BlockSpec((LEV, CHUNK, BY), lambda i: (0, i * (PARTS - 1), 0))
-    else:
-        block = pl.BlockSpec((LEV, CHUNK, BY), lambda i: (0, i + 1, 0))
-    operands = [in_vmem(acc), spread, *before, *rims, in_hbm(control)]
-    specs = [whole] * (len(operands) - 1) + [block]
-    if edge:
-        operands.append(in_hbm(so_far))
-        specs.append(pl.BlockSpec(memory_space=pltpu.HBM))
-    return pl.pallas_call(
-        functools.partial(gradient_kernel, edge),
-        grid=(2 if edge else PARTS - 2,),
-        in_specs=specs,
-        out_specs=block,
-        out_shape=pltpu.HBM((LEV, BX, BY), F32),
-        input_output_aliases={len(operands) - 1: 0} if edge else {},
-        scratch_shapes=[
+    hbm = pl.BlockSpec(memory_space=pltpu.HBM)
+    return pl.pallas_call(
+        interior_kernel,
+        in_specs=[whole] * 7,
+        out_specs=[hbm] + [whole] * 3,
+        out_shape=[
+            pltpu.HBM((LEV, BX, BY), F32),
+            pltpu.VMEM((LEV, INNER, BY), F32),
+            pltpu.VMEM((BX, BY, LEV), F32),
             pltpu.VMEM((PX, PY, LEV), F32),
+        ],
+        input_output_aliases={4: 1, 5: 2, 6: 3},
+        scratch_shapes=[pltpu.SemaphoreType.DMA((INNER // TALL,))],
+        compiler_params=params(4),
+        cost_estimate=cost(5),
+        name="interior",
+    )(in_vmem(acc), in_vmem(coef), *rims, in_vmem(held), in_vmem(grown), in_vmem(scaled))
+
+
+def edges_kernel(
+    acc, coef, x_low, x_high, _out, _grown, _scaled, _low, _high,
+    out, grown, scaled, low, high, line, went,
+):
+    held = (low, high)
+
+    def leave(n):
+        at = pl.ds(n * (BX - CHUNK), CHUNK)
+        return pltpu.make_async_copy(held[n], out.at[:, at], went.at[n])
+
+    main = pl.ds(8, BY)
+    for rows, near, side, inner in ((x_low, 1, 1, 2), (x_high, 0, BX + 2, BX + 1)):
+        here = rows[near * BY : (near + 1) * BY, :].astype(F32)
+        there = rows[(1 - near) * BY : (2 - near) * BY, :].astype(F32)
+        pair = rows[2 * BY : 2 * BY + 16, :].astype(F32)
+        weight = coef[side, main, :]
+        mine = weight * here
+        line[main, :] = mine
+        for n, y in enumerate((7, 8 + BY)):
+            corner = coef[side, y : y + 1, :] * pair[n : n + 1]
+            line[y : y + 1, :] = corner
+            scaled[inner, y : y + 1, :] = (
+                scaled[inner, y : y + 1, :] + coef[inner, y : y + 1, :] * corner
+            )
+        inside = coef[inner, main, :]
+        total = inside * acc[(inner - 2) * BY : (inner - 1) * BY, :]
+        total = total + coef[side + (-1 if side < 8 else 1), main, :] * there
+        total = total + line[9 : 9 + BY, :] + line[7 : 7 + BY, :]
+        scaled[side, main, :] = weight * (here + (total - 4.0 * mine))
+        fixed = grown[inner - 2] + mine
+        grown[inner - 2] = fixed
+        scaled[inner, main, :] = inside * fixed
+    pair = eye_pair()
+    for n in range(2):
+        finish_rows(grown, scaled, held[n], n * (BX - CHUNK), CHUNK, 0, pair)
+        leave(n).start()
+    for n in range(2):
+        leave(n).wait()
+
+
+def edges(acc, coef, rims, so_far, grown, scaled, low, high):
+    whole = pl.BlockSpec(memory_space=pltpu.VMEM)
+    hbm = pl.BlockSpec(memory_space=pltpu.HBM)
+    return pl.pallas_call(
+        edges_kernel,
+        in_specs=[whole] * 4 + [hbm] + [whole] * 4,
+        out_specs=[hbm] + [whole] * 4,
+        out_shape=[
+            pltpu.HBM((LEV, BX, BY), F32),
+            pltpu.VMEM((BX, BY, LEV), F32),
             pltpu.VMEM((PX, PY, LEV), F32),
-            pltpu.VMEM((CHUNK + 4, PY, LEV), F32),
-            pltpu.VMEM((2, CHUNK + 4, PY, LEV), F32),
-        ],
-        compiler_params=params(20, dimension_semantics=("arbitrary",)),
-        cost_estimate=cost(2 if edge else 6),
-        name="edges" if edge else "interior",
-    )(*operands)
+            pltpu.VMEM((LEV, CHUNK, BY), F32),
+            pltpu.VMEM((LEV, CHUNK, BY), F32),
+        ],
+        input_output_aliases={4: 0, 5: 1, 6: 2, 7: 3, 8: 4},
+        scratch_shapes=[pltpu.VMEM((PY, LEV), F32), pltpu.SemaphoreType.DMA((2,))],
+        compiler_params=params(4),
+        cost_estimate=cost(2),
+        name="edges",
+    )(
+        in_vmem(acc), in_vmem(coef), *rims, in_hbm(so_far),
+        in_vmem(grown), in_vmem(scaled), in_vmem(low), in_vmem(high),
+    )[0]
 
 
 def exchange(array):
@@ -714,24 +838,28 @@
     holder = obs_holder.reshape(1, OWN)
     innov = innovation.T
     w_last = w_third.T
-    ct, bgt, x_up, x_down, y_up, y_down = to_columns(control, background, spread)
+    asked = requests(holder, obs_anchor.reshape(1, OWN), obs_frac, innov, inverse_var, w_last)
+    got = exchange(asked.reshape(DEV, ROWS, HID))
+    field, bgt, x_up, x_down, y_up, y_down = to_columns(control, background, spread)
     ay_low, ay_high = shift(y_up, "obs", 1), shift(y_down, "obs", -1)
-    asked = requests(holder, obs_anchor.reshape(1, OWN), obs_frac, innov, inverse_var, w_last)
+    wide = over_lanes(spread)
     x_up, x_down = compose(x_up, x_down, ay_low, ay_high)
     ax_low, ax_high = shift(x_up, "tile", 1), shift(x_down, "tile", -1)
     before = (ax_low, ax_high, ay_low, ay_high)
-    got = exchange(asked.reshape(DEV, ROWS, HID))
-    inct = increments(ct, spread, before)
+    inct = increments(field, wide, before)
     reply, slots = gathered(got, bgt.reshape(CELLS, LEV), inct.reshape(CELLS, LEV))
     reply = exchange(reply.reshape(DEV, ROWS, 2 * LEV))
     acc, x_up, x_down, y_up, y_down = adjoint(
         got, slots, w_first, b_one, w_second, b_two, w_last, inverse_var
     )
     y_low, y_high = shift(y_up, "obs", 1), shift(y_down, "obs", -1)
+    coef, grown, scaled, *held = ready(acc, spread, before, control)
     x_up, x_down = compose(x_up, x_down, y_low, y_high)
     x_low, x_high = shift(x_up, "tile", 1), shift(x_down, "tile", -1)
-    gradient = gradient_of(acc, spread, before, (y_low, y_high), control)
-    gradient = gradient_of(acc, spread, before, (y_low, y_high, x_low, x_high), control, gradient)
+    gradient, _, grown, scaled = interior(acc, coef, (y_low, y_high), held[0], grown, scaled)
+    gradient = edges(
+        acc, coef, (x_low, x_high), gradient, grown, scaled, held[1], held[2]
+    )
     departures = departures_of(
         reply.reshape(DEV * ROWS, 2 * LEV), holder, innov,
         w_first, b_one, w_second, b_two, w_last, inverse_var,

time: 104 us -> 94.3 us (0.907)
  local copies, waits for them, and re-layouts: 9.12 us -> 4.25 us
  Pallas kernels: 52.6 us -> 47.8 us
    unnamed x34 -> x24, local copies, waits for them, and re-layouts: 9.12 us -> 4.25 us
    pallas_call x4 -> x6, Pallas kernels: 28.8 us -> 24.5 us  [the longest x1 6.94 us: to_columns(): pl.pallas_call(columns_kernel, grid=(BX // TALL,), in_specs=[pl.BlockSpec...]
    pallas_call x1, Pallas kernels: 12.2 us -> 10.4 us  [adjoint(): pl.pallas_call(adjoint_kernel, out_shape=[pltpu.VMEM((CELLS, LEV), F32),...]
    pallas_call x1, Pallas kernels: 2.3 us -> 3.59 us  [requests(): pl.pallas_call(request_kernel, out_shape=jax.ShapeDtypeStruct((DEV * ROWS...]
  transfers between devices with their start and end apart: 10 -> 10, of which waited for: 3 -> 3; matrix products, arithmetic and copies ran while one was open for 0% -> 0% of each run, Pallas kernels for 28% -> 26%
where the time goes in v4:
time: 94.3 us; the launch traced here: 94 us
  Pallas kernels  47.8 us (51%)
  starting transfers between devices  35.7 us (38%)
  waiting for transfers between devices  5.39 us (6%)
  local copies, waits for them, and re-layouts  4.25 us (5%)
    all_to_all x2, starting transfers between devices, exchange(): lax.all_to_all(array, ('tile', 'obs'), split_axis=0, concat_axis=0, tiled...  20.3 us
    ppermute x8, starting transfers between devices, shift(): lax.ppermute(array, axis, [(i, (i + by) % count) for i in range(count)])  15.3 us
    pallas_call x1, Pallas kernels, adjoint(): pl.pallas_call(adjoint_kernel, out_shape=[pltpu.VMEM((CELLS, LEV), F32),...  10.4 us
    pallas_call x1, Pallas kernels, to_columns(): pl.pallas_call(columns_kernel, grid=(BX // TALL,), in_specs=[pl.BlockSpec...  6.94 us
    pallas_call x1, Pallas kernels, gathered(): pl.pallas_call(gather_kernel, grid=(1,), in_specs=[pl.BlockSpec((DEV, ROW...  6.71 us
    ppermute x8, waiting for transfers between devices, shift(): lax.ppermute(array, axis, [(i, (i + by) % count) for i in range(count)])  5.39 us
    pallas_call x1, Pallas kernels, increments(): pl.pallas_call(increment_kernel, in_specs=[whole] * 6, out_specs=[pl.Bloc...  5.18 us
    pallas_call x1, Pallas kernels, interior(): pl.pallas_call(interior_kernel, in_specs=[whole] * 7, out_specs=[hbm] + [...  5.15 us
  transfers between devices with their start and end apart: 10, of which 3 were waited for; matrix products, arithmetic and copies ran while one was open for 0% of the time, Pallas kernels for 26%

profile of v4, /device:TPU:1, one launch (start us, length us, event | category | flops | bytes accessed | tf_op | source)
XLA Modules:
  0.0 94.0 jit_solution(11219992743666329949)
XLA Ops:
  0.6 0.0 copy-start.3
  0.6 3.6 %requests.1 = bf16[1024,512]{1,0:T(8,128)(2,1)} custom-call(s32[1,256]{1,0:T(1,128)} %bitcast.22, s32[1,256]{1,0:T(1,128)} %bitcast.24, f32[2,256]{1,0:T(2,128)} %frac.1, f32[616,256]{1,0:T(8,128)} %bitcast.13, f32[616]{0:T(1024)} %ivar.5, bf16[616,512]{1,0:T(8,128)(2,1)} %bitcast.15), custom_call_target="tpu_custom_call" | custom-call | flops 4000000000 | tf_op jit(solution)/shard_map/requests/pallas_call | solution.py:108
  4.2 11.5 %all-to-all-start = ((bf16[128,8,512]{2,1,0:T(8,128)(2,1)}), bf16[128,8,512]{2,1,0:T(8,128)(2,1)S(1)}, u32[]{:S(2)}, u32[]{:S(2)}) async-start(bf16[128,8,512]{2,1,0:T(8,128)(2,1)} %bitcast.4), calls=%async_computation | async-start | bytes 2097152 | tf_op jit(solution)/shard_map/all_to_all | solution.py:818
  15.7 0.0 copy-done.3
  15.7 6.9 %columns.1 = (f32[68,144,128]{2,1,0:T(8,128)S(1)}, bf16[64,128,128]{2,1,0:T(8,128)(2,1)}, bf16[272,128]{1,0:T(8,128)(2,1)S(1)}, bf16[272,128]{1,0:T(8,128)(2,1)S...) custom-call(f32[128,64,128]{2,1,0:T(8,128)} %control.3, bf16[128,64,128]{2,1,0:T(8,128)(2,1)} %background.1, ...), custom_call_target="tpu_custom_call" | custom-call | flops 6000000000 | tf_op jit(solution)/shard_map/columns/pallas_call | solution.py:166
  22.7 1.6 %collective-permute-start = (bf16[144,128]{1,0:T(8,128)(2,1)S(1)}, bf16[144,128]{1,0:T(8,128)(2,1)S(1)}, u32[]{:S(2)}, u32[]{:S(2)}) collective-permute-start(bf16[144,128]{1,0:T(8,128)(2,1)S(1)} %get-tuple-element.34), channel_id=1, source_target_pairs={{0,1},{1,2},{2,3},{3,4},{4,5},{5,6},{6,7},{7,0},{8,9},{9,10},{10,1... | collective-permute-start | bytes 110600 | tf_op jit(solution)/shard_map/ppermute | solution.py:202
  24.3 0.0 collective-permute-start.1
  24.3 2.2 %collective-permute-done.y_low.ay_low = bf16[144,128]{1,0:T(8,128)(2,1)S(1)} collective-permute-done((bf16[144,128]{1,0:T(8,128)(2,1)S(1)}, bf16[144,128]{1,0:T(8,128)(2,1)S(1)}, u32[]{:S(2)}, u32[]{:S(2)}) %collective-permute-start) | collective-permute-done | bytes 36896 | tf_op jit(solution)/shard_map/ppermute | solution.py:202
  26.5 2.8 %collective-permute-done.1.y_high.ay_high = bf16[144,128]{1,0:T(8,128)(2,1)S(1)} collective-permute-done((bf16[144,128]{1,0:T(8,128)(2,1)S(1)}, bf16[144,128]{1,0:T(8,128)(2,1)S(1)}, u32[]{:S(2)}, u32[]{:S(2)}) %collective-permute-start.1) | collective-permute-done | bytes 36896 | tf_op jit(solution)/shard_map/ppermute | solution.py:202
  29.3 1.3 %collective-permute-start.2 = (bf16[320,128]{1,0:T(8,128)(2,1)S(1)}, bf16[320,128]{1,0:T(8,128)(2,1)S(1)}, u32[]{:S(2)}, u32[]{:S(2)}) collective-permute-start(bf16[320,128]{1,0:T(8,128)(2,1)S(1)} %get-tuple-element.36), channel_id=1, source_target_pairs={{0,8},{8,16},{16,24},{24,32},{32,40},{40,48},{48,56},{56,64},{64,7... | collective-permute-start | bytes 245768 | tf_op jit(solution)/shard_map/ppermute | solution.py:202
  30.6 4.3 %collective-permute-start.3 = (bf16[320,128]{1,0:T(8,128)(2,1)S(1)}, bf16[320,128]{1,0:T(8,128)(2,1)S(1)}, u32[]{:S(2)}, u32[]{:S(2)}) collective-permute-start(bf16[320,128]{1,0:T(8,128)(2,1)S(1)} %get-tuple-element.37), channel_id=1, source_target_pairs={{0,120},{8,0},{16,8},{24,16},{32,24},{40,32},{48,40},{56,48},{64,5... | collective-permute-start | bytes 245768 | tf_op jit(solution)/shard_map/ppermute | solution.py:202
  34.9 1.3 %spread.5._coef = f32[68,144,128]{2,1,0:T(8,128)S(1)} custom-call(f32[64,128]{1,0:T(8,128)S(1)} %copy-done.3), custom_call_target="tpu_custom_call" | custom-call | flops 1000000000 | tf_op jit(solution)/shard_map/spread/pallas_call | solution.py:308
  36.2 0.4 collective-permute-done.2.x_low.ax_low
  36.6 0.0 collective-permute-done.3.x_high.ax_high
  36.6 5.2 %increment.1 = (bf16[64,128,128]{2,1,0:T(8,128)(2,1)}, f32[68,144,128]{2,1,0:T(8,128)S(1)}, f32[68,144,128]{2,1,0:T(8,128)S(1)}) custom-call(f32[68,144,128]{2,1,0:T(8,128)S(1)} %get-tuple-element.31._field, f32[68,144,128]{2,1,0:T(8,128)S(1)} %spread.5._coef, ...), custom_call_target="tpu_custom_call", output_to_operand_aliasing={{1}: (0, {}), {2}: (1, {})} | custom-call | flops 6000000000 | tf_op jit(solution)/shard_map/increment/pallas_call | solution.py:361
  41.8 0.0 all-to-all-done.got
  41.8 0.0 copy-start.5
  41.8 0.0 copy-start.6
  41.8 0.0 copy-start.7
  41.8 0.0 copy-start.8
  41.9 0.0 copy-start.9
  41.9 0.0 copy-start.10
  41.9 6.7 %gather.1 = (bf16[1024,256]{1,0:T(8,128)(2,1)}, bf16[768,256]{1,0:T(8,128)(2,1)S(1)}) custom-call(bf16[128,8,512]{2,1,0:T(8,128)(2,1)S(1)} %all-to-all-done.got, bf16[8192,128]{1,0:T(8,128)(2,1)} %bitcast.25, bf16[8192,128]{1,0:T(8,128)(2,1)} %bitcast.26), custom_call_target="tpu_custom_call" | custom-call | flops 5000000000 | tf_op jit(solution)/shard_map/gather/pallas_call | solution.py:457
  48.6 0.0 copy-done.5
  48.6 0.0 copy-done.6
  48.6 0.0 copy-done.7
  48.6 0.0 copy-done.8
  48.6 0.0 copy-done.9
  48.6 0.0 copy-done.10
  48.7 10.4 %adjoint.1 = (f32[8192,128]{1,0:T(8,128)S(1)}, bf16[256,128]{1,0:T(8,128)(2,1)S(1)}, bf16[256,128]{1,0:T(8,128)(2,1)S(1)}, bf16[128,128]{1,0:T(8,128)(2,1)S(1)}, bf16[128,128]{1,0:T(8,128)(2,1)S(1)}) custom-call(bf16[128,8,512]{2,1,0:T(8,128)(2,1)S(1)} %all-to-all-done.got, bf16[768,256]{1,0:T(8,128)(2,1)S(1)} %get-tuple-element.40.slots, ...), custom_call_target="tpu_custom_call" | custom-call | flops 10000000000 | tf_op jit(solution)/shard_map/adjoint/pallas_call | solution.py:560
  59.1 0.0 copy-start
  59.1 2.0 %copy-done = f32[8192,128]{1,0:T(8,128)} copy-done((f32[8192,128]{1,0:T(8,128)}, f32[8192,128]{1,0:T(8,128)S(1)}, u32[]{:S(2)}) %copy-start) | copy-done | bytes 4194328
  61.1 1.9 %collective-permute-start.4 = (bf16[128,128]{1,0:T(8,128)(2,1)S(1)}, bf16[128,128]{1,0:T(8,128)(2,1)S(1)}, u32[]{:S(2)}, u32[]{:S(2)}) collective-permute-start(bf16[128,128]{1,0:T(8,128)(2,1)S(1)} %get-tuple-element.45), channel_id=1, source_target_pairs={{0,1},{1,2},{2,3},{3,4},{4,5},{5,6},{6,7},{7,0},{8,9},{9,10},{10,1... | collective-permute-start | bytes 98312 | tf_op jit(solution)/shard_map/ppermute | solution.py:202
  63.0 0.6 collective-permute-start.5
  63.6 8.9 %all-to-all-start.1 = ((bf16[128,8,256]{2,1,0:T(8,128)(2,1)}), bf16[128,8,256]{2,1,0:T(8,128)(2,1)S(1)}, u32[]{:S(2)}, u32[]{:S(2)}) async-start(bf16[128,8,256]{2,1,0:T(8,128)(2,1)} %bitcast.7), calls=%async_computation.1 | async-start | bytes 1048576 | tf_op jit(solution)/shard_map/all_to_all | solution.py:818
  72.4 0.0 copy-start.1
  72.4 2.2 %copy-done.1 = f32[8192,128]{1,0:T(8,128)S(1)} copy-done((f32[8192,128]{1,0:T(8,128)S(1)}, f32[8192,128]{1,0:T(8,128)}, u32[]{:S(2)}) %copy-start.1) | copy-done | bytes 4194328
  74.6 0.0 copy-start.2
  74.6 4.2 %ready.1 = (f32[68,144,128]{2,1,0:T(8,128)S(1)}, f32[64,128,128]{2,1,0:T(8,128)S(1)}, f32[68,144,128]{2,1,0:T(8,128)S(1)}, f32[128,48,128]{2,1,0:T(8,128)S(1)}, ...) custom-call(f32[8192,128]{1,0:T(8,128)S(1)} %copy-done.1, f32[64,128]{1,0:T(8,128)S(1)} %copy-done.3, ...), custom_call_target="tpu_custom_call" | custom-call | flops 3000000000 | tf_op jit(solution)/shard_map/ready/pallas_call | solution.py:648
  78.8 0.0 collective-permute-done.4.y_low
  78.8 0.0 collective-permute-done.5.y_high
  78.9 1.4 %collective-permute-start.6 = (bf16[272,128]{1,0:T(8,128)(2,1)S(1)}, bf16[272,128]{1,0:T(8,128)(2,1)S(1)}, u32[]{:S(2)}, u32[]{:S(2)}) collective-permute-start(bf16[272,128]{1,0:T(8,128)(2,1)S(1)} %get-tuple-element.47), channel_id=1, source_target_pairs={{0,8},{8,16},{16,24},{24,32},{32,40},{40,48},{48,56},{56,64},{64,7... | collective-permute-start | bytes 208904 | tf_op jit(solution)/shard_map/ppermute | solution.py:202
  80.3 4.3 %collective-permute-start.7 = (bf16[272,128]{1,0:T(8,128)(2,1)S(1)}, bf16[272,128]{1,0:T(8,128)(2,1)S(1)}, u32[]{:S(2)}, u32[]{:S(2)}) collective-permute-start(bf16[272,128]{1,0:T(8,128)(2,1)S(1)} %get-tuple-element.48), channel_id=1, source_target_pairs={{0,120},{8,0},{16,8},{24,16},{32,24},{40,32},{48,40},{56,48},{64,5... | collective-permute-start | bytes 208904 | tf_op jit(solution)/shard_map/ppermute | solution.py:202
  84.6 0.0 copy-done.2
  84.6 5.1 %interior.1 = (f32[128,64,128]{2,1,0:T(8,128)}, f32[128,48,128]{2,1,0:T(8,128)S(1)}, f32[64,128,128]{2,1,0:T(8,128)S(1)}, f32[68,144,128]{2,1,0:T(8,128)S(1)}) custom-call(f32[8192,128]{1,0:T(8,128)S(1)} %copy-done.2, f32[68,144,128]{2,1,0:T(8,128)S(1)} %get-tuple-element.42.coef, ...), custom_call_target="tpu_custom_call", output_to_operand_aliasing={{1}: (4, {}), {2}: (5, {}), {3}: (6, {})} | custom-call | flops 5000000000 | tf_op jit(solution)/shard_map/interior/pallas_call | solution.py:734
  89.7 0.0 collective-permute-done.6.x_low
  89.7 0.0 collective-permute-done.7.x_high
  89.8 0.0 copy-start.4
  89.8 0.0 copy-start.11
  89.8 1.6 %edges.1 = (f32[128,64,128]{2,1,0:T(8,128)}, f32[64,128,128]{2,1,0:T(8,128)S(1)}, f32[68,144,128]{2,1,0:T(8,128)S(1)}, f32[128,8,128]{2,1,0:T(8,128)S(1)}, f32[128,8,128]{2,1,0:T(8,128)S(1)}) custom-call(f32[8192,128]{1,0:T(8,128)S(1)} %copy-done.2, ...), custom_call_target="tpu_custom_call", output_to_operand_aliasing={{0}: (4, {}), {1}: (5, {}), {2}: (6, {}), {3}: (7, {}), {4}... | custom-call | flops 2000000000 | tf_op jit(solution)/shard_map/edges/pallas_call | solution.py:795
  91.4 0.0 all-to-all-done.1
  91.4 0.0 copy-done.4
  91.5 0.0 copy-done.11
  91.5 2.5 %departures.1 = f32[616,256]{1,0:T(8,128)} custom-call(bf16[1024,256]{1,0:T(8,128)(2,1)S(1)} %bitcast.12, s32[1,256]{1,0:T(1,128)S(1)} %bitcast.23, f32[616,256]{1,0:T(8,128)S(1)} %bitcast.14, bf16[128,512]{1,0:T(8,128)(2,1)S(1)} %copy-done.7, f32[1,512]{1,0:T(1,128)S(1)} %bitcast.19, bf16[512,512]{1,0:T(8,128)(2,1)S(1)} %copy-done.6, ...), custom_call_target="tpu_custom_call" | custom-call | flops 4000000000 | tf_op jit(solution)/shard_map/departures/pallas_call | solution.py:598
  (2 shorter events, 0.0 us)
Async XLA Ops:
  0.6 15.1 %copy-start.3 = (f32[64,128]{1,0:T(8,128)S(1)}, f32[64,128]{1,0:T(8,128)}, u32[]{:S(2)}) copy-start(f32[64,128]{1,0:T(8,128)} %spread.7) | copy-start | bytes 98308
  4.2 37.6 %all-to-all-start = ((bf16[128,8,512]{2,1,0:T(8,128)(2,1)}), bf16[128,8,512]{2,1,0:T(8,128)(2,1)S(1)}, u32[]{:S(2)}, u32[]{:S(2)}) async-start(bf16[128,8,512]{2,1,0:T(8,128)(2,1)} %bitcast.4), calls=%async_computation | async-start | bytes 2097152 | tf_op jit(solution)/shard_map/all_to_all | solution.py:818
  22.7 3.8 %collective-permute-start = (bf16[144,128]{1,0:T(8,128)(2,1)S(1)}, bf16[144,128]{1,0:T(8,128)(2,1)S(1)}, u32[]{:S(2)}, u32[]{:S(2)}) collective-permute-start(bf16[144,128]{1,0:T(8,128)(2,1)S(1)} %get-tuple-element.34), channel_id=1, source_target_pairs={{0,1},{1,2},{2,3},{3,4},{4,5},{5,6},{6,7},{7,0},{8,9},{9,10},{10,1... | collective-permute-start | bytes 110600 | tf_op jit(solution)/shard_map/ppermute | solution.py:202
  24.3 5.0 %collective-permute-start.1 = (bf16[144,128]{1,0:T(8,128)(2,1)S(1)}, bf16[144,128]{1,0:T(8,128)(2,1)S(1)}, u32[]{:S(2)}, u32[]{:S(2)}) collective-permute-start(bf16[144,128]{1,0:T(8,128)(2,1)S(1)} %get-tuple-element.35), channel_id=1, source_target_pairs={{0,7},{1,0},{2,1},{3,2},{4,3},{5,4},{6,5},{7,6},{8,15},{9,8},{10,9... | collective-permute-start | bytes 110600 | tf_op jit(solution)/shard_map/ppermute | solution.py:202
  29.3 7.3 %collective-permute-start.2 = (bf16[320,128]{1,0:T(8,128)(2,1)S(1)}, bf16[320,128]{1,0:T(8,128)(2,1)S(1)}, u32[]{:S(2)}, u32[]{:S(2)}) collective-permute-start(bf16[320,128]{1,0:T(8,128)(2,1)S(1)} %get-tuple-element.36), channel_id=1, source_target_pairs={{0,8},{8,16},{16,24},{24,32},{32,40},{40,48},{48,56},{56,64},{64,7... | collective-permute-start | bytes 245768 | tf_op jit(solution)/shard_map/ppermute | solution.py:202
  30.6 6.0 %collective-permute-start.3 = (bf16[320,128]{1,0:T(8,128)(2,1)S(1)}, bf16[320,128]{1,0:T(8,128)(2,1)S(1)}, u32[]{:S(2)}, u32[]{:S(2)}) collective-permute-start(bf16[320,128]{1,0:T(8,128)(2,1)S(1)} %get-tuple-element.37), channel_id=1, source_target_pairs={{0,120},{8,0},{16,8},{24,16},{32,24},{40,32},{48,40},{56,48},{64,5... | collective-permute-start | bytes 245768 | tf_op jit(solution)/shard_map/ppermute | solution.py:202
  41.8 6.8 %copy-start.5 = (bf16[512,616]{0,1:T(8,128)(2,1)S(1)}, bf16[512,616]{0,1:T(8,128)(2,1)}, u32[]{:S(2)}) copy-start(bf16[512,616]{0,1:T(8,128)(2,1)} %param.25) | copy-start | bytes 1892356
  41.8 6.8 %copy-start.6 = (bf16[512,512]{1,0:T(8,128)(2,1)S(1)}, bf16[512,512]{1,0:T(8,128)(2,1)}, u32[]{:S(2)}) copy-start(bf16[512,512]{1,0:T(8,128)(2,1)} %w_second.3) | copy-start | bytes 1572868
  41.8 6.8 %copy-start.7 = (bf16[128,512]{1,0:T(8,128)(2,1)S(1)}, bf16[128,512]{1,0:T(8,128)(2,1)}, u32[]{:S(2)}) copy-start(bf16[128,512]{1,0:T(8,128)(2,1)} %w_first.3) | copy-start | bytes 393220
  41.8 6.8 %copy-start.8 = (f32[616]{0:T(1024)S(1)}, f32[616]{0:T(1024)}, u32[]{:S(2)}) copy-start(f32[616]{0:T(1024)} %ivar.5) | copy-start | bytes 7396
  41.9 6.8 %copy-start.9 = (f32[512]{0:T(512)S(1)}, f32[512]{0:T(512)}, u32[]{:S(2)}) copy-start(f32[512]{0:T(512)} %param.22) | copy-start | bytes 6148
  41.9 6.8 %copy-start.10 = (f32[512]{0:T(512)S(1)}, f32[512]{0:T(512)}, u32[]{:S(2)}) copy-start(f32[512]{0:T(512)} %param.24) | copy-start | bytes 6148
  59.1 2.0 %copy-start = (f32[8192,128]{1,0:T(8,128)}, f32[8192,128]{1,0:T(8,128)S(1)}, u32[]{:S(2)}) copy-start(f32[8192,128]{1,0:T(8,128)S(1)} %get-tuple-element.41.acc) | copy-start | bytes 12582916
  61.1 17.7 %collective-permute-start.4 = (bf16[128,128]{1,0:T(8,128)(2,1)S(1)}, bf16[128,128]{1,0:T(8,128)(2,1)S(1)}, u32[]{:S(2)}, u32[]{:S(2)}) collective-permute-start(bf16[128,128]{1,0:T(8,128)(2,1)S(1)} %get-tuple-element.45), channel_id=1, source_target_pairs={{0,1},{1,2},{2,3},{3,4},{4,5},{5,6},{6,7},{7,0},{8,9},{9,10},{10,1... | collective-permute-start | bytes 98312 | tf_op jit(solution)/shard_map/ppermute | solution.py:202
  63.0 15.9 %collective-permute-start.5 = (bf16[128,128]{1,0:T(8,128)(2,1)S(1)}, bf16[128,128]{1,0:T(8,128)(2,1)S(1)}, u32[]{:S(2)}, u32[]{:S(2)}) collective-permute-start(bf16[128,128]{1,0:T(8,128)(2,1)S(1)} %get-tuple-element.46), channel_id=1, source_target_pairs={{0,7},{1,0},{2,1},{3,2},{4,3},{5,4},{6,5},{7,6},{8,15},{9,8},{10,9... | collective-permute-start | bytes 98312 | tf_op jit(solution)/shard_map/ppermute | solution.py:202
  63.6 27.9 %all-to-all-start.1 = ((bf16[128,8,256]{2,1,0:T(8,128)(2,1)}), bf16[128,8,256]{2,1,0:T(8,128)(2,1)S(1)}, u32[]{:S(2)}, u32[]{:S(2)}) async-start(bf16[128,8,256]{2,1,0:T(8,128)(2,1)} %bitcast.7), calls=%async_computation.1 | async-start | bytes 1048576 | tf_op jit(solution)/shard_map/all_to_all | solution.py:818
  72.4 2.2 %copy-start.1 = (f32[8192,128]{1,0:T(8,128)S(1)}, f32[8192,128]{1,0:T(8,128)}, u32[]{:S(2)}) copy-start(f32[8192,128]{1,0:T(8,128)} %copy-done) | copy-start | bytes 12582916
  74.6 10.0 %copy-start.2 = (f32[8192,128]{1,0:T(8,128)S(1)}, f32[8192,128]{1,0:T(8,128)}, u32[]{:S(2)}) copy-start(f32[8192,128]{1,0:T(8,128)} %copy-done) | copy-start | bytes 12582916
  78.9 10.9 %collective-permute-start.6 = (bf16[272,128]{1,0:T(8,128)(2,1)S(1)}, bf16[272,128]{1,0:T(8,128)(2,1)S(1)}, u32[]{:S(2)}, u32[]{:S(2)}) collective-permute-start(bf16[272,128]{1,0:T(8,128)(2,1)S(1)} %get-tuple-element.47), channel_id=1, source_target_pairs={{0,8},{8,16},{16,24},{24,32},{32,40},{40,48},{48,56},{56,64},{64,7... | collective-permute-start | bytes 208904 | tf_op jit(solution)/shard_map/ppermute | solution.py:202
  80.3 9.4 %collective-permute-start.7 = (bf16[272,128]{1,0:T(8,128)(2,1)S(1)}, bf16[272,128]{1,0:T(8,128)(2,1)S(1)}, u32[]{:S(2)}, u32[]{:S(2)}) collective-permute-start(bf16[272,128]{1,0:T(8,128)(2,1)S(1)} %get-tuple-element.48), channel_id=1, source_target_pairs={{0,120},{8,0},{16,8},{24,16},{32,24},{40,32},{48,40},{56,48},{64,5... | collective-permute-start | bytes 208904 | tf_op jit(solution)/shard_map/ppermute | solution.py:202
  89.8 1.7 %copy-start.4 = (f32[256,616]{0,1:T(8,128)S(1)}, f32[256,616]{0,1:T(8,128)}, u32[]{:S(2)}) copy-start(f32[256,616]{0,1:T(8,128)} %param.19) | copy-start | bytes 1892356
  89.8 1.7 %copy-start.11 = (s32[256,1]{0,1:T(1,128)S(1)}, s32[256,1]{0,1:T(1,128)}, u32[]{:S(2)}) copy-start(s32[256,1]{0,1:T(1,128)} %param.16) | copy-start | bytes 3076

commit v5 on v4

--- a/solution.py
+++ b/solution.py
@@ -66,10 +66,8 @@
     return high, (a - high.astype(F32)).astype(BF16)
 
 
-def eye_pair():
-    row = iota((LEV, 2 * LEV), 0)
-    col = iota((LEV, 2 * LEV), 1)
-    return ((col == row) | (col == row + LEV)).astype(BF16)
+def eye():
+    return (iota((LEV, LEV), 0) == iota((LEV, LEV), 1)).astype(BF16)
 
 
 def ranks(held):
@@ -78,7 +76,7 @@
     return jnp.sum(marks.astype(F32) * nn(marks, before), axis=0, keepdims=True).astype(jnp.int32)
 
 
-def request_kernel(holder, anchor, frac, innov, ivar, w_third, out):
+def request_kernel(holder, anchor, frac, ivar, innov, w_third, out):
     held = holder[...]
     rank = ranks(held)
     at = anchor[...].astype(F32)
@@ -95,11 +93,11 @@
     fields = jnp.concatenate([fields] * (LEV // 8), axis=0)
     fields = jnp.where((iota((LEV, OWN), 0) >> 3) == rank, fields, 0.0).astype(BF16)
     each = down(ivar[...].reshape(1, CH))
-    scaled = (innov[...] * jnp.concatenate([each, each], axis=1)).astype(BF16)
-    pulled = tn(scaled, w_third[...]).astype(BF16)
     row = iota((DEV * ROWS, OWN), 0)
     to_slot = (row == held * ROWS + rank).astype(BF16)
     to_fields = (row == held * ROWS + CAP).astype(BF16)
+    scaled = (innov[...] * jnp.concatenate([each, each], axis=1)).astype(BF16)
+    pulled = tn(scaled, w_third[...]).astype(BF16)
     out[:, :LEV] = (nn(to_slot, pulled[:, :LEV]) + nt(to_fields, fields)).astype(BF16)
     out[:, LEV:] = nn(to_slot, pulled[:, LEV:]).astype(BF16)
 
@@ -111,74 +109,77 @@
         compiler_params=params(12),
         cost_estimate=cost(4),
         name="requests",
-    )(*map(in_hbm, (holder, anchor, frac, innov, ivar, w_third)))
-
-
-def columns_kernel(control, background, spread, field, bgt, x_up, x_down, y_up, y_down, wide, planes):
-    step = pl.program_id(0)
-    pair = eye_pair()
-    wide[...] = background[...].astype(F32).reshape(LEV * TALL, BY)
-    flat = control.reshape(LEV * TALL, BY)
-    for i in range(TALL):
-        here = pl.ds(i, LEV, stride=TALL)
-        high, low = split_two(flat[here, :])
-        back = wide[here, :].astype(BF16)
-        both = jnp.concatenate(
-            [
-                jnp.concatenate([high, low], axis=1),
-                jnp.concatenate([back, jnp.zeros_like(back)], axis=1),
-            ],
-            axis=0,
-        )
-        turned = nt(pair, both)
-        field[step * TALL + i + 2, 8 : 8 + BY, :] = turned[:, :LEV]
-        bgt[i] = turned[:, LEV:].astype(BF16)
-        for n, y in enumerate((0, 1, BY - 2, BY - 1)):
-            planes[n, pl.ds(step * TALL + i, 1), :] = turned[y : y + 1, :LEV]
-
-    @pl.when(step == 0)
-    def _():
-        x_down[:BY, :] = field[2, 8 : 8 + BY, :].astype(BF16)
-        x_down[BY : 2 * BY, :] = field[3, 8 : 8 + BY, :].astype(BF16)
-
-    @pl.when(step == pl.num_programs(0) - 1)
-    def _():
-        x_up[:BY, :] = field[BX, 8 : 8 + BY, :].astype(BF16)
-        x_up[BY : 2 * BY, :] = field[BX + 1, 8 : 8 + BY, :].astype(BF16)
-        s = spread[...]
-        turned = jnp.transpose(jnp.concatenate([s, s], axis=0))
-
-        def rows(two):
-            high, low = split_two(two)
-            zero = jnp.zeros((12, BY), F32)
-            return jnp.concatenate([high.astype(F32), low.astype(F32), zero], axis=0).astype(BF16)
-
-        x_down[2 * BY :, :] = rows(s[0:2, :])
-        x_up[2 * BY :, :] = rows(s[BX - 2 : BX, :])
-        y_down[: 2 * BX, :] = planes[0:2].reshape(2 * BX, LEV).astype(BF16)
-        y_up[: 2 * BX, :] = planes[2:4].reshape(2 * BX, LEV).astype(BF16)
-        y_down[2 * BX :, :] = rows(turned[0:2, :])
-        y_up[2 * BX :, :] = rows(turned[BY - 2 : BY, :])
+    )(*map(in_hbm, (holder, anchor, frac, ivar, innov, w_third)))
+
+
+def columns_kernel(
+    control, background, spread, field, bgt, x_up, x_down, y_up, y_down,
+    held, back_held, wide, turned_back, planes, came, back_came, went,
+):
+    tall = BX // TALL
+
+    def bring(part):
+        at = pl.ds(part * TALL, TALL)
+        return pltpu.make_async_copy(control.at[:, at], held.at[part], came.at[part])
+
+    def leave(part):
+        at = pl.ds(part * TALL, TALL)
+        return pltpu.make_async_copy(turned_back.at[at], bgt.at[at], went.at[part])
+
+    fetch = pltpu.make_async_copy(background, back_held, back_came)
+    bring(0).start()
+    fetch.start()
+    for part in range(1, tall):
+        bring(part).start()
+    unit = eye()
+    fetch.wait()
+
+    def turn(part, carry):
+        first = pl.multiple_of(part * TALL, TALL)
+        wide[...] = back_held[:, pl.ds(first, TALL), :].astype(F32).reshape(LEV * TALL, BY)
+        bring(part).wait()
+        flat = held.at[part].reshape(LEV * TALL, BY)
+        for i in range(TALL):
+            here = pl.ds(i, LEV, stride=TALL)
+            turned = jnp.transpose(flat[here, :])
+            field[first + i + 2, 8 : 8 + BY, :] = turned
+            back = wide[here, :].astype(BF16)
+            turned_back[first + i] = nt(unit, back).astype(BF16)
+            for n, y in enumerate((0, 1, BY - 2, BY - 1)):
+                planes[n, pl.ds(first + i, 1), :] = turned[y : y + 1, :LEV]
+        leave(part).start()
+        return carry
+
+    lax.fori_loop(0, tall, turn, 0)
+    x_down[:BY, :] = field[2, 8 : 8 + BY, :].astype(BF16)
+    x_down[BY : 2 * BY, :] = field[3, 8 : 8 + BY, :].astype(BF16)
+    x_up[:BY, :] = field[BX, 8 : 8 + BY, :].astype(BF16)
+    x_up[BY : 2 * BY, :] = field[BX + 1, 8 : 8 + BY, :].astype(BF16)
+    s = spread[...]
+    turned = jnp.transpose(jnp.concatenate([s, s], axis=0))
+
+    def rows(two):
+        high, low = split_two(two)
+        zero = jnp.zeros((12, BY), F32)
+        return jnp.concatenate([high.astype(F32), low.astype(F32), zero], axis=0).astype(BF16)
+
+    x_down[2 * BY :, :] = rows(s[0:2, :])
+    x_up[2 * BY :, :] = rows(s[BX - 2 : BX, :])
+    y_down[: 2 * BX, :] = planes[0:2].reshape(2 * BX, LEV).astype(BF16)
+    y_up[: 2 * BX, :] = planes[2:4].reshape(2 * BX, LEV).astype(BF16)
+    y_down[2 * BX :, :] = rows(turned[0:2, :])
+    y_up[2 * BX :, :] = rows(turned[BY - 2 : BY, :])
+    for part in range(tall):
+        leave(part).wait()
 
 
 def to_columns(control, background, spread):
-    keep = lambda i: (0, 0)
+    hbm = pl.BlockSpec(memory_space=pltpu.HBM)
+    whole = pl.BlockSpec(memory_space=pltpu.VMEM)
     return pl.pallas_call(
         columns_kernel,
-        grid=(BX // TALL,),
-        in_specs=[
-            pl.BlockSpec((LEV, TALL, BY), lambda i: (0, i, 0)),
-            pl.BlockSpec((LEV, TALL, BY), lambda i: (0, i, 0)),
-            pl.BlockSpec((BX, BY), keep),
-        ],
-        out_specs=[
-            pl.BlockSpec(memory_space=pltpu.VMEM),
-            pl.BlockSpec((TALL, BY, LEV), lambda i: (i, 0, 0)),
-            pl.BlockSpec((2 * BY + 16, LEV), keep),
-            pl.BlockSpec((2 * BY + 16, LEV), keep),
-            pl.BlockSpec((2 * BX + 16, LEV), keep),
-            pl.BlockSpec((2 * BX + 16, LEV), keep),
-        ],
+        in_specs=[hbm, hbm, whole],
+        out_specs=[whole, hbm] + [whole] * 4,
         out_shape=[
             pltpu.VMEM((PX, PY, LEV), F32),
             pltpu.HBM((BX, BY, LEV), BF16),
@@ -188,10 +189,16 @@
             jax.ShapeDtypeStruct((2 * BX + 16, LEV), BF16),
         ],
         scratch_shapes=[
+            pltpu.VMEM((BX // TALL, LEV, TALL, BY), F32),
+            pltpu.VMEM((LEV, BX, BY), BF16),
             pltpu.VMEM((LEV * TALL, BY), F32),
+            pltpu.VMEM((BX, BY, LEV), BF16),
             pltpu.VMEM((4, BX, LEV), F32),
-        ],
-        compiler_params=params(16, dimension_semantics=("arbitrary",)),
+            pltpu.SemaphoreType.DMA((BX // TALL,)),
+            pltpu.SemaphoreType.DMA,
+            pltpu.SemaphoreType.DMA((BX // TALL,)),
+        ],
+        compiler_params=params(16),
         cost_estimate=cost(6),
         name="columns",
     )(in_hbm(control), in_hbm(background), spread)
@@ -300,18 +307,29 @@
         coef[x, 8 + BY : 9 + BY, :] = lanes(right[0:1, lane : lane + 1])
 
 
-def spread_kernel(spread, coef):
+def sweep(to, field, coef, x):
+    middle = field[x, 8 : 8 + BY, :]
+    to[x, 8 : 8 + BY, :] = middle + coef[x, 8 : 8 + BY, :] * laplace(field, x, 8, BY)
+
+
+def early_kernel(spread, field, coef, first):
     main_coefficients(coef, spread)
 
-
-def over_lanes(spread):
-    return pl.pallas_call(
-        spread_kernel,
-        out_shape=pltpu.VMEM((PX, PY, LEV), F32),
+    def one(x, carry):
+        sweep(first, field, coef, x)
+        return carry
+
+    lax.fori_loop(3, PX - 3, one, 0)
+
+
+def early(spread, field):
+    return pl.pallas_call(
+        early_kernel,
+        out_shape=[pltpu.VMEM((PX, PY, LEV), F32), pltpu.VMEM((PX, PY, LEV), F32)],
         compiler_params=params(2),
-        cost_estimate=cost(1),
-        name="spread",
-    )(spread)
+        cost_estimate=cost(2),
+        name="early",
+    )(spread, in_vmem(field))
 
 
 def joined(rows, at):
@@ -323,23 +341,22 @@
 
 
 def increment_kernel(
-    _field, _coef, x_low, x_high, y_low, y_high, inc, field, coef, first, done, went
+    _field, _coef, _first, x_low, x_high, y_low, y_high,
+    inc, kept, field, coef, first, done, went, kept_went,
 ):
     def leave(part):
         at = pl.ds(part * CHUNK, CHUNK)
         return pltpu.make_async_copy(done.at[at], inc.at[at], went.at[part])
 
     rim_coefficients(coef, x_low, x_high, y_low, y_high)
+    keep = pltpu.make_async_copy(coef, kept, kept_went)
+    keep.start()
     fill_x(field, x_low, x_high, 2 * BY + 16)
     fill_y(field, y_low, y_high)
 
-    def sweep_one(x, carry):
-        middle = field[x, 8 : 8 + BY, :]
-        first[x, 8 : 8 + BY, :] = middle + coef[x, 8 : 8 + BY, :] * laplace(field, x, 8, BY)
-        return carry
-
-    lax.fori_loop(1, PX - 1, sweep_one, 0)
-    for y in (7, 8 + BY):
+    for x in (1, 2, BX + 1, BX + 2):
+        sweep(first, field, coef, x)
+    for y in (7, 8, 7 + BY, 8 + BY):
         moved = plane(field, 2, y, BX) + plane(coef, 2, y, BX) * plane_laplace(field, y)
         set_plane(first, 2, y, BX, moved)
 
@@ -354,29 +371,33 @@
         leave(part).start()
     for part in range(PARTS):
         leave(part).wait()
-
-
-def increments(field, coef, rims):
+    keep.wait()
+
+
+def increments(field, coef, first, rims):
     whole = pl.BlockSpec(memory_space=pltpu.VMEM)
+    padded = pltpu.VMEM((PX, PY, LEV), F32)
     return pl.pallas_call(
         increment_kernel,
-        in_specs=[whole] * 6,
-        out_specs=[pl.BlockSpec(memory_space=pltpu.HBM), whole, whole],
+        in_specs=[whole] * 7,
+        out_specs=[pl.BlockSpec(memory_space=pltpu.HBM)] * 2 + [whole] * 3,
         out_shape=[
             pltpu.HBM((BX, BY, LEV), BF16),
-            pltpu.VMEM((PX, PY, LEV), F32),
-            pltpu.VMEM((PX, PY, LEV), F32),
-        ],
-        input_output_aliases={0: 1, 1: 2},
+            pltpu.HBM((PX, PY, LEV), F32),
+            padded,
+            padded,
+            padded,
+        ],
+        input_output_aliases={0: 2, 1: 3, 2: 4},
         scratch_shapes=[
-            pltpu.VMEM((PX, PY, LEV), F32),
             pltpu.VMEM((BX, BY, LEV), BF16),
             pltpu.SemaphoreType.DMA((PARTS,)),
-        ],
-        compiler_params=params(12),
+            pltpu.SemaphoreType.DMA,
+        ],
+        compiler_params=params(8),
         cost_estimate=cost(6),
         name="increment",
-    )(in_vmem(field), in_vmem(coef), *rims)[0]
+    )(in_vmem(field), in_vmem(coef), in_vmem(first), *rims)[:2]
 
 
 def decode(rows):
@@ -384,7 +405,7 @@
     frac_x = back(2) + back(3) + back(4)
     frac_y = back(5) + back(6) + back(7)
     valid = rows > 0.5
-    cell = jnp.where(valid, (rows - 1.0) * BY + back(1), 0.0).astype(jnp.int32)
+    cell = jnp.where(valid, ((rows - 1.0) * BY + back(1)).astype(jnp.int32), 2 * iota(rows.shape, 0))
     off = lambda w: jnp.where(valid, w, 0.0)
     return cell, (
         off((1.0 - frac_x) * (1.0 - frac_y)),
@@ -396,7 +417,7 @@
 
 def gather_kernel(
     got, background, increment, reply, slots,
-    wide, cells, table, ga, gb, gc, gd, spaced, bgt, inct, packed, came,
+    wide, cells, table, ga, gb, spaced, both, packed, came,
 ):
     part = CELLS // PARTS
 
@@ -413,12 +434,12 @@
     cells[...] = cell
     pltpu.sync_copy(cells, table)
     for i in range(PARTS):
-        for n, wider in ((0, bgt), (1, inct)):
+        for n in range(2):
             bring(n, i).wait()
 
             def widen(j, carry):
-                at = pl.ds(pl.multiple_of(i * part + j * BY, BY), BY)
-                wider[at, :] = packed[n, at, :].astype(F32)
+                first = pl.multiple_of(i * part + j * BY, BY)
+                both[pl.ds(2 * first + n, BY, stride=2), :] = packed[n, pl.ds(first, BY), :].astype(F32)
                 return carry
 
             lax.fori_loop(0, part // BY, widen, 0)
@@ -428,23 +449,21 @@
             for n in range(8):
                 owner = step * 8 + n
                 at = table[owner, 8 * k]
-                to = pl.ds(2 * (k * DEV + owner), 2)
-                ga[to, :] = bgt[pl.ds(at, 2), :]
-                gb[to, :] = bgt[pl.ds(at + BY, 2), :]
-                gc[to, :] = inct[pl.ds(at, 2), :]
-                gd[to, :] = inct[pl.ds(at + BY, 2), :]
+                to = pl.ds(4 * (k * DEV + owner), 4)
+                ga[to, :] = both[pl.ds(2 * at, 4), :]
+                gb[to, :] = both[pl.ds(2 * (at + BY), 4), :]
             return carry
 
         lax.fori_loop(0, DEV // 8, fetch, 0)
     spaced[...] = jnp.zeros_like(spaced)
     for k in range(CAP):
         w = [lanes(weight[:, 8 * k : 8 * k + 1]) for weight in weights]
-        even = pl.ds(2 * DEV * k, DEV, stride=2)
-        odd = pl.ds(2 * DEV * k + 1, DEV, stride=2)
-        for n, (one, two) in enumerate(((ga, gb), (gc, gd))):
-            mixed = w[0] * one[even, :] + w[1] * two[even, :]
-            mixed = mixed + w[2] * one[odd, :]
-            mixed = mixed + w[3] * two[odd, :]
+        for n in range(2):
+            here = pl.ds(4 * DEV * k + n, DEV, stride=4)
+            next_to = pl.ds(4 * DEV * k + 2 + n, DEV, stride=4)
+            mixed = w[0] * ga[here, :] + w[1] * gb[here, :]
+            mixed = mixed + w[2] * ga[next_to, :]
+            mixed = mixed + w[3] * gb[next_to, :]
             slots[k * DEV : (k + 1) * DEV, n * LEV : (n + 1) * LEV] = mixed.astype(BF16)
             spaced[n, pl.ds(k, DEV, stride=ROWS), :] = mixed
     reply[:, :LEV] = spaced[0].astype(BF16)
@@ -452,7 +471,7 @@
 
 
 def gathered(got, bgt, inct):
-    rows = pltpu.VMEM((2 * SLOTS, LEV), F32)
+    rows = pltpu.VMEM((4 * SLOTS, LEV), F32)
     whole = pl.BlockSpec(memory_space=pltpu.VMEM)
     return pl.pallas_call(
         gather_kernel,
@@ -470,11 +489,8 @@
             pltpu.SMEM((DEV, LEV), jnp.int32),
             rows,
             rows,
-            rows,
-            rows,
             pltpu.VMEM((2, DEV * ROWS, LEV), F32),
-            pltpu.VMEM((CELLS, LEV), F32),
-            pltpu.VMEM((CELLS, LEV), F32),
+            pltpu.VMEM((2 * CELLS, LEV), F32),
             pltpu.VMEM((2, CELLS, LEV), BF16),
             pltpu.SemaphoreType.DMA((2, PARTS)),
         ],
@@ -498,10 +514,16 @@
 
 
 def adjoint_kernel(
-    got, slots, w_first, b_first, w_second, b_second, w_third, ivar,
-    acc, x_up, x_down, y_up, y_down,
-    wide, pulled, profile, cells, table, ca, cb,
+    got, slots, w_first, b_first, w_second, b_second, w_third, ivar, kept, control,
+    acc, x_up, x_down, y_up, y_down, coef, held, low, high,
+    wide, pulled, profile, cells, table, ca, cb, came,
 ):
+    copies = [pltpu.make_async_copy(kept, coef, came.at[3])] + [
+        pltpu.make_async_copy(control.at[:, pl.ds(at, to.shape[1])], to, came.at[n])
+        for n, (to, at) in enumerate(((held, CHUNK), (low, 0), (high, BX - CHUNK)))
+    ]
+    for copy in copies:
+        copy.start()
     for n in range(HID // LEV):
         at = slice(n * LEV, (n + 1) * LEV)
         wide[...] = got[:, :, at].astype(F32).reshape(DEV * ROWS, LEV)
@@ -554,17 +576,29 @@
     for n in range(2):
         y_down[n * BX : (n + 1) * BX, :] = acc[pl.ds(n, BX, stride=BY), :].astype(BF16)
         y_up[n * BX : (n + 1) * BX, :] = acc[pl.ds(BY - 2 + n, BX, stride=BY), :].astype(BF16)
-
-
-def adjoint(got, slots, w_first, b_first, w_second, b_second, w_third, ivar):
+    for copy in copies:
+        copy.wait()
+
+
+INNER = BX - 2 * CHUNK
+
+
+def adjoint(got, slots, w_first, b_first, w_second, b_second, w_third, ivar, kept, control):
+    whole = pl.BlockSpec(memory_space=pltpu.VMEM)
     return pl.pallas_call(
         adjoint_kernel,
+        in_specs=[whole] * 8 + [pl.BlockSpec(memory_space=pltpu.HBM)] * 2,
+        out_specs=[whole] * 9,
         out_shape=[
             pltpu.VMEM((CELLS, LEV), F32),
             jax.ShapeDtypeStruct((2 * BY, LEV), BF16),
             jax.ShapeDtypeStruct((2 * BY, LEV), BF16),
             jax.ShapeDtypeStruct((2 * BX, LEV), BF16),
             jax.ShapeDtypeStruct((2 * BX, LEV), BF16),
+            pltpu.VMEM((PX, PY, LEV), F32),
+            pltpu.VMEM((LEV, INNER, BY), F32),
+            pltpu.VMEM((LEV, CHUNK, BY), F32),
+            pltpu.VMEM((LEV, CHUNK, BY), F32),
         ],
         scratch_shapes=[
             pltpu.VMEM((DEV * ROWS, LEV), F32),
@@ -574,11 +608,15 @@
             pltpu.SMEM((DEV, LEV), jnp.int32),
             pltpu.VMEM((2 * SLOTS, LEV), F32),
             pltpu.VMEM((2 * SLOTS, LEV), F32),
+            pltpu.SemaphoreType.DMA((4,)),
         ],
         compiler_params=params(32),
         cost_estimate=cost(10),
         name="adjoint",
-    )(got, slots, w_first, b_first, w_second, b_second, w_third, ivar)
+    )(
+        got, slots, w_first, b_first, w_second, b_second, w_third, ivar,
+        in_hbm(kept), in_hbm(control),
+    )
 
 
 def departure_kernel(
@@ -604,18 +642,7 @@
     )(reply, holder, innov, w_first, b_first, w_second, b_second, w_third, ivar)
 
 
-def ready_kernel(
-    acc, spread, ax_low, ax_high, ay_low, ay_high, control,
-    coef, grown, scaled, held, low, high, field, came,
-):
-    copies = [
-        pltpu.make_async_copy(control.at[:, pl.ds(at, to.shape[1])], to, came.at[n])
-        for n, (to, at) in enumerate(((held, CHUNK), (low, 0), (high, BX - CHUNK)))
-    ]
-    for copy in copies:
-        copy.start()
-    main_coefficients(coef, spread)
-    rim_coefficients(coef, ax_low, ax_high, ay_low, ay_high)
+def ready_kernel(acc, coef, grown, scaled, field):
     for x in (1, BX + 2):
         field[x] = jnp.zeros((PY, LEV), F32)
     for y in (7, 8 + BY):
@@ -636,43 +663,26 @@
         return carry
 
     lax.fori_loop(2, PX - 2, sweep_one, 0)
-    for copy in copies:
-        copy.wait()
-
-
-INNER = BX - 2 * CHUNK
-
-
-def ready(acc, spread, before, control):
-    whole = pl.BlockSpec(memory_space=pltpu.VMEM)
+
+
+def ready(acc, coef):
     return pl.pallas_call(
         ready_kernel,
-        in_specs=[whole] * 6 + [pl.BlockSpec(memory_space=pltpu.HBM)],
-        out_specs=[whole] * 6,
-        out_shape=[
-            pltpu.VMEM((PX, PY, LEV), F32),
-            pltpu.VMEM((BX, BY, LEV), F32),
-            pltpu.VMEM((PX, PY, LEV), F32),
-            pltpu.VMEM((LEV, INNER, BY), F32),
-            pltpu.VMEM((LEV, CHUNK, BY), F32),
-            pltpu.VMEM((LEV, CHUNK, BY), F32),
-        ],
-        scratch_shapes=[pltpu.VMEM((PX, PY, LEV), F32), pltpu.SemaphoreType.DMA((3,))],
+        out_shape=[pltpu.VMEM((BX, BY, LEV), F32), pltpu.VMEM((PX, PY, LEV), F32)],
+        scratch_shapes=[pltpu.VMEM((PX, PY, LEV), F32)],
         compiler_params=params(8),
         cost_estimate=cost(3),
         name="ready",
-    )(in_vmem(acc), spread, *before, in_hbm(control))
-
-
-def finish_rows(grown, scaled, held, first, count, offset, pair):
+    )(in_vmem(acc), in_vmem(coef))
+
+
+def finish_rows(grown, scaled, held, first, count):
     flat = held.reshape(LEV * held.shape[1], BY)
     for i in range(count):
         x = first + i
         value = grown[x] + laplace(scaled, x + 2, 8, BY)
-        high, low = split_two(value)
-        turned = nt(pair, jnp.concatenate([high, low], axis=1))
-        here = pl.ds(offset + i, LEV, stride=held.shape[1])
-        flat[here, :] = turned + flat[here, :]
+        here = pl.ds(i, LEV, stride=held.shape[1])
+        flat[here, :] = jnp.transpose(value) + flat[here, :]
 
 
 def interior_kernel(
@@ -699,7 +709,6 @@
         fixed = flat[at, :] + mine
         flat[at, :] = fixed
         set_plane(scaled, 2, inner, BX, inside * fixed)
-    pair = eye_pair()
 
     def leave(part):
         return pltpu.make_async_copy(
@@ -716,10 +725,8 @@
             for i in range(4):
                 at = first + step * 4 + i
                 value = grown[CHUNK + at] + laplace(scaled, CHUNK + at + 2, 8, BY)
-                high, low = split_two(value)
-                turned = nt(pair, jnp.concatenate([high, low], axis=1))
                 here = pl.ds(at, LEV, stride=INNER)
-                flat[here, :] = turned + flat[here, :]
+                flat[here, :] = jnp.transpose(value) + flat[here, :]
             return carry
 
         lax.fori_loop(0, TALL // 4, some, 0)
@@ -781,9 +788,8 @@
         fixed = grown[inner - 2] + mine
         grown[inner - 2] = fixed
         scaled[inner, main, :] = inside * fixed
-    pair = eye_pair()
     for n in range(2):
-        finish_rows(grown, scaled, held[n], n * (BX - CHUNK), CHUNK, 0, pair)
+        finish_rows(grown, scaled, held[n], n * (BX - CHUNK), CHUNK)
         leave(n).start()
     for n in range(2):
         leave(n).wait()
@@ -842,18 +848,18 @@
     got = exchange(asked.reshape(DEV, ROWS, HID))
     field, bgt, x_up, x_down, y_up, y_down = to_columns(control, background, spread)
     ay_low, ay_high = shift(y_up, "obs", 1), shift(y_down, "obs", -1)
-    wide = over_lanes(spread)
+    wide, first = early(spread, field)
     x_up, x_down = compose(x_up, x_down, ay_low, ay_high)
     ax_low, ax_high = shift(x_up, "tile", 1), shift(x_down, "tile", -1)
     before = (ax_low, ax_high, ay_low, ay_high)
-    inct = increments(field, wide, before)
+    inct, kept = increments(field, wide, first, before)
     reply, slots = gathered(got, bgt.reshape(CELLS, LEV), inct.reshape(CELLS, LEV))
     reply = exchange(reply.reshape(DEV, ROWS, 2 * LEV))
-    acc, x_up, x_down, y_up, y_down = adjoint(
-        got, slots, w_first, b_one, w_second, b_two, w_last, inverse_var
+    acc, x_up, x_down, y_up, y_down, coef, *held = adjoint(
+        got, slots, w_first, b_one, w_second, b_two, w_last, inverse_var, kept, control
     )
     y_low, y_high = shift(y_up, "obs", 1), shift(y_down, "obs", -1)
-    coef, grown, scaled, *held = ready(acc, spread, before, control)
+    grown, scaled = ready(acc, coef)
     x_up, x_down = compose(x_up, x_down, y_low, y_high)
     x_low, x_high = shift(x_up, "tile", 1), shift(x_down, "tile", -1)
     gradient, _, grown, scaled = interior(acc, coef, (y_low, y_high), held[0], grown, scaled)

time: 94.3 us -> 96.6 us (1.024)
  local copies, waits for them, and re-layouts: 4.25 us -> 12.6 us
  Pallas kernels: 47.8 us -> 42.6 us
    unnamed x24 -> x46, local copies, waits for them, and re-layouts: 4.25 us -> 12.6 us
    pallas_call x5, Pallas kernels: 28.1 us -> 25 us  [the longest x1 8.86 us: adjoint(): pl.pallas_call(adjoint_kernel, in_specs=[whole] * 8 + [pl.BlockSpec(memor...]
    pallas_call x1, Pallas kernels: 5.15 us -> 3.59 us  [interior(): pl.pallas_call(interior_kernel, in_specs=[whole] * 7, out_specs=[hbm] + [...]
    pallas_call x1, Pallas kernels: 6.71 us -> 5.33 us  [gathered(): pl.pallas_call(gather_kernel, grid=(1,), in_specs=[pl.BlockSpec((DEV, ROW...]
    pallas_call x1, Pallas kernels: 2.52 us -> 3.57 us  [departures_of(): pl.pallas_call(departure_kernel, out_shape=jax.ShapeDtypeStruct((CH, OWN)...]
  transfers between devices with their start and end apart: 10 -> 10, of which waited for: 3 -> 2; matrix products, arithmetic and copies ran while one was open for 0% -> 0% of each run, Pallas kernels for 26% -> 22%
where the time goes in v5:
time: 96.6 us; the launch traced here: 96.2 us
  Pallas kernels  42.6 us (44%)
  starting transfers between devices  34.8 us (36%)
  local copies, waits for them, and re-layouts  12.6 us (13%)
  waiting for transfers between devices  5.16 us (5%)
  between operations  1 us (1%)
    all_to_all x2, starting transfers between devices, exchange(): lax.all_to_all(array, ('tile', 'obs'), split_axis=0, concat_axis=0, tiled...  20.3 us
    ppermute x8, starting transfers between devices, shift(): lax.ppermute(array, axis, [(i, (i + by) % count) for i in range(count)])  14.6 us
    unnamed x46, local copies, waits for them, and re-layouts  12.6 us
    pallas_call x1, Pallas kernels, adjoint(): pl.pallas_call(adjoint_kernel, in_specs=[whole] * 8 + [pl.BlockSpec(memor...  8.86 us
    pallas_call x1, Pallas kernels, to_columns(): pl.pallas_call(columns_kernel, in_specs=[hbm, hbm, whole], out_specs=[who...  6.76 us
    pallas_call x1, Pallas kernels, gathered(): pl.pallas_call(gather_kernel, grid=(1,), in_specs=[pl.BlockSpec((DEV, ROW...  5.33 us
    ppermute x8, waiting for transfers between devices, shift(): lax.ppermute(array, axis, [(i, (i + by) % count) for i in range(count)])  5.15 us
    pallas_call x1, Pallas kernels, requests(): pl.pallas_call(request_kernel, out_shape=jax.ShapeDtypeStruct((DEV * ROWS...  3.68 us
  transfers between devices with their start and end apart: 10, of which 2 were waited for; matrix products, arithmetic and copies ran while one was open for 0% of the time, Pallas kernels for 22%

profile of v5, /device:TPU:1, one launch (start us, length us, event | category | flops | bytes accessed | tf_op | source)
XLA Modules:
  0.0 96.2 jit_solution(8530434262019825053)
XLA Ops:
  0.6 0.0 copy-start.18
  0.6 3.7 %requests.1 = bf16[1024,512]{1,0:T(8,128)(2,1)} custom-call(s32[1,256]{1,0:T(1,128)} %bitcast.22, s32[1,256]{1,0:T(1,128)} %bitcast.24, f32[2,256]{1,0:T(2,128)} %frac.1, f32[616]{0:T(1024)} %ivar.5, f32[616,256]{1,0:T(8,128)} %bitcast.13, bf16[616,512]{1,0:T(8,128)(2,1)} %bitcast.15), custom_call_target="tpu_custom_call" | custom-call | flops 4000000000 | tf_op jit(solution)/shard_map/requests/pallas_call | solution.py:106
  4.3 11.5 %all-to-all-start = ((bf16[128,8,512]{2,1,0:T(8,128)(2,1)}), bf16[128,8,512]{2,1,0:T(8,128)(2,1)S(1)}, u32[]{:S(2)}, u32[]{:S(2)}) async-start(bf16[128,8,512]{2,1,0:T(8,128)(2,1)} %bitcast.4), calls=%async_computation | async-start | bytes 2097152 | tf_op jit(solution)/shard_map/all_to_all | solution.py:824
  15.8 0.0 copy-done.18
  15.8 6.8 %columns.1 = (f32[68,144,128]{2,1,0:T(8,128)S(1)}, bf16[64,128,128]{2,1,0:T(8,128)(2,1)}, bf16[272,128]{1,0:T(8,128)(2,1)S(1)}, bf16[272,128]{1,0:T(8,128)(2,1)S...) custom-call(f32[128,64,128]{2,1,0:T(8,128)} %control.3, bf16[128,64,128]{2,1,0:T(8,128)(2,1)} %background.1, ...), custom_call_target="tpu_custom_call" | custom-call | flops 6000000000 | tf_op jit(solution)/shard_map/columns/pallas_call | solution.py:179
  22.6 1.6 %collective-permute-start = (bf16[144,128]{1,0:T(8,128)(2,1)S(1)}, bf16[144,128]{1,0:T(8,128)(2,1)S(1)}, u32[]{:S(2)}, u32[]{:S(2)}) collective-permute-start(bf16[144,128]{1,0:T(8,128)(2,1)S(1)} %get-tuple-element.39), channel_id=1, source_target_pairs={{0,1},{1,2},{2,3},{3,4},{4,5},{5,6},{6,7},{7,0},{8,9},{9,10},{10,1... | collective-permute-start | bytes 110600 | tf_op jit(solution)/shard_map/ppermute | solution.py:209
  24.2 0.0 collective-permute-start.1
  24.2 2.3 %collective-permute-done.y_low = bf16[144,128]{1,0:T(8,128)(2,1)S(1)} collective-permute-done((bf16[144,128]{1,0:T(8,128)(2,1)S(1)}, bf16[144,128]{1,0:T(8,128)(2,1)S(1)}, u32[]{:S(2)}, u32[]{:S(2)}) %collective-permute-start) | collective-permute-done | bytes 36896 | tf_op jit(solution)/shard_map/ppermute | solution.py:209
  26.6 2.8 %collective-permute-done.1.y_high = bf16[144,128]{1,0:T(8,128)(2,1)S(1)} collective-permute-done((bf16[144,128]{1,0:T(8,128)(2,1)S(1)}, bf16[144,128]{1,0:T(8,128)(2,1)S(1)}, u32[]{:S(2)}, u32[]{:S(2)}) %collective-permute-start.1) | collective-permute-done | bytes 36896 | tf_op jit(solution)/shard_map/ppermute | solution.py:209
  29.4 1.3 %collective-permute-start.2 = (bf16[320,128]{1,0:T(8,128)(2,1)S(1)}, bf16[320,128]{1,0:T(8,128)(2,1)S(1)}, u32[]{:S(2)}, u32[]{:S(2)}) collective-permute-start(bf16[320,128]{1,0:T(8,128)(2,1)S(1)} %get-tuple-element.41), channel_id=1, source_target_pairs={{0,8},{8,16},{16,24},{24,32},{32,40},{40,48},{48,56},{56,64},{64,7... | collective-permute-start | bytes 245768 | tf_op jit(solution)/shard_map/ppermute | solution.py:209
  30.7 4.3 %collective-permute-start.3 = (bf16[320,128]{1,0:T(8,128)(2,1)S(1)}, bf16[320,128]{1,0:T(8,128)(2,1)S(1)}, u32[]{:S(2)}, u32[]{:S(2)}) collective-permute-start(bf16[320,128]{1,0:T(8,128)(2,1)S(1)} %get-tuple-element.42), channel_id=1, source_target_pairs={{0,120},{8,0},{16,8},{24,16},{32,24},{40,32},{48,40},{56,48},{64,5... | collective-permute-start | bytes 245768 | tf_op jit(solution)/shard_map/ppermute | solution.py:209
  34.9 3.2 %early.1 = (f32[68,144,128]{2,1,0:T(8,128)S(1)}, f32[68,144,128]{2,1,0:T(8,128)S(1)}) custom-call(f32[64,128]{1,0:T(8,128)S(1)} %copy-done.18, f32[68,144,128]{2,1,0:T(8,128)S(1)} %get-tuple-element.34.field._field), custom_call_target="tpu_custom_call" | custom-call | flops 2000000000 | tf_op jit(solution)/shard_map/early/pallas_call | solution.py:326
  38.2 0.0 collective-permute-done.2.x_low
  38.2 0.0 collective-permute-done.3.x_high
  38.2 3.4 %increment.1 = (bf16[64,128,128]{2,1,0:T(8,128)(2,1)}, f32[68,144,128]{2,1,0:T(8,128)}, f32[68,144,128]{2,1,0:T(8,128)S(1)}, f32[68,144,128]{2,1,0:T(8,128)S(1)}, f32[68,144,128]{2,1,0:T(8,128)S(1)}) custom-call(f32[68,144,128]{2,1,0:T(8,128)S(1)} %get-tuple-element.34.field._field, ...), custom_call_target="tpu_custom_call", output_to_operand_aliasing={{2}: (0, {}), {3}: (1, {}), {4}: (2, {})} | custom-call | flops 6000000000 | tf_op jit(solution)/shard_map/increment/pallas_call | solution.py:380
  41.6 0.0 all-to-all-done.got
  41.6 0.0 copy-start.5
  41.6 0.0 copy-start.13
  41.7 0.0 copy-start.15
  41.7 0.0 copy-start.17
  41.7 0.0 copy-start.19
  41.7 0.0 copy-start.20
  41.7 0.0 copy-start.21
  41.7 5.3 %gather.1 = (bf16[1024,256]{1,0:T(8,128)(2,1)S(1)}, bf16[768,256]{1,0:T(8,128)(2,1)S(1)}) custom-call(bf16[128,8,512]{2,1,0:T(8,128)(2,1)S(1)} %all-to-all-done.got, bf16[8192,128]{1,0:T(8,128)(2,1)} %bitcast.25, bf16[8192,128]{1,0:T(8,128)(2,1)} %bitcast.26), custom_call_target="tpu_custom_call" | custom-call | flops 5000000000 | tf_op jit(solution)/shard_map/gather/pallas_call | solution.py:476
  47.1 0.0 copy-done.5
  47.1 0.0 copy-start.11
  47.1 0.8 copy-done.11
  47.9 0.0 copy-done.13
  47.9 0.0 copy-done.15
  47.9 0.0 copy-done.17
  47.9 0.0 copy-done.19
  47.9 0.0 copy-done.20
  47.9 0.0 copy-done.21
  47.9 0.0 copy-start.6
  47.9 1.2 %copy-done.6 = bf16[128,8,512]{2,1,0:T(8,128)(2,1)S(1)} copy-done((bf16[128,8,512]{2,1,0:T(8,128)(2,1)S(1)}, bf16[128,8,512]{2,1,0:T(8,128)(2,1)}, u32[]{:S(2)}) %copy-start.6) | copy-done | bytes 1048600
  49.1 8.9 %adjoint.1 = (f32[8192,128]{1,0:T(8,128)S(1)}, bf16[256,128]{1,0:T(8,128)(2,1)S(1)}, bf16[256,128]{1,0:T(8,128)(2,1)S(1)}, bf16[128,128]{1,0:T(8,128)(2,1)S(1)},...) custom-call(bf16[128,8,512]{2,1,0:T(8,128)(2,1)S(1)} %copy-done.6, ...), custom_call_target="tpu_custom_call" | custom-call | flops 10000000000 | tf_op jit(solution)/shard_map/adjoint/pallas_call | solution.py:588
  58.0 0.0 copy-start
  58.0 2.2 %copy-done = f32[68,144,128]{2,1,0:T(8,128)} copy-done((f32[68,144,128]{2,1,0:T(8,128)}, f32[68,144,128]{2,1,0:T(8,128)S(1)}, u32[]{:S(2)}) %copy-start) | copy-done | bytes 5013528
  60.2 2.0 %copy-done.3 = f32[8192,128]{1,0:T(8,128)} copy-done((f32[8192,128]{1,0:T(8,128)}, f32[8192,128]{1,0:T(8,128)S(1)}, u32[]{:S(2)}) %copy-start.3) | copy-done | bytes 4194328
  62.3 0.8 copy-done.7
  63.1 0.8 copy-done.9
  63.9 0.7 collective-permute-start.4
  64.5 0.9 collective-permute-start.5
  65.4 8.8 %all-to-all-start.1 = ((bf16[128,8,256]{2,1,0:T(8,128)(2,1)}), bf16[128,8,256]{2,1,0:T(8,128)(2,1)}, u32[]{:S(2)}, u32[]{:S(2)}) async-start(bf16[128,8,256]{2,1,0:T(8,128)(2,1)} %bitcast.12), calls=%async_computation.1 | async-start | bytes 1048576 | tf_op jit(solution)/shard_map/all_to_all | solution.py:824
  74.2 2.4 %copy-done.1 = f32[68,144,128]{2,1,0:T(8,128)S(1)} copy-done((f32[68,144,128]{2,1,0:T(8,128)S(1)}, f32[68,144,128]{2,1,0:T(8,128)}, u32[]{:S(2)}) %copy-start.1) | copy-done | bytes 5013528
  76.6 2.2 %copy-done.4 = f32[8192,128]{1,0:T(8,128)S(1)} copy-done((f32[8192,128]{1,0:T(8,128)S(1)}, f32[8192,128]{1,0:T(8,128)}, u32[]{:S(2)}) %copy-start.4) | copy-done | bytes 4194328
  78.8 2.7 %ready.1 = (f32[64,128,128]{2,1,0:T(8,128)S(1)}, f32[68,144,128]{2,1,0:T(8,128)S(1)}) custom-call(f32[8192,128]{1,0:T(8,128)S(1)} %copy-done.4, f32[68,144,128]{2,1,0:T(8,128)S(1)} %copy-done.1), custom_call_target="tpu_custom_call" | custom-call | flops 3000000000 | tf_op jit(solution)/shard_map/ready/pallas_call | solution.py:669
  81.5 0.0 collective-permute-done.4.y_low
  81.5 0.0 collective-permute-done.5.y_high
  81.5 1.4 %collective-permute-start.6 = (bf16[272,128]{1,0:T(8,128)(2,1)S(1)}, bf16[272,128]{1,0:T(8,128)(2,1)S(1)}, u32[]{:S(2)}, u32[]{:S(2)}) collective-permute-start(bf16[272,128]{1,0:T(8,128)(2,1)S(1)} %get-tuple-element.53), channel_id=1, source_target_pairs={{0,8},{8,16},{16,24},{24,32},{32,40},{40,48},{48,56},{56,64},{64,7... | collective-permute-start | bytes 208904 | tf_op jit(solution)/shard_map/ppermute | solution.py:209
  83.0 4.4 %collective-permute-start.7 = (bf16[272,128]{1,0:T(8,128)(2,1)S(1)}, bf16[272,128]{1,0:T(8,128)(2,1)S(1)}, u32[]{:S(2)}, u32[]{:S(2)}) collective-permute-start(bf16[272,128]{1,0:T(8,128)(2,1)S(1)} %get-tuple-element.54), channel_id=1, source_target_pairs={{0,120},{8,0},{16,8},{24,16},{32,24},{40,32},{48,40},{56,48},{64,5... | collective-permute-start | bytes 208904 | tf_op jit(solution)/shard_map/ppermute | solution.py:209
  87.4 0.0 copy-done.2
  87.4 3.6 %interior.1 = (f32[128,64,128]{2,1,0:T(8,128)}, f32[128,48,128]{2,1,0:T(8,128)S(1)}, f32[64,128,128]{2,1,0:T(8,128)S(1)}, f32[68,144,128]{2,1,0:T(8,128)S(1)}) custom-call(f32[8192,128]{1,0:T(8,128)S(1)} %copy-done.4, f32[68,144,128]{2,1,0:T(8,128)S(1)} %copy-done.2, ...), custom_call_target="tpu_custom_call", output_to_operand_aliasing={{1}: (4, {}), {2}: (5, {}), {3}: (6, {})} | custom-call | flops 5000000000 | tf_op jit(solution)/shard_map/interior/pallas_call | solution.py:741
  91.0 0.0 collective-permute-done.6.x_low
  91.0 0.0 collective-permute-done.7.x_high
  91.0 0.0 copy-done.8
  91.0 0.0 copy-done.10
  91.1 0.0 copy-start.12
  91.1 0.0 copy-start.14
  91.1 0.0 copy-start.16
  91.1 0.0 copy-start.22
  91.1 1.5 %edges.1 = (f32[128,64,128]{2,1,0:T(8,128)}, f32[64,128,128]{2,1,0:T(8,128)S(1)}, f32[68,144,128]{2,1,0:T(8,128)S(1)}, f32[128,8,128]{2,1,0:T(8,128)S(1)}, f32[128,8,128]{2,1,0:T(8,128)S(1)}) custom-call(f32[8192,128]{1,0:T(8,128)S(1)} %copy-done.4, ...), custom_call_target="tpu_custom_call", output_to_operand_aliasing={{0}: (4, {}), {1}: (5, {}), {2}: (6, {}), {3}: (7, {}), {4}... | custom-call | flops 2000000000 | tf_op jit(solution)/shard_map/edges/pallas_call | solution.py:801
  92.6 0.0 all-to-all-done.1
  92.6 3.6 %departures.1 = f32[616,256]{1,0:T(8,128)} custom-call(bf16[1024,256]{1,0:T(8,128)(2,1)} %bitcast.8.reply, s32[1,256]{1,0:T(1,128)S(1)} %bitcast.23, f32[616,256]{1,0:T(8,128)S(1)} %bitcast.14, bf16[128,512]{1,0:T(8,128)(2,1)S(1)} %copy-done.17, f32[1,512]{1,0:T(1,128)S(1)} %bitcast.19, bf16[512,512]{1,0:T(8,128)(2,1)S(1)} %copy-done.16, ...), custom_call_target="tpu_custom_call" | custom-call | flops 4000000000 | tf_op jit(solution)/shard_map/departures/pallas_call | solution.py:636
  (14 shorter events, 0.1 us)
Async XLA Ops:
  0.6 15.2 %copy-start.18 = (f32[64,128]{1,0:T(8,128)S(1)}, f32[64,128]{1,0:T(8,128)}, u32[]{:S(2)}) copy-start(f32[64,128]{1,0:T(8,128)} %spread.3) | copy-start | bytes 98308
  4.3 37.3 %all-to-all-start = ((bf16[128,8,512]{2,1,0:T(8,128)(2,1)}), bf16[128,8,512]{2,1,0:T(8,128)(2,1)S(1)}, u32[]{:S(2)}, u32[]{:S(2)}) async-start(bf16[128,8,512]{2,1,0:T(8,128)(2,1)} %bitcast.4), calls=%async_computation | async-start | bytes 2097152 | tf_op jit(solution)/shard_map/all_to_all | solution.py:824
  22.6 4.0 %collective-permute-start = (bf16[144,128]{1,0:T(8,128)(2,1)S(1)}, bf16[144,128]{1,0:T(8,128)(2,1)S(1)}, u32[]{:S(2)}, u32[]{:S(2)}) collective-permute-start(bf16[144,128]{1,0:T(8,128)(2,1)S(1)} %get-tuple-element.39), channel_id=1, source_target_pairs={{0,1},{1,2},{2,3},{3,4},{4,5},{5,6},{6,7},{7,0},{8,9},{9,10},{10,1... | collective-permute-start | bytes 110600 | tf_op jit(solution)/shard_map/ppermute | solution.py:209
  24.2 5.1 %collective-permute-start.1 = (bf16[144,128]{1,0:T(8,128)(2,1)S(1)}, bf16[144,128]{1,0:T(8,128)(2,1)S(1)}, u32[]{:S(2)}, u32[]{:S(2)}) collective-permute-start(bf16[144,128]{1,0:T(8,128)(2,1)S(1)} %get-tuple-element.40), channel_id=1, source_target_pairs={{0,7},{1,0},{2,1},{3,2},{4,3},{5,4},{6,5},{7,6},{8,15},{9,8},{10,9... | collective-permute-start | bytes 110600 | tf_op jit(solution)/shard_map/ppermute | solution.py:209
  29.4 8.8 %collective-permute-start.2 = (bf16[320,128]{1,0:T(8,128)(2,1)S(1)}, bf16[320,128]{1,0:T(8,128)(2,1)S(1)}, u32[]{:S(2)}, u32[]{:S(2)}) collective-permute-start(bf16[320,128]{1,0:T(8,128)(2,1)S(1)} %get-tuple-element.41), channel_id=1, source_target_pairs={{0,8},{8,16},{16,24},{24,32},{32,40},{40,48},{48,56},{56,64},{64,7... | collective-permute-start | bytes 245768 | tf_op jit(solution)/shard_map/ppermute | solution.py:209
  30.7 7.5 %collective-permute-start.3 = (bf16[320,128]{1,0:T(8,128)(2,1)S(1)}, bf16[320,128]{1,0:T(8,128)(2,1)S(1)}, u32[]{:S(2)}, u32[]{:S(2)}) collective-permute-start(bf16[320,128]{1,0:T(8,128)(2,1)S(1)} %get-tuple-element.42), channel_id=1, source_target_pairs={{0,120},{8,0},{16,8},{24,16},{32,24},{40,32},{48,40},{56,48},{64,5... | collective-permute-start | bytes 245768 | tf_op jit(solution)/shard_map/ppermute | solution.py:209
  41.6 5.4 %copy-start.5 = (bf16[128,8,512]{2,1,0:T(8,128)(2,1)}, bf16[128,8,512]{2,1,0:T(8,128)(2,1)S(1)}, u32[]{:S(2)}) copy-start(bf16[128,8,512]{2,1,0:T(8,128)(2,1)S(1)} %all-to-all-done.got) | copy-start | bytes 3145732
  41.6 6.2 %copy-start.13 = (bf16[512,616]{0,1:T(8,128)(2,1)S(1)}, bf16[512,616]{0,1:T(8,128)(2,1)}, u32[]{:S(2)}) copy-start(bf16[512,616]{0,1:T(8,128)(2,1)} %param.25) | copy-start | bytes 1892356
  41.7 6.2 %copy-start.15 = (bf16[512,512]{1,0:T(8,128)(2,1)S(1)}, bf16[512,512]{1,0:T(8,128)(2,1)}, u32[]{:S(2)}) copy-start(bf16[512,512]{1,0:T(8,128)(2,1)} %w_second.3) | copy-start | bytes 1572868
  41.7 6.2 %copy-start.17 = (bf16[128,512]{1,0:T(8,128)(2,1)S(1)}, bf16[128,512]{1,0:T(8,128)(2,1)}, u32[]{:S(2)}) copy-start(bf16[128,512]{1,0:T(8,128)(2,1)} %w_first.3) | copy-start | bytes 393220
  41.7 6.2 %copy-start.19 = (f32[616]{0:T(1024)S(1)}, f32[616]{0:T(1024)}, u32[]{:S(2)}) copy-start(f32[616]{0:T(1024)} %ivar.5) | copy-start | bytes 7396
  41.7 6.2 %copy-start.20 = (f32[512]{0:T(512)S(1)}, f32[512]{0:T(512)}, u32[]{:S(2)}) copy-start(f32[512]{0:T(512)} %param.22) | copy-start | bytes 6148
  41.7 6.2 %copy-start.21 = (f32[512]{0:T(512)S(1)}, f32[512]{0:T(512)}, u32[]{:S(2)}) copy-start(f32[512]{0:T(512)} %param.24) | copy-start | bytes 6148
  47.1 0.8 copy-start.11
  47.9 1.2 %copy-start.6 = (bf16[128,8,512]{2,1,0:T(8,128)(2,1)S(1)}, bf16[128,8,512]{2,1,0:T(8,128)(2,1)}, u32[]{:S(2)}) copy-start(bf16[128,8,512]{2,1,0:T(8,128)(2,1)} %copy-done.5) | copy-start | bytes 3145732
  58.0 2.3 %copy-start = (f32[68,144,128]{2,1,0:T(8,128)}, f32[68,144,128]{2,1,0:T(8,128)S(1)}, u32[]{:S(2)}) copy-start(f32[68,144,128]{2,1,0:T(8,128)S(1)} %get-tuple-element.48.coef) | copy-start | bytes 15040516
  60.2 2.0 %copy-start.3 = (f32[8192,128]{1,0:T(8,128)}, f32[8192,128]{1,0:T(8,128)S(1)}, u32[]{:S(2)}) copy-start(f32[8192,128]{1,0:T(8,128)S(1)} %get-tuple-element.47.acc) | copy-start | bytes 12582916
  62.3 0.8 copy-start.7
  63.1 0.8 copy-start.9
  63.9 17.6 %collective-permute-start.4 = (bf16[128,128]{1,0:T(8,128)(2,1)S(1)}, bf16[128,128]{1,0:T(8,128)(2,1)S(1)}, u32[]{:S(2)}, u32[]{:S(2)}) collective-permute-start(bf16[128,128]{1,0:T(8,128)(2,1)S(1)} %get-tuple-element.51), channel_id=1, source_target_pairs={{0,1},{1,2},{2,3},{3,4},{4,5},{5,6},{6,7},{7,0},{8,9},{9,10},{10,1... | collective-permute-start | bytes 98312 | tf_op jit(solution)/shard_map/ppermute | solution.py:209
  64.5 17.0 %collective-permute-start.5 = (bf16[128,128]{1,0:T(8,128)(2,1)S(1)}, bf16[128,128]{1,0:T(8,128)(2,1)S(1)}, u32[]{:S(2)}, u32[]{:S(2)}) collective-permute-start(bf16[128,128]{1,0:T(8,128)(2,1)S(1)} %get-tuple-element.52), channel_id=1, source_target_pairs={{0,7},{1,0},{2,1},{3,2},{4,3},{5,4},{6,5},{7,6},{8,15},{9,8},{10,9... | collective-permute-start | bytes 98312 | tf_op jit(solution)/shard_map/ppermute | solution.py:209
  65.4 27.2 %all-to-all-start.1 = ((bf16[128,8,256]{2,1,0:T(8,128)(2,1)}), bf16[128,8,256]{2,1,0:T(8,128)(2,1)}, u32[]{:S(2)}, u32[]{:S(2)}) async-start(bf16[128,8,256]{2,1,0:T(8,128)(2,1)} %bitcast.12), calls=%async_computation.1 | async-start | bytes 1048576 | tf_op jit(solution)/shard_map/all_to_all | solution.py:824
  74.2 2.4 %copy-start.1 = (f32[68,144,128]{2,1,0:T(8,128)S(1)}, f32[68,144,128]{2,1,0:T(8,128)}, u32[]{:S(2)}) copy-start(f32[68,144,128]{2,1,0:T(8,128)} %copy-done) | copy-start | bytes 15040516
  76.6 2.2 %copy-start.4 = (f32[8192,128]{1,0:T(8,128)S(1)}, f32[8192,128]{1,0:T(8,128)}, u32[]{:S(2)}) copy-start(f32[8192,128]{1,0:T(8,128)} %copy-done.3) | copy-start | bytes 12582916
  78.8 8.6 %copy-start.2 = (f32[68,144,128]{2,1,0:T(8,128)S(1)}, f32[68,144,128]{2,1,0:T(8,128)}, u32[]{:S(2)}) copy-start(f32[68,144,128]{2,1,0:T(8,128)} %copy-done) | copy-start | bytes 15040516
  81.5 9.5 %collective-permute-start.6 = (bf16[272,128]{1,0:T(8,128)(2,1)S(1)}, bf16[272,128]{1,0:T(8,128)(2,1)S(1)}, u32[]{:S(2)}, u32[]{:S(2)}) collective-permute-start(bf16[272,128]{1,0:T(8,128)(2,1)S(1)} %get-tuple-element.53), channel_id=1, source_target_pairs={{0,8},{8,16},{16,24},{24,32},{32,40},{40,48},{48,56},{56,64},{64,7... | collective-permute-start | bytes 208904 | tf_op jit(solution)/shard_map/ppermute | solution.py:209
  83.0 8.1 %collective-permute-start.7 = (bf16[272,128]{1,0:T(8,128)(2,1)S(1)}, bf16[272,128]{1,0:T(8,128)(2,1)S(1)}, u32[]{:S(2)}, u32[]{:S(2)}) collective-permute-start(bf16[272,128]{1,0:T(8,128)(2,1)S(1)} %get-tuple-element.54), channel_id=1, source_target_pairs={{0,120},{8,0},{16,8},{24,16},{32,24},{40,32},{48,40},{56,48},{64,5... | collective-permute-start | bytes 208904 | tf_op jit(solution)/shard_map/ppermute | solution.py:209
  87.4 3.6 %copy-start.8 = (f32[128,8,128]{2,1,0:T(8,128)S(1)}, f32[128,8,128]{2,1,0:T(8,128)}, u32[]{:S(2)}) copy-start(f32[128,8,128]{2,1,0:T(8,128)} %copy-done.7) | copy-start | bytes 1572868
  87.4 3.6 %copy-start.10 = (f32[128,8,128]{2,1,0:T(8,128)S(1)}, f32[128,8,128]{2,1,0:T(8,128)}, u32[]{:S(2)}) copy-start(f32[128,8,128]{2,1,0:T(8,128)} %copy-done.9) | copy-start | bytes 1572868
  91.1 1.6 %copy-start.12 = (f32[256,616]{0,1:T(8,128)S(1)}, f32[256,616]{0,1:T(8,128)}, u32[]{:S(2)}) copy-start(f32[256,616]{0,1:T(8,128)} %param.19) | copy-start | bytes 1892356
  91.1 1.6 %copy-start.14 = (bf16[512,616]{0,1:T(8,128)(2,1)S(1)}, bf16[512,616]{0,1:T(8,128)(2,1)}, u32[]{:S(2)}) copy-start(bf16[512,616]{0,1:T(8,128)(2,1)} %param.25) | copy-start | bytes 1892356
  91.1 1.6 %copy-start.16 = (bf16[512,512]{1,0:T(8,128)(2,1)S(1)}, bf16[512,512]{1,0:T(8,128)(2,1)}, u32[]{:S(2)}) copy-start(bf16[512,512]{1,0:T(8,128)(2,1)} %w_second.3) | copy-start | bytes 1572868
  91.1 1.6 %copy-start.22 = (s32[256,1]{0,1:T(1,128)S(1)}, s32[256,1]{0,1:T(1,128)}, u32[]{:S(2)}) copy-start(s32[256,1]{0,1:T(1,128)} %param.16) | copy-start | bytes 3076

commit v6 on v5

--- a/solution.py
+++ b/solution.py
@@ -1,3 +1,5 @@
+import functools
+
 import jax
 import jax.numpy as jnp
 from jax import lax
@@ -64,10 +66,6 @@
 def split_two(a):
     high = a.astype(BF16)
     return high, (a - high.astype(F32)).astype(BF16)
-
-
-def eye():
-    return (iota((LEV, LEV), 0) == iota((LEV, LEV), 1)).astype(BF16)
 
 
 def ranks(held):
@@ -131,7 +129,6 @@
     fetch.start()
     for part in range(1, tall):
         bring(part).start()
-    unit = eye()
     fetch.wait()
 
     def turn(part, carry):
@@ -143,8 +140,7 @@
             here = pl.ds(i, LEV, stride=TALL)
             turned = jnp.transpose(flat[here, :])
             field[first + i + 2, 8 : 8 + BY, :] = turned
-            back = wide[here, :].astype(BF16)
-            turned_back[first + i] = nt(unit, back).astype(BF16)
+            turned_back[first + i] = jnp.transpose(wide[here, :]).astype(BF16)
             for n, y in enumerate((0, 1, BY - 2, BY - 1)):
                 planes[n, pl.ds(first + i, 1), :] = turned[y : y + 1, :LEV]
         leave(part).start()
@@ -209,26 +205,26 @@
     return lax.ppermute(array, axis, [(i, (i + by) % count) for i in range(count)])
 
 
-def compose_kernel(x_up, x_down, y_low, y_high, up, down):
-    rows = x_up.shape[0]
-    up[:rows, :] = x_up[...]
-    down[:rows, :] = x_down[...]
-    low = y_low[...].astype(F32)
-    high = y_high[...].astype(F32)
-    fields = [low[2 * BX :], high[2 * BX :]] if low.shape[0] > 2 * BX else []
-    for out, row in ((up, BX - 1), (down, 0)):
-        pair = [low[BX + row : BX + row + 1], high[row : row + 1], jnp.zeros((14, LEV), F32)]
+def compose_kernel(count, first_up, first_down, low, high, up, down):
+    rows = first_up.shape[0]
+    up[:rows, :] = first_up[...]
+    down[:rows, :] = first_down[...]
+    low = low[...].astype(F32)
+    high = high[...].astype(F32)
+    fields = [low[2 * count :], high[2 * count :]] if low.shape[0] > 2 * count else []
+    for out, row in ((up, count - 1), (down, 0)):
+        pair = [low[count + row : count + row + 1], high[row : row + 1], jnp.zeros((14, LEV), F32)]
         out[rows:, :] = jnp.concatenate(pair + fields, axis=0).astype(BF16)
 
 
-def compose(x_up, x_down, y_low, y_high):
-    rows = x_up.shape[0] + 16 + 2 * (y_low.shape[0] - 2 * BX)
-    return pl.pallas_call(
-        compose_kernel,
+def compose(count, first_up, first_down, low, high):
+    rows = first_up.shape[0] + 16 + 2 * (low.shape[0] - 2 * count)
+    return pl.pallas_call(
+        functools.partial(compose_kernel, count),
         out_shape=[jax.ShapeDtypeStruct((rows, LEV), BF16)] * 2,
         compiler_params=params(2),
         name="compose",
-    )(x_up, x_down, y_low, y_high)
+    )(first_up, first_down, low, high)
 
 
 def laplace(field, x, first, count):
@@ -269,14 +265,17 @@
         set_plane(field, 2, 8 + BY + n, BX, y_high[n * BX : (n + 1) * BX, :].astype(F32))
 
 
-def fill_x(field, x_low, x_high, at):
+def fill_x(field, x_low, x_high):
     for n in range(2):
         field[n, 8 : 8 + BY, :] = x_low[n * BY : (n + 1) * BY, :].astype(F32)
         field[BX + 2 + n, 8 : 8 + BY, :] = x_high[n * BY : (n + 1) * BY, :].astype(F32)
-    for rows, x in ((x_low, 1), (x_high, BX + 2)):
-        pair = rows[at : at + 16, :].astype(F32)
-        field[x, 7:8, :] = pair[0:1]
-        field[x, 8 + BY : 9 + BY, :] = pair[1:2]
+
+
+def fill_corners(field, y_low, y_high):
+    for rows, y in ((y_low, 7), (y_high, 8 + BY)):
+        pair = rows[2 * BX + 16 : 2 * BX + 32, :].astype(F32)
+        field[1, y : y + 1, :] = pair[0:1]
+        field[BX + 2, y : y + 1, :] = pair[1:2]
 
 
 def main_coefficients(coef, spread):
@@ -300,11 +299,11 @@
     for n in range(2):
         set_plane(coef, 2, 6 + n, BX, lanes(sides[:, n : n + 1]))
         set_plane(coef, 2, 8 + BY + n, BX, lanes(sides[:, 2 + n : 3 + n]))
-    for block, x, lane in ((x_low, 1, BX - 1), (x_high, BX + 2, 0)):
-        left = joined(block, 2 * BY + 32)
-        right = joined(block, 2 * BY + 48)
-        coef[x, 7:8, :] = lanes(left[1:2, lane : lane + 1])
-        coef[x, 8 + BY : 9 + BY, :] = lanes(right[0:1, lane : lane + 1])
+    for block, y, lane in ((y_low, 7, BY - 1), (y_high, 8 + BY, 0)):
+        left = joined(block, 2 * BX + 32)
+        right = joined(block, 2 * BX + 48)
+        coef[1, y : y + 1, :] = lanes(left[1:2, lane : lane + 1])
+        coef[BX + 2, y : y + 1, :] = lanes(right[0:1, lane : lane + 1])
 
 
 def sweep(to, field, coef, x):
@@ -351,7 +350,8 @@
     rim_coefficients(coef, x_low, x_high, y_low, y_high)
     keep = pltpu.make_async_copy(coef, kept, kept_went)
     keep.start()
-    fill_x(field, x_low, x_high, 2 * BY + 16)
+    fill_x(field, x_low, x_high)
+    fill_corners(field, y_low, y_high)
     fill_y(field, y_low, y_high)
 
     for x in (1, 2, BX + 1, BX + 2):
@@ -415,9 +415,18 @@
     )
 
 
+def to_table(cell, cells, table, arrived):
+    across = jnp.transpose(cell)
+    for k in range(CAP):
+        cells[k : k + 1, :] = across[8 * k : 8 * k + 1, :]
+    copy = pltpu.make_async_copy(cells, table, arrived)
+    copy.start()
+    return copy
+
+
 def gather_kernel(
     got, background, increment, reply, slots,
-    wide, cells, table, ga, gb, spaced, both, packed, came,
+    wide, cells, table, ga, gb, spaced, both, packed, came, arrived,
 ):
     part = CELLS // PARTS
 
@@ -431,8 +440,7 @@
         bring(1, i).start()
     wide[...] = got[...].astype(F32).reshape(DEV * ROWS, LEV)
     cell, weights = decode(wide[pl.ds(CAP, DEV, stride=ROWS), :])
-    cells[...] = cell
-    pltpu.sync_copy(cells, table)
+    placed = to_table(cell, cells, table, arrived)
     for i in range(PARTS):
         for n in range(2):
             bring(n, i).wait()
@@ -443,12 +451,13 @@
                 return carry
 
             lax.fori_loop(0, part // BY, widen, 0)
+    placed.wait()
     for k in range(CAP):
 
         def fetch(step, carry):
             for n in range(8):
                 owner = step * 8 + n
-                at = table[owner, 8 * k]
+                at = table[k, owner]
                 to = pl.ds(4 * (k * DEV + owner), 4)
                 ga[to, :] = both[pl.ds(2 * at, 4), :]
                 gb[to, :] = both[pl.ds(2 * (at + BY), 4), :]
@@ -485,14 +494,15 @@
         ],
         scratch_shapes=[
             pltpu.VMEM((DEV * ROWS, LEV), F32),
-            pltpu.VMEM((DEV, LEV), jnp.int32),
-            pltpu.SMEM((DEV, LEV), jnp.int32),
+            pltpu.VMEM((8, LEV), jnp.int32),
+            pltpu.SMEM((8, LEV), jnp.int32),
             rows,
             rows,
             pltpu.VMEM((2, DEV * ROWS, LEV), F32),
             pltpu.VMEM((2 * CELLS, LEV), F32),
             pltpu.VMEM((2, CELLS, LEV), BF16),
             pltpu.SemaphoreType.DMA((2, PARTS)),
+            pltpu.SemaphoreType.DMA,
         ],
         compiler_params=params(26),
         cost_estimate=cost(5),
@@ -516,7 +526,7 @@
 def adjoint_kernel(
     got, slots, w_first, b_first, w_second, b_second, w_third, ivar, kept, control,
     acc, x_up, x_down, y_up, y_down, coef, held, low, high,
-    wide, pulled, profile, cells, table, ca, cb, came,
+    wide, pulled, profile, cells, table, ca, cb, came, arrived,
 ):
     copies = [pltpu.make_async_copy(kept, coef, came.at[3])] + [
         pltpu.make_async_copy(control.at[:, pl.ds(at, to.shape[1])], to, came.at[n])
@@ -531,8 +541,7 @@
             pulled[k * DEV : (k + 1) * DEV, at] = wide[pl.ds(k, DEV, stride=ROWS), :]
         if n == 0:
             cell, weights = decode(wide[pl.ds(CAP, DEV, stride=ROWS), :])
-    cells[...] = cell
-    pltpu.sync_copy(cells, table)
+    placed = to_table(cell, cells, table, arrived)
 
     def block(i, carry):
         here = pl.ds(pl.multiple_of(i * BLOCK, BLOCK), BLOCK)
@@ -557,12 +566,13 @@
         cb[even, :] = w[1] * grad
         ca[odd, :] = w[2] * grad
         cb[odd, :] = w[3] * grad
+    placed.wait()
     for k in range(CAP):
 
         def add(step, carry):
             for n in range(8):
                 owner = step * 8 + n
-                at = table[owner, 8 * k]
+                at = table[k, owner]
                 there = pl.ds(2 * (k * DEV + owner), 2)
                 one = acc[pl.ds(at, 2), :] + ca[there, :]
                 two = acc[pl.ds(at + BY, 2), :] + cb[there, :]
@@ -604,11 +614,12 @@
             pltpu.VMEM((DEV * ROWS, LEV), F32),
             pltpu.VMEM((SLOTS, HID), F32),
             pltpu.VMEM((SLOTS, LEV), F32),
-            pltpu.VMEM((DEV, LEV), jnp.int32),
-            pltpu.SMEM((DEV, LEV), jnp.int32),
+            pltpu.VMEM((8, LEV), jnp.int32),
+            pltpu.SMEM((8, LEV), jnp.int32),
             pltpu.VMEM((2 * SLOTS, LEV), F32),
             pltpu.VMEM((2 * SLOTS, LEV), F32),
             pltpu.SemaphoreType.DMA((4,)),
+            pltpu.SemaphoreType.DMA,
         ],
         compiler_params=params(32),
         cost_estimate=cost(10),
@@ -847,10 +858,10 @@
     asked = requests(holder, obs_anchor.reshape(1, OWN), obs_frac, innov, inverse_var, w_last)
     got = exchange(asked.reshape(DEV, ROWS, HID))
     field, bgt, x_up, x_down, y_up, y_down = to_columns(control, background, spread)
+    ax_low, ax_high = shift(x_up, "tile", 1), shift(x_down, "tile", -1)
+    wide, first = early(spread, field)
+    y_up, y_down = compose(BY, y_up, y_down, ax_low, ax_high)
     ay_low, ay_high = shift(y_up, "obs", 1), shift(y_down, "obs", -1)
-    wide, first = early(spread, field)
-    x_up, x_down = compose(x_up, x_down, ay_low, ay_high)
-    ax_low, ax_high = shift(x_up, "tile", 1), shift(x_down, "tile", -1)
     before = (ax_low, ax_high, ay_low, ay_high)
     inct, kept = increments(field, wide, first, before)
     reply, slots = gathered(got, bgt.reshape(CELLS, LEV), inct.reshape(CELLS, LEV))
@@ -860,7 +871,7 @@
     )
     y_low, y_high = shift(y_up, "obs", 1), shift(y_down, "obs", -1)
     grown, scaled = ready(acc, coef)
-    x_up, x_down = compose(x_up, x_down, y_low, y_high)
+    x_up, x_down = compose(BX, x_up, x_down, y_low, y_high)
     x_low, x_high = shift(x_up, "tile", 1), shift(x_down, "tile", -1)
     gradient, _, grown, scaled = interior(acc, coef, (y_low, y_high), held[0], grown, scaled)
     gradient = edges(

time: 96.6 us -> 97 us (level)
  waiting for transfers between devices: 5.16 us -> 6.93 us
    ppermute x8, waiting for transfers between devices: 5.15 us -> 6.93 us  [shift(): lax.ppermute(array, axis, [(i, (i + by) % count) for i in range(count)])]
    all_to_all x2, starting transfers between devices: 20.3 us -> 18.9 us  [exchange(): lax.all_to_all(array, ('tile', 'obs'), split_axis=0, concat_axis=0, tiled...]
    pallas_call x1, Pallas kernels: 8.86 us -> 7.86 us  [adjoint(): pl.pallas_call(adjoint_kernel, in_specs=[whole] * 8 + [pl.BlockSpec(memor...]
where the time goes in v6:
time: 97 us; the launch traced here: 96.6 us
  Pallas kernels  41.9 us (43%)
  starting transfers between devices  34.1 us (35%)
  local copies, waits for them, and re-layouts  12.6 us (13%)
  waiting for transfers between devices  6.93 us (7%)
  between operations  1 us (1%)
    all_to_all x2, starting transfers between devices, exchange(): lax.all_to_all(array, ('tile', 'obs'), split_axis=0, concat_axis=0, tiled...  18.9 us
    ppermute x8, starting transfers between devices, shift(): lax.ppermute(array, axis, [(i, (i + by) % count) for i in range(count)])  15.2 us
    unnamed x46, local copies, waits for them, and re-layouts  12.6 us
    pallas_call x1, Pallas kernels, adjoint(): pl.pallas_call(adjoint_kernel, in_specs=[whole] * 8 + [pl.BlockSpec(memor...  7.86 us
    ppermute x8, waiting for transfers between devices, shift(): lax.ppermute(array, axis, [(i, (i + by) % count) for i in range(count)])  6.93 us
    pallas_call x1, Pallas kernels, to_columns(): pl.pallas_call(columns_kernel, in_specs=[hbm, hbm, whole], out_specs=[who...  6.6 us
    pallas_call x1, Pallas kernels, gathered(): pl.pallas_call(gather_kernel, grid=(1,), in_specs=[pl.BlockSpec((DEV, ROW...  5.81 us
    pallas_call x1, Pallas kernels, requests(): pl.pallas_call(request_kernel, out_shape=jax.ShapeDtypeStruct((DEV * ROWS...  3.68 us
  transfers between devices with their start and end apart: 10, of which 2 were waited for; matrix products, arithmetic and copies ran while one was open for 0% of the time, Pallas kernels for 22%

profile of v6, /device:TPU:1, one launch (start us, length us, event | category | flops | bytes accessed | tf_op | source)
XLA Modules:
  0.0 96.6 jit_solution(8203154248022839197)
XLA Ops:
  0.6 0.0 copy-start.18
  0.6 3.7 %requests.1 = bf16[1024,512]{1,0:T(8,128)(2,1)} custom-call(s32[1,256]{1,0:T(1,128)} %bitcast.22, s32[1,256]{1,0:T(1,128)} %bitcast.24, f32[2,256]{1,0:T(2,128)} %frac.1, f32[616]{0:T(1024)} %ivar.5, f32[616,256]{1,0:T(8,128)} %bitcast.13, bf16[616,512]{1,0:T(8,128)(2,1)} %bitcast.15), custom_call_target="tpu_custom_call" | custom-call | flops 4000000000 | tf_op jit(solution)/shard_map/requests/pallas_call | solution.py:104
  4.3 11.5 %all-to-all-start = ((bf16[128,8,512]{2,1,0:T(8,128)(2,1)}), bf16[128,8,512]{2,1,0:T(8,128)(2,1)S(1)}, u32[]{:S(2)}, u32[]{:S(2)}) async-start(bf16[128,8,512]{2,1,0:T(8,128)(2,1)} %bitcast.4), calls=%async_computation | async-start | bytes 2097152 | tf_op jit(solution)/shard_map/all_to_all | solution.py:835
  15.8 0.0 copy-done.18
  15.8 6.6 %columns.1 = (f32[68,144,128]{2,1,0:T(8,128)S(1)}, bf16[64,128,128]{2,1,0:T(8,128)(2,1)}, bf16[272,128]{1,0:T(8,128)(2,1)S(1)}, bf16[272,128]{1,0:T(8,128)(2,1)S...) custom-call(f32[128,64,128]{2,1,0:T(8,128)} %control.3, bf16[128,64,128]{2,1,0:T(8,128)(2,1)} %background.1, ...), custom_call_target="tpu_custom_call" | custom-call | flops 6000000000 | tf_op jit(solution)/shard_map/columns/pallas_call | solution.py:175
  22.4 1.4 %collective-permute-start = (bf16[272,128]{1,0:T(8,128)(2,1)S(1)}, bf16[272,128]{1,0:T(8,128)(2,1)S(1)}, u32[]{:S(2)}, u32[]{:S(2)}) collective-permute-start(bf16[272,128]{1,0:T(8,128)(2,1)S(1)} %get-tuple-element.37), channel_id=1, source_target_pairs={{0,8},{8,16},{16,24},{24,32},{32,40},{40,48},{48,56},{56,64},{64,7... | collective-permute-start | bytes 208904 | tf_op jit(solution)/shard_map/ppermute | solution.py:205
  23.9 4.3 %collective-permute-start.1 = (bf16[272,128]{1,0:T(8,128)(2,1)S(1)}, bf16[272,128]{1,0:T(8,128)(2,1)S(1)}, u32[]{:S(2)}, u32[]{:S(2)}) collective-permute-start(bf16[272,128]{1,0:T(8,128)(2,1)S(1)} %get-tuple-element.38), channel_id=1, source_target_pairs={{0,120},{8,0},{16,8},{24,16},{32,24},{40,32},{48,40},{56,48},{64,5... | collective-permute-start | bytes 208904 | tf_op jit(solution)/shard_map/ppermute | solution.py:205
  28.1 6.4 %collective-permute-done.low.x_low = bf16[272,128]{1,0:T(8,128)(2,1)S(1)} collective-permute-done((bf16[272,128]{1,0:T(8,128)(2,1)S(1)}, bf16[272,128]{1,0:T(8,128)(2,1)S(1)}, u32[]{:S(2)}, u32[]{:S(2)}) %collective-permute-start) | collective-permute-done | bytes 69664 | tf_op jit(solution)/shard_map/ppermute | solution.py:205
  34.6 0.0 collective-permute-done.1.high.x_high
  34.6 1.7 %collective-permute-start.2 = (bf16[192,128]{1,0:T(8,128)(2,1)S(1)}, bf16[192,128]{1,0:T(8,128)(2,1)S(1)}, u32[]{:S(2)}, u32[]{:S(2)}) collective-permute-start(bf16[192,128]{1,0:T(8,128)(2,1)S(1)} %get-tuple-element.41), channel_id=1, source_target_pairs={{0,1},{1,2},{2,3},{3,4},{4,5},{5,6},{6,7},{7,0},{8,9},{9,10},{10,1... | collective-permute-start | bytes 147464 | tf_op jit(solution)/shard_map/ppermute | solution.py:205
  36.2 0.0 collective-permute-start.3
  36.3 3.2 %early.1 = (f32[68,144,128]{2,1,0:T(8,128)S(1)}, f32[68,144,128]{2,1,0:T(8,128)S(1)}) custom-call(f32[64,128]{1,0:T(8,128)S(1)} %copy-done.18, f32[68,144,128]{2,1,0:T(8,128)S(1)} %get-tuple-element.34.field._field), custom_call_target="tpu_custom_call" | custom-call | flops 2000000000 | tf_op jit(solution)/shard_map/early/pallas_call | solution.py:325
  39.5 0.0 collective-permute-done.2.y_low
  39.5 0.5 collective-permute-done.3.y_high
  40.0 3.4 %increment.1 = (bf16[64,128,128]{2,1,0:T(8,128)(2,1)}, f32[68,144,128]{2,1,0:T(8,128)}, f32[68,144,128]{2,1,0:T(8,128)S(1)}, f32[68,144,128]{2,1,0:T(8,128)S(1)}, f32[68,144,128]{2,1,0:T(8,128)S(1)}) custom-call(f32[68,144,128]{2,1,0:T(8,128)S(1)} %get-tuple-element.34.field._field, ...), custom_call_target="tpu_custom_call", output_to_operand_aliasing={{2}: (0, {}), {3}: (1, {}), {4}: (2, {})} | custom-call | flops 6000000000 | tf_op jit(solution)/shard_map/increment/pallas_call | solution.py:380
  43.4 0.0 all-to-all-done.got
  43.4 0.0 copy-start.5
  43.4 0.0 copy-start.13
  43.4 0.0 copy-start.15
  43.4 0.0 copy-start.17
  43.4 0.0 copy-start.19
  43.4 0.0 copy-start.20
  43.4 0.0 copy-start.21
  43.5 5.8 %gather.1 = (bf16[1024,256]{1,0:T(8,128)(2,1)S(1)}, bf16[768,256]{1,0:T(8,128)(2,1)S(1)}) custom-call(bf16[128,8,512]{2,1,0:T(8,128)(2,1)S(1)} %all-to-all-done.got, bf16[8192,128]{1,0:T(8,128)(2,1)} %bitcast.25, bf16[8192,128]{1,0:T(8,128)(2,1)} %bitcast.26), custom_call_target="tpu_custom_call" | custom-call | flops 5000000000 | tf_op jit(solution)/shard_map/gather/pallas_call | solution.py:485
  49.3 0.0 copy-done.5
  49.3 0.0 copy-start.11
  49.3 0.8 copy-done.11
  50.1 0.0 copy-done.13
  50.1 0.0 copy-done.15
  50.1 0.0 copy-done.17
  50.1 0.0 copy-done.19
  50.1 0.0 copy-done.20
  50.1 0.0 copy-done.21
  50.1 0.0 copy-start.6
  50.1 1.2 %copy-done.6 = bf16[128,8,512]{2,1,0:T(8,128)(2,1)S(1)} copy-done((bf16[128,8,512]{2,1,0:T(8,128)(2,1)S(1)}, bf16[128,8,512]{2,1,0:T(8,128)(2,1)}, u32[]{:S(2)}) %copy-start.6) | copy-done | bytes 1048600
  51.3 7.9 %adjoint.1 = (f32[8192,128]{1,0:T(8,128)S(1)}, bf16[256,128]{1,0:T(8,128)(2,1)S(1)}, bf16[256,128]{1,0:T(8,128)(2,1)S(1)}, bf16[128,128]{1,0:T(8,128)(2,1)S(1)},...) custom-call(bf16[128,8,512]{2,1,0:T(8,128)(2,1)S(1)} %copy-done.6, ...), custom_call_target="tpu_custom_call" | custom-call | flops 10000000000 | tf_op jit(solution)/shard_map/adjoint/pallas_call | solution.py:598
  59.2 0.0 copy-start
  59.2 2.2 %copy-done = f32[68,144,128]{2,1,0:T(8,128)} copy-done((f32[68,144,128]{2,1,0:T(8,128)}, f32[68,144,128]{2,1,0:T(8,128)S(1)}, u32[]{:S(2)}) %copy-start) | copy-done | bytes 5013528
  61.5 2.0 %copy-done.3 = f32[8192,128]{1,0:T(8,128)} copy-done((f32[8192,128]{1,0:T(8,128)}, f32[8192,128]{1,0:T(8,128)S(1)}, u32[]{:S(2)}) %copy-start.3) | copy-done | bytes 4194328
  63.5 0.8 copy-done.7
  64.3 0.8 copy-done.9
  65.1 1.3 %collective-permute-start.4 = (bf16[128,128]{1,0:T(8,128)(2,1)S(1)}, bf16[128,128]{1,0:T(8,128)(2,1)S(1)}, u32[]{:S(2)}, u32[]{:S(2)}) collective-permute-start(bf16[128,128]{1,0:T(8,128)(2,1)S(1)} %get-tuple-element.51), channel_id=1, source_target_pairs={{0,1},{1,2},{2,3},{3,4},{4,5},{5,6},{6,7},{7,0},{8,9},{9,10},{10,1... | collective-permute-start | bytes 98312 | tf_op jit(solution)/shard_map/ppermute | solution.py:205
  66.4 0.6 collective-permute-start.5
  67.0 7.4 %all-to-all-start.1 = ((bf16[128,8,256]{2,1,0:T(8,128)(2,1)}), bf16[128,8,256]{2,1,0:T(8,128)(2,1)}, u32[]{:S(2)}, u32[]{:S(2)}) async-start(bf16[128,8,256]{2,1,0:T(8,128)(2,1)} %bitcast.12), calls=%async_computation.1 | async-start | bytes 1048576 | tf_op jit(solution)/shard_map/all_to_all | solution.py:835
  74.4 0.0 copy-start.1
  74.4 2.4 %copy-done.1 = f32[68,144,128]{2,1,0:T(8,128)S(1)} copy-done((f32[68,144,128]{2,1,0:T(8,128)S(1)}, f32[68,144,128]{2,1,0:T(8,128)}, u32[]{:S(2)}) %copy-start.1) | copy-done | bytes 5013528
  76.8 2.2 %copy-done.4 = f32[8192,128]{1,0:T(8,128)S(1)} copy-done((f32[8192,128]{1,0:T(8,128)S(1)}, f32[8192,128]{1,0:T(8,128)}, u32[]{:S(2)}) %copy-start.4) | copy-done | bytes 4194328
  79.0 2.7 %ready.1 = (f32[64,128,128]{2,1,0:T(8,128)S(1)}, f32[68,144,128]{2,1,0:T(8,128)S(1)}) custom-call(f32[8192,128]{1,0:T(8,128)S(1)} %copy-done.4, f32[68,144,128]{2,1,0:T(8,128)S(1)} %copy-done.1), custom_call_target="tpu_custom_call" | custom-call | flops 3000000000 | tf_op jit(solution)/shard_map/ready/pallas_call | solution.py:680
  81.7 0.0 collective-permute-done.4.low.y_low
  81.7 0.0 collective-permute-done.5.high.y_high
  81.7 1.5 %collective-permute-start.6 = (bf16[272,128]{1,0:T(8,128)(2,1)S(1)}, bf16[272,128]{1,0:T(8,128)(2,1)S(1)}, u32[]{:S(2)}, u32[]{:S(2)}) collective-permute-start(bf16[272,128]{1,0:T(8,128)(2,1)S(1)} %get-tuple-element.53), channel_id=1, source_target_pairs={{0,8},{8,16},{16,24},{24,32},{32,40},{40,48},{48,56},{56,64},{64,7... | collective-permute-start | bytes 208904 | tf_op jit(solution)/shard_map/ppermute | solution.py:205
  83.2 4.5 %collective-permute-start.7 = (bf16[272,128]{1,0:T(8,128)(2,1)S(1)}, bf16[272,128]{1,0:T(8,128)(2,1)S(1)}, u32[]{:S(2)}, u32[]{:S(2)}) collective-permute-start(bf16[272,128]{1,0:T(8,128)(2,1)S(1)} %get-tuple-element.54), channel_id=1, source_target_pairs={{0,120},{8,0},{16,8},{24,16},{32,24},{40,32},{48,40},{56,48},{64,5... | collective-permute-start | bytes 208904 | tf_op jit(solution)/shard_map/ppermute | solution.py:205
  87.8 0.0 copy-done.2
  87.8 3.6 %interior.1 = (f32[128,64,128]{2,1,0:T(8,128)}, f32[128,48,128]{2,1,0:T(8,128)S(1)}, f32[64,128,128]{2,1,0:T(8,128)S(1)}, f32[68,144,128]{2,1,0:T(8,128)S(1)}) custom-call(f32[8192,128]{1,0:T(8,128)S(1)} %copy-done.4, f32[68,144,128]{2,1,0:T(8,128)S(1)} %copy-done.2, ...), custom_call_target="tpu_custom_call", output_to_operand_aliasing={{1}: (4, {}), {2}: (5, {}), {3}: (6, {})} | custom-call | flops 5000000000 | tf_op jit(solution)/shard_map/interior/pallas_call | solution.py:752
  91.4 0.0 collective-permute-done.6.x_low
  91.4 0.0 collective-permute-done.7.x_high
  91.4 0.0 copy-done.8
  91.4 0.0 copy-start.12
  91.4 0.0 copy-start.14
  91.4 0.0 copy-start.16
  91.4 0.0 copy-start.22
  91.4 1.5 %edges.1 = (f32[128,64,128]{2,1,0:T(8,128)}, f32[64,128,128]{2,1,0:T(8,128)S(1)}, f32[68,144,128]{2,1,0:T(8,128)S(1)}, f32[128,8,128]{2,1,0:T(8,128)S(1)}, f32[128,8,128]{2,1,0:T(8,128)S(1)}) custom-call(f32[8192,128]{1,0:T(8,128)S(1)} %copy-done.4, ...), custom_call_target="tpu_custom_call", output_to_operand_aliasing={{0}: (4, {}), {1}: (5, {}), {2}: (6, {}), {3}: (7, {}), {4}... | custom-call | flops 2000000000 | tf_op jit(solution)/shard_map/edges/pallas_call | solution.py:812
  92.9 0.0 all-to-all-done.1
  93.0 3.6 %departures.1 = f32[616,256]{1,0:T(8,128)} custom-call(bf16[1024,256]{1,0:T(8,128)(2,1)} %bitcast.8.reply, s32[1,256]{1,0:T(1,128)S(1)} %bitcast.23, f32[616,256]{1,0:T(8,128)S(1)} %bitcast.14, bf16[128,512]{1,0:T(8,128)(2,1)S(1)} %copy-done.17, f32[1,512]{1,0:T(1,128)S(1)} %bitcast.19, bf16[512,512]{1,0:T(8,128)(2,1)S(1)} %copy-done.16, ...), custom_call_target="tpu_custom_call" | custom-call | flops 4000000000 | tf_op jit(solution)/shard_map/departures/pallas_call | solution.py:647
  (14 shorter events, 0.1 us)
Async XLA Ops:
  0.6 15.2 %copy-start.18 = (f32[64,128]{1,0:T(8,128)S(1)}, f32[64,128]{1,0:T(8,128)}, u32[]{:S(2)}) copy-start(f32[64,128]{1,0:T(8,128)} %spread.3) | copy-start | bytes 98308
  4.3 39.0 %all-to-all-start = ((bf16[128,8,512]{2,1,0:T(8,128)(2,1)}), bf16[128,8,512]{2,1,0:T(8,128)(2,1)S(1)}, u32[]{:S(2)}, u32[]{:S(2)}) async-start(bf16[128,8,512]{2,1,0:T(8,128)(2,1)} %bitcast.4), calls=%async_computation | async-start | bytes 2097152 | tf_op jit(solution)/shard_map/all_to_all | solution.py:835
  22.4 12.1 %collective-permute-start = (bf16[272,128]{1,0:T(8,128)(2,1)S(1)}, bf16[272,128]{1,0:T(8,128)(2,1)S(1)}, u32[]{:S(2)}, u32[]{:S(2)}) collective-permute-start(bf16[272,128]{1,0:T(8,128)(2,1)S(1)} %get-tuple-element.37), channel_id=1, source_target_pairs={{0,8},{8,16},{16,24},{24,32},{32,40},{40,48},{48,56},{56,64},{64,7... | collective-permute-start | bytes 208904 | tf_op jit(solution)/shard_map/ppermute | solution.py:205
  23.9 10.7 %collective-permute-start.1 = (bf16[272,128]{1,0:T(8,128)(2,1)S(1)}, bf16[272,128]{1,0:T(8,128)(2,1)S(1)}, u32[]{:S(2)}, u32[]{:S(2)}) collective-permute-start(bf16[272,128]{1,0:T(8,128)(2,1)S(1)} %get-tuple-element.38), channel_id=1, source_target_pairs={{0,120},{8,0},{16,8},{24,16},{32,24},{40,32},{48,40},{56,48},{64,5... | collective-permute-start | bytes 208904 | tf_op jit(solution)/shard_map/ppermute | solution.py:205
  34.6 4.9 %collective-permute-start.2 = (bf16[192,128]{1,0:T(8,128)(2,1)S(1)}, bf16[192,128]{1,0:T(8,128)(2,1)S(1)}, u32[]{:S(2)}, u32[]{:S(2)}) collective-permute-start(bf16[192,128]{1,0:T(8,128)(2,1)S(1)} %get-tuple-element.41), channel_id=1, source_target_pairs={{0,1},{1,2},{2,3},{3,4},{4,5},{5,6},{6,7},{7,0},{8,9},{9,10},{10,1... | collective-permute-start | bytes 147464 | tf_op jit(solution)/shard_map/ppermute | solution.py:205
  36.2 3.7 %collective-permute-start.3 = (bf16[192,128]{1,0:T(8,128)(2,1)S(1)}, bf16[192,128]{1,0:T(8,128)(2,1)S(1)}, u32[]{:S(2)}, u32[]{:S(2)}) collective-permute-start(bf16[192,128]{1,0:T(8,128)(2,1)S(1)} %get-tuple-element.42), channel_id=1, source_target_pairs={{0,7},{1,0},{2,1},{3,2},{4,3},{5,4},{6,5},{7,6},{8,15},{9,8},{10,9... | collective-permute-start | bytes 147464 | tf_op jit(solution)/shard_map/ppermute | solution.py:205
  43.4 5.9 %copy-start.5 = (bf16[128,8,512]{2,1,0:T(8,128)(2,1)}, bf16[128,8,512]{2,1,0:T(8,128)(2,1)S(1)}, u32[]{:S(2)}) copy-start(bf16[128,8,512]{2,1,0:T(8,128)(2,1)S(1)} %all-to-all-done.got) | copy-start | bytes 3145732
  43.4 6.7 %copy-start.13 = (bf16[512,616]{0,1:T(8,128)(2,1)S(1)}, bf16[512,616]{0,1:T(8,128)(2,1)}, u32[]{:S(2)}) copy-start(bf16[512,616]{0,1:T(8,128)(2,1)} %param.25) | copy-start | bytes 1892356
  43.4 6.7 %copy-start.15 = (bf16[512,512]{1,0:T(8,128)(2,1)S(1)}, bf16[512,512]{1,0:T(8,128)(2,1)}, u32[]{:S(2)}) copy-start(bf16[512,512]{1,0:T(8,128)(2,1)} %w_second.3) | copy-start | bytes 1572868
  43.4 6.7 %copy-start.17 = (bf16[128,512]{1,0:T(8,128)(2,1)S(1)}, bf16[128,512]{1,0:T(8,128)(2,1)}, u32[]{:S(2)}) copy-start(bf16[128,512]{1,0:T(8,128)(2,1)} %w_first.3) | copy-start | bytes 393220
  43.4 6.7 %copy-start.19 = (f32[616]{0:T(1024)S(1)}, f32[616]{0:T(1024)}, u32[]{:S(2)}) copy-start(f32[616]{0:T(1024)} %ivar.5) | copy-start | bytes 7396
  43.4 6.7 %copy-start.20 = (f32[512]{0:T(512)S(1)}, f32[512]{0:T(512)}, u32[]{:S(2)}) copy-start(f32[512]{0:T(512)} %param.22) | copy-start | bytes 6148
  43.4 6.7 %copy-start.21 = (f32[512]{0:T(512)S(1)}, f32[512]{0:T(512)}, u32[]{:S(2)}) copy-start(f32[512]{0:T(512)} %param.24) | copy-start | bytes 6148
  49.3 0.8 copy-start.11
  50.1 1.2 %copy-start.6 = (bf16[128,8,512]{2,1,0:T(8,128)(2,1)S(1)}, bf16[128,8,512]{2,1,0:T(8,128)(2,1)}, u32[]{:S(2)}) copy-start(bf16[128,8,512]{2,1,0:T(8,128)(2,1)} %copy-done.5) | copy-start | bytes 3145732
  59.2 2.3 %copy-start = (f32[68,144,128]{2,1,0:T(8,128)}, f32[68,144,128]{2,1,0:T(8,128)S(1)}, u32[]{:S(2)}) copy-start(f32[68,144,128]{2,1,0:T(8,128)S(1)} %get-tuple-element.48.coef) | copy-start | bytes 15040516
  61.5 2.0 %copy-start.3 = (f32[8192,128]{1,0:T(8,128)}, f32[8192,128]{1,0:T(8,128)S(1)}, u32[]{:S(2)}) copy-start(f32[8192,128]{1,0:T(8,128)S(1)} %get-tuple-element.47.acc) | copy-start | bytes 12582916
  63.5 0.8 copy-start.7
  64.3 0.8 copy-start.9
  65.1 16.6 %collective-permute-start.4 = (bf16[128,128]{1,0:T(8,128)(2,1)S(1)}, bf16[128,128]{1,0:T(8,128)(2,1)S(1)}, u32[]{:S(2)}, u32[]{:S(2)}) collective-permute-start(bf16[128,128]{1,0:T(8,128)(2,1)S(1)} %get-tuple-element.51), channel_id=1, source_target_pairs={{0,1},{1,2},{2,3},{3,4},{4,5},{5,6},{6,7},{7,0},{8,9},{9,10},{10,1... | collective-permute-start | bytes 98312 | tf_op jit(solution)/shard_map/ppermute | solution.py:205
  66.4 15.3 %collective-permute-start.5 = (bf16[128,128]{1,0:T(8,128)(2,1)S(1)}, bf16[128,128]{1,0:T(8,128)(2,1)S(1)}, u32[]{:S(2)}, u32[]{:S(2)}) collective-permute-start(bf16[128,128]{1,0:T(8,128)(2,1)S(1)} %get-tuple-element.52), channel_id=1, source_target_pairs={{0,7},{1,0},{2,1},{3,2},{4,3},{5,4},{6,5},{7,6},{8,15},{9,8},{10,9... | collective-permute-start | bytes 98312 | tf_op jit(solution)/shard_map/ppermute | solution.py:205
  67.0 26.0 %all-to-all-start.1 = ((bf16[128,8,256]{2,1,0:T(8,128)(2,1)}), bf16[128,8,256]{2,1,0:T(8,128)(2,1)}, u32[]{:S(2)}, u32[]{:S(2)}) async-start(bf16[128,8,256]{2,1,0:T(8,128)(2,1)} %bitcast.12), calls=%async_computation.1 | async-start | bytes 1048576 | tf_op jit(solution)/shard_map/all_to_all | solution.py:835
  74.4 2.4 %copy-start.1 = (f32[68,144,128]{2,1,0:T(8,128)S(1)}, f32[68,144,128]{2,1,0:T(8,128)}, u32[]{:S(2)}) copy-start(f32[68,144,128]{2,1,0:T(8,128)} %copy-done) | copy-start | bytes 15040516
  76.8 2.2 %copy-start.4 = (f32[8192,128]{1,0:T(8,128)S(1)}, f32[8192,128]{1,0:T(8,128)}, u32[]{:S(2)}) copy-start(f32[8192,128]{1,0:T(8,128)} %copy-done.3) | copy-start | bytes 12582916
  79.0 8.7 %copy-start.2 = (f32[68,144,128]{2,1,0:T(8,128)S(1)}, f32[68,144,128]{2,1,0:T(8,128)}, u32[]{:S(2)}) copy-start(f32[68,144,128]{2,1,0:T(8,128)} %copy-done) | copy-start | bytes 15040516
  81.7 9.6 %collective-permute-start.6 = (bf16[272,128]{1,0:T(8,128)(2,1)S(1)}, bf16[272,128]{1,0:T(8,128)(2,1)S(1)}, u32[]{:S(2)}, u32[]{:S(2)}) collective-permute-start(bf16[272,128]{1,0:T(8,128)(2,1)S(1)} %get-tuple-element.53), channel_id=1, source_target_pairs={{0,8},{8,16},{16,24},{24,32},{32,40},{40,48},{48,56},{56,64},{64,7... | collective-permute-start | bytes 208904 | tf_op jit(solution)/shard_map/ppermute | solution.py:205
  83.2 8.1 %collective-permute-start.7 = (bf16[272,128]{1,0:T(8,128)(2,1)S(1)}, bf16[272,128]{1,0:T(8,128)(2,1)S(1)}, u32[]{:S(2)}, u32[]{:S(2)}) collective-permute-start(bf16[272,128]{1,0:T(8,128)(2,1)S(1)} %get-tuple-element.54), channel_id=1, source_target_pairs={{0,120},{8,0},{16,8},{24,16},{32,24},{40,32},{48,40},{56,48},{64,5... | collective-permute-start | bytes 208904 | tf_op jit(solution)/shard_map/ppermute | solution.py:205
  87.8 3.6 %copy-start.8 = (f32[128,8,128]{2,1,0:T(8,128)S(1)}, f32[128,8,128]{2,1,0:T(8,128)}, u32[]{:S(2)}) copy-start(f32[128,8,128]{2,1,0:T(8,128)} %copy-done.7) | copy-start | bytes 1572868
  87.8 3.6 %copy-start.10 = (f32[128,8,128]{2,1,0:T(8,128)S(1)}, f32[128,8,128]{2,1,0:T(8,128)}, u32[]{:S(2)}) copy-start(f32[128,8,128]{2,1,0:T(8,128)} %copy-done.9) | copy-start | bytes 1572868
  91.4 1.6 %copy-start.12 = (f32[256,616]{0,1:T(8,128)S(1)}, f32[256,616]{0,1:T(8,128)}, u32[]{:S(2)}) copy-start(f32[256,616]{0,1:T(8,128)} %param.19) | copy-start | bytes 1892356
  91.4 1.6 %copy-start.14 = (bf16[512,616]{0,1:T(8,128)(2,1)S(1)}, bf16[512,616]{0,1:T(8,128)(2,1)}, u32[]{:S(2)}) copy-start(bf16[512,616]{0,1:T(8,128)(2,1)} %param.25) | copy-start | bytes 1892356
  91.4 1.6 %copy-start.16 = (bf16[512,512]{1,0:T(8,128)(2,1)S(1)}, bf16[512,512]{1,0:T(8,128)(2,1)}, u32[]{:S(2)}) copy-start(bf16[512,512]{1,0:T(8,128)(2,1)} %w_second.3) | copy-start | bytes 1572868
  91.4 1.6 %copy-start.22 = (s32[256,1]{0,1:T(1,128)S(1)}, s32[256,1]{0,1:T(1,128)}, u32[]{:S(2)}) copy-start(s32[256,1]{0,1:T(1,128)} %param.16) | copy-start | bytes 3076

commit v7 on v6

--- a/solution.py
+++ b/solution.py
@@ -455,15 +455,15 @@
     for k in range(CAP):
 
         def fetch(step, carry):
-            for n in range(8):
-                owner = step * 8 + n
+            for n in range(16):
+                owner = step * 16 + n
                 at = table[k, owner]
                 to = pl.ds(4 * (k * DEV + owner), 4)
                 ga[to, :] = both[pl.ds(2 * at, 4), :]
                 gb[to, :] = both[pl.ds(2 * (at + BY), 4), :]
             return carry
 
-        lax.fori_loop(0, DEV // 8, fetch, 0)
+        lax.fori_loop(0, DEV // 16, fetch, 0)
     spaced[...] = jnp.zeros_like(spaced)
     for k in range(CAP):
         w = [lanes(weight[:, 8 * k : 8 * k + 1]) for weight in weights]
@@ -570,8 +570,8 @@
     for k in range(CAP):
 
         def add(step, carry):
-            for n in range(8):
-                owner = step * 8 + n
+            for n in range(16):
+                owner = step * 16 + n
                 at = table[k, owner]
                 there = pl.ds(2 * (k * DEV + owner), 2)
                 one = acc[pl.ds(at, 2), :] + ca[there, :]
@@ -580,7 +580,7 @@
                 acc[pl.ds(at + BY, 2), :] = two
             return carry
 
-        lax.fori_loop(0, DEV // 8, add, 0)
+        lax.fori_loop(0, DEV // 16, add, 0)
     x_down[...] = acc[: 2 * BY, :].astype(BF16)
     x_up[...] = acc[CELLS - 2 * BY :, :].astype(BF16)
     for n in range(2):

time: 97 us -> 97 us (level)
  no operation moved by 1% of the time
where the time goes in v7:
time: 97 us; the launch traced here: 96.6 us
  Pallas kernels  41.9 us (43%)
  starting transfers between devices  34.1 us (35%)
  local copies, waits for them, and re-layouts  12.6 us (13%)
  waiting for transfers between devices  6.93 us (7%)
  between operations  1 us (1%)
    all_to_all x2, starting transfers between devices, exchange(): lax.all_to_all(array, ('tile', 'obs'), split_axis=0, concat_axis=0, tiled...  18.9 us
    ppermute x8, starting transfers between devices, shift(): lax.ppermute(array, axis, [(i, (i + by) % count) for i in range(count)])  15.2 us
    unnamed x46, local copies, waits for them, and re-layouts  12.6 us
    pallas_call x1, Pallas kernels, adjoint(): pl.pallas_call(adjoint_kernel, in_specs=[whole] * 8 + [pl.BlockSpec(memor...  8.18 us
    ppermute x8, waiting for transfers between devices, shift(): lax.ppermute(array, axis, [(i, (i + by) % count) for i in range(count)])  6.93 us
    pallas_call x1, Pallas kernels, to_columns(): pl.pallas_call(columns_kernel, in_specs=[hbm, hbm, whole], out_specs=[who...  6.6 us
    pallas_call x1, Pallas kernels, gathered(): pl.pallas_call(gather_kernel, grid=(1,), in_specs=[pl.BlockSpec((DEV, ROW...  5.51 us
    pallas_call x1, Pallas kernels, requests(): pl.pallas_call(request_kernel, out_shape=jax.ShapeDtypeStruct((DEV * ROWS...  3.68 us
  transfers between devices with their start and end apart: 10, of which 2 were waited for; matrix products, arithmetic and copies ran while one was open for 0% of the time, Pallas kernels for 22%

profile of v7, /device:TPU:1, one launch (start us, length us, event | category | flops | bytes accessed | tf_op | source)
XLA Modules:
  0.0 96.6 jit_solution(6325936605960689473)
XLA Ops:
  0.6 0.0 copy-start.18
  0.6 3.7 %requests.1 = bf16[1024,512]{1,0:T(8,128)(2,1)} custom-call(s32[1,256]{1,0:T(1,128)} %bitcast.22, s32[1,256]{1,0:T(1,128)} %bitcast.24, f32[2,256]{1,0:T(2,128)} %frac.1, f32[616]{0:T(1024)} %ivar.5, f32[616,256]{1,0:T(8,128)} %bitcast.13, bf16[616,512]{1,0:T(8,128)(2,1)} %bitcast.15), custom_call_target="tpu_custom_call" | custom-call | flops 4000000000 | tf_op jit(solution)/shard_map/requests/pallas_call | solution.py:104
  4.3 11.5 %all-to-all-start = ((bf16[128,8,512]{2,1,0:T(8,128)(2,1)}), bf16[128,8,512]{2,1,0:T(8,128)(2,1)S(1)}, u32[]{:S(2)}, u32[]{:S(2)}) async-start(bf16[128,8,512]{2,1,0:T(8,128)(2,1)} %bitcast.4), calls=%async_computation | async-start | bytes 2097152 | tf_op jit(solution)/shard_map/all_to_all | solution.py:835
  15.8 0.0 copy-done.18
  15.8 6.6 %columns.1 = (f32[68,144,128]{2,1,0:T(8,128)S(1)}, bf16[64,128,128]{2,1,0:T(8,128)(2,1)}, bf16[272,128]{1,0:T(8,128)(2,1)S(1)}, bf16[272,128]{1,0:T(8,128)(2,1)S...) custom-call(f32[128,64,128]{2,1,0:T(8,128)} %control.3, bf16[128,64,128]{2,1,0:T(8,128)(2,1)} %background.1, ...), custom_call_target="tpu_custom_call" | custom-call | flops 6000000000 | tf_op jit(solution)/shard_map/columns/pallas_call | solution.py:175
  22.4 1.4 %collective-permute-start = (bf16[272,128]{1,0:T(8,128)(2,1)S(1)}, bf16[272,128]{1,0:T(8,128)(2,1)S(1)}, u32[]{:S(2)}, u32[]{:S(2)}) collective-permute-start(bf16[272,128]{1,0:T(8,128)(2,1)S(1)} %get-tuple-element.37), channel_id=1, source_target_pairs={{0,8},{8,16},{16,24},{24,32},{32,40},{40,48},{48,56},{56,64},{64,7... | collective-permute-start | bytes 208904 | tf_op jit(solution)/shard_map/ppermute | solution.py:205
  23.9 4.3 %collective-permute-start.1 = (bf16[272,128]{1,0:T(8,128)(2,1)S(1)}, bf16[272,128]{1,0:T(8,128)(2,1)S(1)}, u32[]{:S(2)}, u32[]{:S(2)}) collective-permute-start(bf16[272,128]{1,0:T(8,128)(2,1)S(1)} %get-tuple-element.38), channel_id=1, source_target_pairs={{0,120},{8,0},{16,8},{24,16},{32,24},{40,32},{48,40},{56,48},{64,5... | collective-permute-start | bytes 208904 | tf_op jit(solution)/shard_map/ppermute | solution.py:205
  28.1 6.4 %collective-permute-done.low.x_low = bf16[272,128]{1,0:T(8,128)(2,1)S(1)} collective-permute-done((bf16[272,128]{1,0:T(8,128)(2,1)S(1)}, bf16[272,128]{1,0:T(8,128)(2,1)S(1)}, u32[]{:S(2)}, u32[]{:S(2)}) %collective-permute-start) | collective-permute-done | bytes 69664 | tf_op jit(solution)/shard_map/ppermute | solution.py:205
  34.6 0.0 collective-permute-done.1.high.x_high
  34.6 1.7 %collective-permute-start.2 = (bf16[192,128]{1,0:T(8,128)(2,1)S(1)}, bf16[192,128]{1,0:T(8,128)(2,1)S(1)}, u32[]{:S(2)}, u32[]{:S(2)}) collective-permute-start(bf16[192,128]{1,0:T(8,128)(2,1)S(1)} %get-tuple-element.41), channel_id=1, source_target_pairs={{0,1},{1,2},{2,3},{3,4},{4,5},{5,6},{6,7},{7,0},{8,9},{9,10},{10,1... | collective-permute-start | bytes 147464 | tf_op jit(solution)/shard_map/ppermute | solution.py:205
  36.2 0.0 collective-permute-start.3
  36.3 3.2 %early.1 = (f32[68,144,128]{2,1,0:T(8,128)S(1)}, f32[68,144,128]{2,1,0:T(8,128)S(1)}) custom-call(f32[64,128]{1,0:T(8,128)S(1)} %copy-done.18, f32[68,144,128]{2,1,0:T(8,128)S(1)} %get-tuple-element.34.field._field), custom_call_target="tpu_custom_call" | custom-call | flops 2000000000 | tf_op jit(solution)/shard_map/early/pallas_call | solution.py:325
  39.5 0.0 collective-permute-done.2.y_low
  39.5 0.5 collective-permute-done.3.y_high
  40.0 3.4 %increment.1 = (bf16[64,128,128]{2,1,0:T(8,128)(2,1)}, f32[68,144,128]{2,1,0:T(8,128)}, f32[68,144,128]{2,1,0:T(8,128)S(1)}, f32[68,144,128]{2,1,0:T(8,128)S(1)}, f32[68,144,128]{2,1,0:T(8,128)S(1)}) custom-call(f32[68,144,128]{2,1,0:T(8,128)S(1)} %get-tuple-element.34.field._field, ...), custom_call_target="tpu_custom_call", output_to_operand_aliasing={{2}: (0, {}), {3}: (1, {}), {4}: (2, {})} | custom-call | flops 6000000000 | tf_op jit(solution)/shard_map/increment/pallas_call | solution.py:380
  43.4 0.0 all-to-all-done.got
  43.4 0.0 copy-start.5
  43.4 0.0 copy-start.13
  43.4 0.0 copy-start.15
  43.4 0.0 copy-start.17
  43.4 0.0 copy-start.19
  43.4 0.0 copy-start.20
  43.4 0.0 copy-start.21
  43.5 5.5 %gather.1 = (bf16[1024,256]{1,0:T(8,128)(2,1)S(1)}, bf16[768,256]{1,0:T(8,128)(2,1)S(1)}) custom-call(bf16[128,8,512]{2,1,0:T(8,128)(2,1)S(1)} %all-to-all-done.got, bf16[8192,128]{1,0:T(8,128)(2,1)} %bitcast.25, bf16[8192,128]{1,0:T(8,128)(2,1)} %bitcast.26), custom_call_target="tpu_custom_call" | custom-call | flops 5000000000 | tf_op jit(solution)/shard_map/gather/pallas_call | solution.py:485
  49.0 0.0 copy-done.5
  49.0 0.0 copy-start.11
  49.0 0.8 copy-done.11
  49.8 0.0 copy-done.13
  49.8 0.0 copy-done.15
  49.8 0.0 copy-done.17
  49.8 0.0 copy-done.19
  49.8 0.0 copy-done.20
  49.8 0.0 copy-done.21
  49.8 0.0 copy-start.6
  49.8 1.2 %copy-done.6 = bf16[128,8,512]{2,1,0:T(8,128)(2,1)S(1)} copy-done((bf16[128,8,512]{2,1,0:T(8,128)(2,1)S(1)}, bf16[128,8,512]{2,1,0:T(8,128)(2,1)}, u32[]{:S(2)}) %copy-start.6) | copy-done | bytes 1048600
  51.0 8.2 %adjoint.1 = (f32[8192,128]{1,0:T(8,128)S(1)}, bf16[256,128]{1,0:T(8,128)(2,1)S(1)}, bf16[256,128]{1,0:T(8,128)(2,1)S(1)}, bf16[128,128]{1,0:T(8,128)(2,1)S(1)},...) custom-call(bf16[128,8,512]{2,1,0:T(8,128)(2,1)S(1)} %copy-done.6, ...), custom_call_target="tpu_custom_call" | custom-call | flops 10000000000 | tf_op jit(solution)/shard_map/adjoint/pallas_call | solution.py:598
  59.2 0.0 copy-start
  59.2 2.2 %copy-done = f32[68,144,128]{2,1,0:T(8,128)} copy-done((f32[68,144,128]{2,1,0:T(8,128)}, f32[68,144,128]{2,1,0:T(8,128)S(1)}, u32[]{:S(2)}) %copy-start) | copy-done | bytes 5013528
  61.5 2.0 %copy-done.3 = f32[8192,128]{1,0:T(8,128)} copy-done((f32[8192,128]{1,0:T(8,128)}, f32[8192,128]{1,0:T(8,128)S(1)}, u32[]{:S(2)}) %copy-start.3) | copy-done | bytes 4194328
  63.5 0.8 copy-done.7
  64.3 0.8 copy-done.9
  65.1 1.3 %collective-permute-start.4 = (bf16[128,128]{1,0:T(8,128)(2,1)S(1)}, bf16[128,128]{1,0:T(8,128)(2,1)S(1)}, u32[]{:S(2)}, u32[]{:S(2)}) collective-permute-start(bf16[128,128]{1,0:T(8,128)(2,1)S(1)} %get-tuple-element.51), channel_id=1, source_target_pairs={{0,1},{1,2},{2,3},{3,4},{4,5},{5,6},{6,7},{7,0},{8,9},{9,10},{10,1... | collective-permute-start | bytes 98312 | tf_op jit(solution)/shard_map/ppermute | solution.py:205
  66.4 0.6 collective-permute-start.5
  67.0 7.4 %all-to-all-start.1 = ((bf16[128,8,256]{2,1,0:T(8,128)(2,1)}), bf16[128,8,256]{2,1,0:T(8,128)(2,1)}, u32[]{:S(2)}, u32[]{:S(2)}) async-start(bf16[128,8,256]{2,1,0:T(8,128)(2,1)} %bitcast.12), calls=%async_computation.1 | async-start | bytes 1048576 | tf_op jit(solution)/shard_map/all_to_all | solution.py:835
  74.4 0.0 copy-start.1
  74.4 2.4 %copy-done.1 = f32[68,144,128]{2,1,0:T(8,128)S(1)} copy-done((f32[68,144,128]{2,1,0:T(8,128)S(1)}, f32[68,144,128]{2,1,0:T(8,128)}, u32[]{:S(2)}) %copy-start.1) | copy-done | bytes 5013528
  76.8 2.2 %copy-done.4 = f32[8192,128]{1,0:T(8,128)S(1)} copy-done((f32[8192,128]{1,0:T(8,128)S(1)}, f32[8192,128]{1,0:T(8,128)}, u32[]{:S(2)}) %copy-start.4) | copy-done | bytes 4194328
  79.0 2.7 %ready.1 = (f32[64,128,128]{2,1,0:T(8,128)S(1)}, f32[68,144,128]{2,1,0:T(8,128)S(1)}) custom-call(f32[8192,128]{1,0:T(8,128)S(1)} %copy-done.4, f32[68,144,128]{2,1,0:T(8,128)S(1)} %copy-done.1), custom_call_target="tpu_custom_call" | custom-call | flops 3000000000 | tf_op jit(solution)/shard_map/ready/pallas_call | solution.py:680
  81.7 0.0 collective-permute-done.4.low.y_low
  81.7 0.0 collective-permute-done.5.high.y_high
  81.8 1.5 %collective-permute-start.6 = (bf16[272,128]{1,0:T(8,128)(2,1)S(1)}, bf16[272,128]{1,0:T(8,128)(2,1)S(1)}, u32[]{:S(2)}, u32[]{:S(2)}) collective-permute-start(bf16[272,128]{1,0:T(8,128)(2,1)S(1)} %get-tuple-element.53), channel_id=1, source_target_pairs={{0,8},{8,16},{16,24},{24,32},{32,40},{40,48},{48,56},{56,64},{64,7... | collective-permute-start | bytes 208904 | tf_op jit(solution)/shard_map/ppermute | solution.py:205
  83.3 4.5 %collective-permute-start.7 = (bf16[272,128]{1,0:T(8,128)(2,1)S(1)}, bf16[272,128]{1,0:T(8,128)(2,1)S(1)}, u32[]{:S(2)}, u32[]{:S(2)}) collective-permute-start(bf16[272,128]{1,0:T(8,128)(2,1)S(1)} %get-tuple-element.54), channel_id=1, source_target_pairs={{0,120},{8,0},{16,8},{24,16},{32,24},{40,32},{48,40},{56,48},{64,5... | collective-permute-start | bytes 208904 | tf_op jit(solution)/shard_map/ppermute | solution.py:205
  87.8 0.0 copy-done.2
  87.8 3.6 %interior.1 = (f32[128,64,128]{2,1,0:T(8,128)}, f32[128,48,128]{2,1,0:T(8,128)S(1)}, f32[64,128,128]{2,1,0:T(8,128)S(1)}, f32[68,144,128]{2,1,0:T(8,128)S(1)}) custom-call(f32[8192,128]{1,0:T(8,128)S(1)} %copy-done.4, f32[68,144,128]{2,1,0:T(8,128)S(1)} %copy-done.2, ...), custom_call_target="tpu_custom_call", output_to_operand_aliasing={{1}: (4, {}), {2}: (5, {}), {3}: (6, {})} | custom-call | flops 5000000000 | tf_op jit(solution)/shard_map/interior/pallas_call | solution.py:752
  91.4 0.0 collective-permute-done.6.x_low
  91.4 0.0 collective-permute-done.7.x_high
  91.4 0.0 copy-done.8
  91.4 0.0 copy-start.12
  91.4 0.0 copy-start.14
  91.4 0.0 copy-start.16
  91.5 0.0 copy-start.22
  91.5 1.5 %edges.1 = (f32[128,64,128]{2,1,0:T(8,128)}, f32[64,128,128]{2,1,0:T(8,128)S(1)}, f32[68,144,128]{2,1,0:T(8,128)S(1)}, f32[128,8,128]{2,1,0:T(8,128)S(1)}, f32[128,8,128]{2,1,0:T(8,128)S(1)}) custom-call(f32[8192,128]{1,0:T(8,128)S(1)} %copy-done.4, ...), custom_call_target="tpu_custom_call", output_to_operand_aliasing={{0}: (4, {}), {1}: (5, {}), {2}: (6, {}), {3}: (7, {}), {4}... | custom-call | flops 2000000000 | tf_op jit(solution)/shard_map/edges/pallas_call | solution.py:812
  93.0 0.0 all-to-all-done.1
  93.0 3.6 %departures.1 = f32[616,256]{1,0:T(8,128)} custom-call(bf16[1024,256]{1,0:T(8,128)(2,1)} %bitcast.8.reply, s32[1,256]{1,0:T(1,128)S(1)} %bitcast.23, f32[616,256]{1,0:T(8,128)S(1)} %bitcast.14, bf16[128,512]{1,0:T(8,128)(2,1)S(1)} %copy-done.17, f32[1,512]{1,0:T(1,128)S(1)} %bitcast.19, bf16[512,512]{1,0:T(8,128)(2,1)S(1)} %copy-done.16, ...), custom_call_target="tpu_custom_call" | custom-call | flops 4000000000 | tf_op jit(solution)/shard_map/departures/pallas_call | solution.py:647
  (14 shorter events, 0.1 us)
Async XLA Ops:
  0.6 15.2 %copy-start.18 = (f32[64,128]{1,0:T(8,128)S(1)}, f32[64,128]{1,0:T(8,128)}, u32[]{:S(2)}) copy-start(f32[64,128]{1,0:T(8,128)} %spread.3) | copy-start | bytes 98308
  4.3 39.0 %all-to-all-start = ((bf16[128,8,512]{2,1,0:T(8,128)(2,1)}), bf16[128,8,512]{2,1,0:T(8,128)(2,1)S(1)}, u32[]{:S(2)}, u32[]{:S(2)}) async-start(bf16[128,8,512]{2,1,0:T(8,128)(2,1)} %bitcast.4), calls=%async_computation | async-start | bytes 2097152 | tf_op jit(solution)/shard_map/all_to_all | solution.py:835
  22.4 12.1 %collective-permute-start = (bf16[272,128]{1,0:T(8,128)(2,1)S(1)}, bf16[272,128]{1,0:T(8,128)(2,1)S(1)}, u32[]{:S(2)}, u32[]{:S(2)}) collective-permute-start(bf16[272,128]{1,0:T(8,128)(2,1)S(1)} %get-tuple-element.37), channel_id=1, source_target_pairs={{0,8},{8,16},{16,24},{24,32},{32,40},{40,48},{48,56},{56,64},{64,7... | collective-permute-start | bytes 208904 | tf_op jit(solution)/shard_map/ppermute | solution.py:205
  23.9 10.7 %collective-permute-start.1 = (bf16[272,128]{1,0:T(8,128)(2,1)S(1)}, bf16[272,128]{1,0:T(8,128)(2,1)S(1)}, u32[]{:S(2)}, u32[]{:S(2)}) collective-permute-start(bf16[272,128]{1,0:T(8,128)(2,1)S(1)} %get-tuple-element.38), channel_id=1, source_target_pairs={{0,120},{8,0},{16,8},{24,16},{32,24},{40,32},{48,40},{56,48},{64,5... | collective-permute-start | bytes 208904 | tf_op jit(solution)/shard_map/ppermute | solution.py:205
  34.6 4.9 %collective-permute-start.2 = (bf16[192,128]{1,0:T(8,128)(2,1)S(1)}, bf16[192,128]{1,0:T(8,128)(2,1)S(1)}, u32[]{:S(2)}, u32[]{:S(2)}) collective-permute-start(bf16[192,128]{1,0:T(8,128)(2,1)S(1)} %get-tuple-element.41), channel_id=1, source_target_pairs={{0,1},{1,2},{2,3},{3,4},{4,5},{5,6},{6,7},{7,0},{8,9},{9,10},{10,1... | collective-permute-start | bytes 147464 | tf_op jit(solution)/shard_map/ppermute | solution.py:205
  36.2 3.7 %collective-permute-start.3 = (bf16[192,128]{1,0:T(8,128)(2,1)S(1)}, bf16[192,128]{1,0:T(8,128)(2,1)S(1)}, u32[]{:S(2)}, u32[]{:S(2)}) collective-permute-start(bf16[192,128]{1,0:T(8,128)(2,1)S(1)} %get-tuple-element.42), channel_id=1, source_target_pairs={{0,7},{1,0},{2,1},{3,2},{4,3},{5,4},{6,5},{7,6},{8,15},{9,8},{10,9... | collective-permute-start | bytes 147464 | tf_op jit(solution)/shard_map/ppermute | solution.py:205
  43.4 5.6 %copy-start.5 = (bf16[128,8,512]{2,1,0:T(8,128)(2,1)}, bf16[128,8,512]{2,1,0:T(8,128)(2,1)S(1)}, u32[]{:S(2)}) copy-start(bf16[128,8,512]{2,1,0:T(8,128)(2,1)S(1)} %all-to-all-done.got) | copy-start | bytes 3145732
  43.4 6.4 %copy-start.13 = (bf16[512,616]{0,1:T(8,128)(2,1)S(1)}, bf16[512,616]{0,1:T(8,128)(2,1)}, u32[]{:S(2)}) copy-start(bf16[512,616]{0,1:T(8,128)(2,1)} %param.25) | copy-start | bytes 1892356
  43.4 6.4 %copy-start.15 = (bf16[512,512]{1,0:T(8,128)(2,1)S(1)}, bf16[512,512]{1,0:T(8,128)(2,1)}, u32[]{:S(2)}) copy-start(bf16[512,512]{1,0:T(8,128)(2,1)} %w_second.3) | copy-start | bytes 1572868
  43.4 6.4 %copy-start.17 = (bf16[128,512]{1,0:T(8,128)(2,1)S(1)}, bf16[128,512]{1,0:T(8,128)(2,1)}, u32[]{:S(2)}) copy-start(bf16[128,512]{1,0:T(8,128)(2,1)} %w_first.3) | copy-start | bytes 393220
  43.4 6.4 %copy-start.19 = (f32[616]{0:T(1024)S(1)}, f32[616]{0:T(1024)}, u32[]{:S(2)}) copy-start(f32[616]{0:T(1024)} %ivar.5) | copy-start | bytes 7396
  43.4 6.4 %copy-start.20 = (f32[512]{0:T(512)S(1)}, f32[512]{0:T(512)}, u32[]{:S(2)}) copy-start(f32[512]{0:T(512)} %param.22) | copy-start | bytes 6148
  43.4 6.4 %copy-start.21 = (f32[512]{0:T(512)S(1)}, f32[512]{0:T(512)}, u32[]{:S(2)}) copy-start(f32[512]{0:T(512)} %param.24) | copy-start | bytes 6148
  49.0 0.8 copy-start.11
  49.8 1.2 %copy-start.6 = (bf16[128,8,512]{2,1,0:T(8,128)(2,1)S(1)}, bf16[128,8,512]{2,1,0:T(8,128)(2,1)}, u32[]{:S(2)}) copy-start(bf16[128,8,512]{2,1,0:T(8,128)(2,1)} %copy-done.5) | copy-start | bytes 3145732
  59.2 2.3 %copy-start = (f32[68,144,128]{2,1,0:T(8,128)}, f32[68,144,128]{2,1,0:T(8,128)S(1)}, u32[]{:S(2)}) copy-start(f32[68,144,128]{2,1,0:T(8,128)S(1)} %get-tuple-element.48.coef) | copy-start | bytes 15040516
  61.5 2.0 %copy-start.3 = (f32[8192,128]{1,0:T(8,128)}, f32[8192,128]{1,0:T(8,128)S(1)}, u32[]{:S(2)}) copy-start(f32[8192,128]{1,0:T(8,128)S(1)} %get-tuple-element.47.acc) | copy-start | bytes 12582916
  63.5 0.8 copy-start.7
  64.3 0.8 copy-start.9
  65.1 16.6 %collective-permute-start.4 = (bf16[128,128]{1,0:T(8,128)(2,1)S(1)}, bf16[128,128]{1,0:T(8,128)(2,1)S(1)}, u32[]{:S(2)}, u32[]{:S(2)}) collective-permute-start(bf16[128,128]{1,0:T(8,128)(2,1)S(1)} %get-tuple-element.51), channel_id=1, source_target_pairs={{0,1},{1,2},{2,3},{3,4},{4,5},{5,6},{6,7},{7,0},{8,9},{9,10},{10,1... | collective-permute-start | bytes 98312 | tf_op jit(solution)/shard_map/ppermute | solution.py:205
  66.4 15.3 %collective-permute-start.5 = (bf16[128,128]{1,0:T(8,128)(2,1)S(1)}, bf16[128,128]{1,0:T(8,128)(2,1)S(1)}, u32[]{:S(2)}, u32[]{:S(2)}) collective-permute-start(bf16[128,128]{1,0:T(8,128)(2,1)S(1)} %get-tuple-element.52), channel_id=1, source_target_pairs={{0,7},{1,0},{2,1},{3,2},{4,3},{5,4},{6,5},{7,6},{8,15},{9,8},{10,9... | collective-permute-start | bytes 98312 | tf_op jit(solution)/shard_map/ppermute | solution.py:205
  67.0 26.0 %all-to-all-start.1 = ((bf16[128,8,256]{2,1,0:T(8,128)(2,1)}), bf16[128,8,256]{2,1,0:T(8,128)(2,1)}, u32[]{:S(2)}, u32[]{:S(2)}) async-start(bf16[128,8,256]{2,1,0:T(8,128)(2,1)} %bitcast.12), calls=%async_computation.1 | async-start | bytes 1048576 | tf_op jit(solution)/shard_map/all_to_all | solution.py:835
  74.4 2.4 %copy-start.1 = (f32[68,144,128]{2,1,0:T(8,128)S(1)}, f32[68,144,128]{2,1,0:T(8,128)}, u32[]{:S(2)}) copy-start(f32[68,144,128]{2,1,0:T(8,128)} %copy-done) | copy-start | bytes 15040516
  76.8 2.2 %copy-start.4 = (f32[8192,128]{1,0:T(8,128)S(1)}, f32[8192,128]{1,0:T(8,128)}, u32[]{:S(2)}) copy-start(f32[8192,128]{1,0:T(8,128)} %copy-done.3) | copy-start | bytes 12582916
  79.0 8.7 %copy-start.2 = (f32[68,144,128]{2,1,0:T(8,128)S(1)}, f32[68,144,128]{2,1,0:T(8,128)}, u32[]{:S(2)}) copy-start(f32[68,144,128]{2,1,0:T(8,128)} %copy-done) | copy-start | bytes 15040516
  81.8 9.6 %collective-permute-start.6 = (bf16[272,128]{1,0:T(8,128)(2,1)S(1)}, bf16[272,128]{1,0:T(8,128)(2,1)S(1)}, u32[]{:S(2)}, u32[]{:S(2)}) collective-permute-start(bf16[272,128]{1,0:T(8,128)(2,1)S(1)} %get-tuple-element.53), channel_id=1, source_target_pairs={{0,8},{8,16},{16,24},{24,32},{32,40},{40,48},{48,56},{56,64},{64,7... | collective-permute-start | bytes 208904 | tf_op jit(solution)/shard_map/ppermute | solution.py:205
  83.3 8.1 %collective-permute-start.7 = (bf16[272,128]{1,0:T(8,128)(2,1)S(1)}, bf16[272,128]{1,0:T(8,128)(2,1)S(1)}, u32[]{:S(2)}, u32[]{:S(2)}) collective-permute-start(bf16[272,128]{1,0:T(8,128)(2,1)S(1)} %get-tuple-element.54), channel_id=1, source_target_pairs={{0,120},{8,0},{16,8},{24,16},{32,24},{40,32},{48,40},{56,48},{64,5... | collective-permute-start | bytes 208904 | tf_op jit(solution)/shard_map/ppermute | solution.py:205
  87.8 3.6 %copy-start.8 = (f32[128,8,128]{2,1,0:T(8,128)S(1)}, f32[128,8,128]{2,1,0:T(8,128)}, u32[]{:S(2)}) copy-start(f32[128,8,128]{2,1,0:T(8,128)} %copy-done.7) | copy-start | bytes 1572868
  87.8 3.6 %copy-start.10 = (f32[128,8,128]{2,1,0:T(8,128)S(1)}, f32[128,8,128]{2,1,0:T(8,128)}, u32[]{:S(2)}) copy-start(f32[128,8,128]{2,1,0:T(8,128)} %copy-done.9) | copy-start | bytes 1572868
  91.4 1.6 %copy-start.12 = (f32[256,616]{0,1:T(8,128)S(1)}, f32[256,616]{0,1:T(8,128)}, u32[]{:S(2)}) copy-start(f32[256,616]{0,1:T(8,128)} %param.19) | copy-start | bytes 1892356
  91.4 1.6 %copy-start.14 = (bf16[512,616]{0,1:T(8,128)(2,1)S(1)}, bf16[512,616]{0,1:T(8,128)(2,1)}, u32[]{:S(2)}) copy-start(bf16[512,616]{0,1:T(8,128)(2,1)} %param.25) | copy-start | bytes 1892356
  91.4 1.6 %copy-start.16 = (bf16[512,512]{1,0:T(8,128)(2,1)S(1)}, bf16[512,512]{1,0:T(8,128)(2,1)}, u32[]{:S(2)}) copy-start(bf16[512,512]{1,0:T(8,128)(2,1)} %w_second.3) | copy-start | bytes 1572868
  91.5 1.6 %copy-start.22 = (s32[256,1]{0,1:T(1,128)S(1)}, s32[256,1]{0,1:T(1,128)}, u32[]{:S(2)}) copy-start(s32[256,1]{0,1:T(1,128)} %param.16) | copy-start | bytes 3076
